TPU v7x, 32 devices: a whole 2x2x4 slice. The times are simulated.
32 devices in a mesh: lat: 2 (over core), lon: 4 (over y, x), lev: 4 (over z).
Axes of the slice: x: 2, y: 2, z: 4, core: 2. Of those that a mesh axis runs over, the one named last changes fastest.
Arguments:
- field_values: float32 [16, 512, 64, 128], P('lat', 'lon', 'lev'), may hold values from 0.2 to 1.8
- crowding: float32 [16, 512, 64, 128], P('lat', 'lon', 'lev'), may hold values from 0.5 to 2
Outputs:
- potential: float32 [16, 512, 64, 128], P('lat', 'lon', 'lev')
- field_values_end: float32 [16, 512, 64, 128], P('lat', 'lon', 'lev')
All inputs are finite; a program needn't handle non-finite values.
Results may differ from a plain program's by a relative error of at most 0.00002.
Values sent between devices are 32-bit elements; how exact they have to be, the bound alone decides.
No kernel may reach another device: no remote copies, remote signals or barrier semaphores. Data moves between devices by JAX's collectives and lax.ppermute only.
A program may use at most 256 MiB of HBM per device.

v0:
```python
import jax
import jax.numpy as jnp
from jax import lax
from jax.sharding import PartitionSpec as P

STEPS = 4


def with_halo(cells, sides, width):
    for axis, dim in sides:
        count = lax.axis_size(axis)
        head = lax.slice_in_dim(cells, 0, width, axis=dim)
        tail = lax.slice_in_dim(cells, cells.shape[dim] - width, cells.shape[dim], axis=dim)
        cells = jnp.concatenate(
            [
                lax.ppermute(tail, axis, [(i, (i + 1) % count) for i in range(count)]),
                cells,
                lax.ppermute(head, axis, [((i + 1) % count, i) for i in range(count)]),
            ],
            axis=dim,
        )
    return cells


def entering(part, axis, combine, identity):
    place = lax.axis_index(axis)
    gathered = lax.all_gather(part, axis)
    state = jnp.zeros_like(part) + jnp.asarray(identity, part.dtype)

    def one(turn, state):
        return combine(state, lax.dynamic_index_in_dim(gathered, turn, 0, False))

    return lax.fori_loop(0, place, one, state)


def without_rim(values, dims):
    for dim in dims:
        values = lax.slice_in_dim(values, 1, values.shape[dim] - 1, axis=dim)
    return values


def shifted_cells(values, dim, start, dims):
    others = [other for other in dims if other != dim]
    values = without_rim(values, others)
    return lax.slice_in_dim(values, start, start + values.shape[dim] - 2, axis=dim)


def march_step(padded, crowding):
    middle = without_rim(padded, (0, 1, 2))
    lower = [shifted_cells(padded, dim, 0, (0, 1, 2)) for dim in (0, 1, 2)]
    upper = [shifted_cells(padded, dim, 2, (0, 1, 2)) for dim in (0, 1, 2)]
    spread = lower[0] + upper[0] + lower[1] + upper[1] + lower[2] + upper[2] - 6.0 * middle
    return middle + 0.1 * spread + 0.2 * middle * (1.0 - middle * crowding)


def per_device(field_values, crowding):
    for step in range(STEPS):
        padded = with_halo(field_values, (("lat", 0), ("lon", 1), ("lev", 2)), 1)
        field_values = march_step(padded, crowding)
    here = jnp.cumsum(field_values, axis=2)
    total = lax.slice_in_dim(here, here.shape[2] - 1, here.shape[2], axis=2)

    def add_pair(earlier_total, later_total):
        return earlier_total + later_total

    below = entering(total, "lev", add_pair, jnp.zeros_like(total))
    potential = (here + below) / (field_values.shape[2] * lax.axis_size("lev"))
    return (potential, field_values)


def solution(mesh):
    return jax.shard_map(
        per_device,
        mesh=mesh,
        in_specs=(P("lat", "lon", "lev", None), P("lat", "lon", "lev", None)),
        out_specs=(P("lat", "lon", "lev", None), P("lat", "lon", "lev", None)),
        check_vma=False,
    )
```

profile of v0, /device:TPU:25, one launch (start us, length us, event | category | flops | bytes accessed | tf_op | source)
XLA Modules:
  0.0 361.5 jit_solution(2941315530111769444)
XLA Ops:
  7.2 1.7 fusion.42
  9.7 2.2 collective-permute-done
  12.0 4.0 %constant_dynamic-update-slice_fusion.1 = f32[10,128,16,128]{3,2,1,0:T(8,128)S(1)} fusion(f32[10,128,16,128]{3,2,1,0:T(8,128)S(1)} %constant_dynamic-update-slice_fusion.2, f32[8,128,16,128]{3,2,1,0:T(8,128)} %param.4), kind=kLoop, calls=%fused_computation.132 | loop fusion | bytes 16777216
  16.1 1.3 collective-permute-start.2
  17.4 1.2 collective-permute-start.3
  18.5 2.2 collective-permute-done.2
  20.7 1.8 collective-permute-done.3
  23.8 3.1 collective-permute-start.4
  26.9 14.5 %collective-permute-done.5 = f32[10,130,1,128]{3,1,2,0:T(8,128)S(1)} collective-permute-done((f32[10,130,1,128]{3,1,2,0:T(8,128)S(1)}, f32[10,130,1,128]{3,1,2,0:T(8,128)S(1)}, u32[]{:S(2)}, u32[]{:S(2)}) %collective-permute-start.5) | collective-permute-done | bytes 665632 | tf_op jit(solution)/shard_map/ppermute | solution.py:18
  42.1 12.7 %collective-permute-done.4 = f32[10,130,1,128]{3,1,2,0:T(8,128)S(1)} collective-permute-done((f32[10,130,1,128]{3,1,2,0:T(8,128)S(1)}, f32[10,130,1,128]{3,1,2,0:T(8,128)S(1)}, u32[]{:S(2)}, u32[]{:S(2)}) %collective-permute-start.4) | collective-permute-done | bytes 665632 | tf_op jit(solution)/shard_map/ppermute | solution.py:16
  55.5 24.4 %fusion.31 = f32[8,128,16,128]{3,2,1,0:T(8,128)S(1)} fusion(f32[8,128,16,128]{3,2,1,0:T(8,128)} %param.4, f32[10,130,1,128]{3,2,1,0:T(1,128)S(1)} %copy.26, f32[10,1,16,128]{3,2,1,0:T(8,128)S(1)} %collective-permute-done.3, f32[10,128,16,128]{3,2,1,0:T(8,128)} %copy-done.2, f32[10,1,16,128]{3,2,1,0:T(8,128)S(1)} %collective-permute-done.2, ...), kind=kLoop, calls=%fused_computation.87 | loop fusion | flops 50331648 | bytes 39243776 | tf_op jit(solution)/shard_map/add | solution.py:53
  80.0 2.1 collective-permute-start.6
  82.2 2.2 collective-permute-done.6
  84.4 1.5 collective-permute-done.7
  85.9 1.5 collective-permute-start.8
  88.3 2.2 collective-permute-done.8
  90.5 1.2 collective-permute-done.9
  91.6 1.9 pad_maximum_fusion.78
  93.9 3.3 collective-permute-start.10
  97.2 14.4 %collective-permute-done.11 = f32[10,130,1,128]{3,1,2,0:T(8,128)S(1)} collective-permute-done((f32[10,130,1,128]{3,1,2,0:T(8,128)S(1)}, f32[10,130,1,128]{3,1,2,0:T(8,128)S(1)}, u32[]{:S(2)}, u32[]{:S(2)}) %collective-permute-start.11) | collective-permute-done | bytes 665632 | tf_op jit(solution)/shard_map/ppermute | solution.py:18
  111.6 1.5 copy.30
  113.2 13.1 %collective-permute-done.10 = f32[10,130,1,128]{3,1,2,0:T(8,128)S(1)} collective-permute-done((f32[10,130,1,128]{3,1,2,0:T(8,128)S(1)}, f32[10,130,1,128]{3,1,2,0:T(8,128)S(1)}, u32[]{:S(2)}, u32[]{:S(2)}) %collective-permute-start.10) | collective-permute-done | bytes 665632 | tf_op jit(solution)/shard_map/ppermute | solution.py:16
  126.3 1.5 copy.28
  127.8 16.0 %fusion.22 = f32[8,128,16,128]{3,2,1,0:T(8,128)} fusion(f32[8,128,16,128]{3,2,1,0:T(8,128)S(1)} %fusion.31, f32[10,130,1,128]{3,2,1,0:T(1,128)} %copy.30, f32[10,1,16,128]{3,2,1,0:T(8,128)S(1)} %collective-permute-done.9, f32[10,1,16,128]{3,2,1,0:T(8,128)S(1)} %collective-permute-done.8, f32[1,128,16,128]{3,2,1,0:T(8,128)} %copy-done.3, ...), kind=kLoop, calls=%fused_computation.60 | loop fusion | flops 67108864 | bytes 28758016 | tf_op jit(solution)/shard_map/add | solution.py:53
  143.8 1.8 fusion.40
  145.6 1.4 collective-permute-start.12
  147.1 2.2 collective-permute-done.12
  149.3 1.5 collective-permute-done.13
  150.8 1.0 pad_maximum_fusion.87
  151.8 1.3 collective-permute-start.14
  153.2 1.1 collective-permute-start.15
  154.3 2.2 collective-permute-done.14
  156.4 1.4 collective-permute-done.15
  157.9 1.9 pad_maximum_fusion.73
  159.8 1.2 collective-permute-start.17
  161.1 2.2 collective-permute-start.16
  163.3 14.4 %collective-permute-done.17 = f32[10,130,1,128]{3,1,2,0:T(8,128)S(1)} collective-permute-done((f32[10,130,1,128]{3,1,2,0:T(8,128)S(1)}, f32[10,130,1,128]{3,1,2,0:T(8,128)S(1)}, u32[]{:S(2)}, u32[]{:S(2)}) %collective-permute-start.17) | collective-permute-done | bytes 665632 | tf_op jit(solution)/shard_map/ppermute | solution.py:18
  177.7 1.5 copy.34
  179.2 14.0 %collective-permute-done.16 = f32[10,130,1,128]{3,1,2,0:T(8,128)S(1)} collective-permute-done((f32[10,130,1,128]{3,1,2,0:T(8,128)S(1)}, f32[10,130,1,128]{3,1,2,0:T(8,128)S(1)}, u32[]{:S(2)}, u32[]{:S(2)}) %collective-permute-start.16) | collective-permute-done | bytes 665632 | tf_op jit(solution)/shard_map/ppermute | solution.py:16
  193.3 1.5 copy.32
  194.8 16.0 %fusion.13 = f32[8,128,16,128]{3,2,1,0:T(8,128)} fusion(f32[8,128,16,128]{3,2,1,0:T(8,128)S(1)} %copy-done, f32[10,130,1,128]{3,2,1,0:T(1,128)} %copy.34, f32[10,1,16,128]{3,2,1,0:T(8,128)S(1)} %collective-permute-done.15, f32[10,1,16,128]{3,2,1,0:T(8,128)S(1)} %collective-permute-done.14, f32[1,128,16,128]{3,2,1,0:T(8,128)} %copy-done.4, ...), kind=kLoop, calls=%fused_computation.33 | loop fusion | flops 67108864 | bytes 28758016 | tf_op jit(solution)/shard_map/add | solution.py:53
  210.8 1.8 fusion.39
  212.6 1.0 collective-permute-start.18
  213.7 2.2 collective-permute-done.18
  215.9 1.5 collective-permute-done.19
  218.4 1.5 collective-permute-start.20
  220.9 2.2 collective-permute-done.20
  223.0 1.4 collective-permute-done.21
  224.4 1.9 pad_maximum_fusion.68
  227.2 2.8 collective-permute-start.22
  230.0 14.2 %collective-permute-done.23 = f32[10,130,1,128]{3,1,2,0:T(8,128)S(1)} collective-permute-done((f32[10,130,1,128]{3,1,2,0:T(8,128)S(1)}, f32[10,130,1,128]{3,1,2,0:T(8,128)S(1)}, u32[]{:S(2)}, u32[]{:S(2)}) %collective-permute-start.23) | collective-permute-done | bytes 665632 | tf_op jit(solution)/shard_map/ppermute | solution.py:18
  244.3 1.5 copy.38
  245.8 14.8 %collective-permute-done.22 = f32[10,130,1,128]{3,1,2,0:T(8,128)S(1)} collective-permute-done((f32[10,130,1,128]{3,1,2,0:T(8,128)S(1)}, f32[10,130,1,128]{3,1,2,0:T(8,128)S(1)}, u32[]{:S(2)}, u32[]{:S(2)}) %collective-permute-start.22) | collective-permute-done | bytes 665632 | tf_op jit(solution)/shard_map/ppermute | solution.py:16
  260.6 1.6 copy.36
  262.2 16.0 %fusion.4 = f32[8,128,16,128]{3,2,1,0:T(8,128)} fusion(f32[8,128,16,128]{3,2,1,0:T(8,128)S(1)} %copy-done.1, f32[10,130,1,128]{3,2,1,0:T(1,128)} %copy.38, f32[10,1,16,128]{3,2,1,0:T(8,128)S(1)} %collective-permute-done.21, f32[10,1,16,128]{3,2,1,0:T(8,128)S(1)} %collective-permute-done.20, f32[1,128,16,128]{3,2,1,0:T(8,128)} %copy-done.5, ...), kind=kLoop, calls=%fused_computation.6 | loop fusion | flops 67108864 | bytes 28758016 | tf_op jit(solution)/shard_map/add | solution.py:53
  278.2 11.6 %fusion.36 = f32[8,128,16,128]{3,1,2,0:T(8,128)} fusion(f32[8,128,16,128]{3,2,1,0:T(8,128)} %fusion.4), kind=kOutput, calls=%fused_computation.101 | output fusion | flops 31457280 | bytes 16777216 | tf_op jit(solution)/shard_map/jit(cumsum)/reduce_window_sum | solution.py:60
  289.8 1.9 slice.360
  291.7 44.8 %all-gather.3.cloned.1.call-done = f32[32,128,1,128]{3,1,2,0:T(8,128)} async-done(((f32[8,128,1,128]{3,1,2,0:T(8,128)}), f32[32,128,1,128]{3,1,2,0:T(8,128)}) %all-gather.3.cloned.1.call-update) | async-done | bytes 2097168 | tf_op jit(solution)/shard_map/all_gather | solution.py:27
  336.8 5.3 %while.10 = (s32[]{:T(128)}, f32[8,128,1,128]{3,2,1,0:T(1,128)S(1)}, s32[]{:T(128)}, f32[4,8,128,1,128]{4,2,1,3,0:T(8,128)}, s32[]{:T(128)}, /*index=5*/s32[]{:T(128)}, s32[]{:T(128)}) while((s32[]{:T(128)}, f32[8,128,1,128]{3,2,1,0:T(1,128)S(1)}, s32[]{:T(128)}, f32[4,8,128,1,128]{4,2,1,3,0:T(8,128)}, s32[]{:T(128)}, /*index=5*/s32[]{:T(128)}, ...), condition=%wide.region_2.3_spmd, body=%wide.region_1.2_spmd.sunk | while | flops 131077 | bytes 2621563 | solution.py:33
  336.8 1.1 constant_dynamic-slice_fusion.2
  338.5 1.1 constant_dynamic-slice_fusion.2
  340.2 1.1 constant_dynamic-slice_fusion.2
  342.2 4.4 %add_multiply_fusion = f32[8,128,16,128]{3,1,2,0:T(8,128)S(1)} fusion(f32[8,128,16,128]{3,1,2,0:T(8,128)} %fusion.36, f32[8,128,128]{2,1,0:T(8,128)S(1)} %bitcast.8), kind=kLoop, calls=%fused_computation.103 | loop fusion | flops 4194304 | bytes 17301504 | tf_op jit(solution)/shard_map/div | solution.py:67
  346.6 8.1 %copy.41 = f32[8,128,16,128]{3,2,1,0:T(8,128)} copy(f32[8,128,16,128]{3,1,2,0:T(8,128)S(1)} %add_multiply_fusion) | data formatting | bytes 16777216
  (46 shorter events, 10.2 us)
Async XLA Ops:
  7.2 329.4 %all-gather.3.cloned.1.call-start = ((), (), s32[]{:S(2)}) async-start(), calls=%async_computation | async-start | bytes 2621440 | tf_op jit(solution)/shard_map/all_gather | solution.py:27
  8.9 3.0 collective-permute-start
  9.6 6.4 %collective-permute-start.1 = (f32[1,128,16,128]{3,2,1,0:T(8,128)S(1)}, f32[1,128,16,128]{3,2,1,0:T(8,128)S(1)}, u32[]{:S(2)}, u32[]{:S(2)}) collective-permute-start(f32[1,128,16,128]{3,2,1,0:T(8,128)S(1)} %get-tuple-element.74), channel_id=1, source_target_pairs={{16,0},{0,16},{17,1},{1,17},{18,2},{2,18},{19,3},{3,19},{20,4},{4,... | collective-permute-start | bytes 3145736 | tf_op jit(solution)/shard_map/ppermute | solution.py:18
  16.1 38.7 %copy-start.2 = (f32[10,128,16,128]{3,2,1,0:T(8,128)}, f32[10,128,16,128]{3,2,1,0:T(8,128)S(1)}, u32[]{:S(2)}) copy-start(f32[10,128,16,128]{3,2,1,0:T(8,128)S(1)} %constant_dynamic-update-slice_fusion) | copy-start | bytes 31457284
  16.1 4.6 %collective-permute-start.2 = (f32[10,1,16,128]{3,2,1,0:T(8,128)S(1)}, f32[10,1,16,128]{3,2,1,0:T(8,128)S(1)}, u32[]{:S(2)}, u32[]{:S(2)}) collective-permute-start(f32[10,1,16,128]{3,2,1,0:T(8,128)S(1)} %get-tuple-element.66), channel_id=1, source_target_pairs={{0,4},{4,8},{8,12},{12,0},{1,5},{5,9},{9,13},{13,1},{2,6},{6,10},{... | collective-permute-start | bytes 245768 | tf_op jit(solution)/shard_map/ppermute | solution.py:16
  17.4 5.1 %collective-permute-start.3 = (f32[10,1,16,128]{3,2,1,0:T(8,128)S(1)}, f32[10,1,16,128]{3,2,1,0:T(8,128)S(1)}, u32[]{:S(2)}, u32[]{:S(2)}) collective-permute-start(f32[10,1,16,128]{3,2,1,0:T(8,128)S(1)} %get-tuple-element.67), channel_id=1, source_target_pairs={{4,0},{8,4},{12,8},{0,12},{5,1},{9,5},{13,9},{1,13},{6,2},{10,6},{... | collective-permute-start | bytes 245768 | tf_op jit(solution)/shard_map/ppermute | solution.py:18
  23.5 17.9 %collective-permute-start.5 = (f32[10,130,1,128]{3,1,2,0:T(8,128)S(1)}, f32[10,130,1,128]{3,1,2,0:T(8,128)S(1)}, u32[]{:S(2)}, u32[]{:S(2)}) collective-permute-start(f32[10,130,1,128]{3,1,2,0:T(8,128)S(1)} %copy.25), channel_id=1, source_target_pairs={{1,0},{2,1},{3,2},{0,3},{5,4},{6,5},{7,6},{4,7},{9,8},{10,9},{11,1... | collective-permute-start | bytes 1996808 | tf_op jit(solution)/shard_map/ppermute | solution.py:18
  23.8 31.0 %collective-permute-start.4 = (f32[10,130,1,128]{3,1,2,0:T(8,128)S(1)}, f32[10,130,1,128]{3,1,2,0:T(8,128)S(1)}, u32[]{:S(2)}, u32[]{:S(2)}) collective-permute-start(f32[10,130,1,128]{3,1,2,0:T(8,128)S(1)} %copy.23), channel_id=1, source_target_pairs={{0,1},{1,2},{2,3},{3,0},{4,5},{5,6},{6,7},{7,4},{8,9},{9,10},{10,1... | collective-permute-start | bytes 1996808 | tf_op jit(solution)/shard_map/ppermute | solution.py:16
  80.0 4.4 %collective-permute-start.6 = (f32[1,128,16,128]{3,2,1,0:T(8,128)S(1)}, f32[1,128,16,128]{3,2,1,0:T(8,128)S(1)}, u32[]{:S(2)}, u32[]{:S(2)}) collective-permute-start(f32[1,128,16,128]{3,2,1,0:T(8,128)S(1)} %get-tuple-element.72), channel_id=1, source_target_pairs={{0,16},{16,0},{1,17},{17,1},{2,18},{18,2},{3,19},{19,3},{4,20},{20... | collective-permute-start | bytes 3145736 | tf_op jit(solution)/shard_map/ppermute | solution.py:16
  82.1 3.8 %collective-permute-start.7 = (f32[1,128,16,128]{3,2,1,0:T(8,128)S(1)}, f32[1,128,16,128]{3,2,1,0:T(8,128)S(1)}, u32[]{:S(2)}, u32[]{:S(2)}) collective-permute-start(f32[1,128,16,128]{3,2,1,0:T(8,128)S(1)} %get-tuple-element.73), channel_id=1, source_target_pairs={{16,0},{0,16},{17,1},{1,17},{18,2},{2,18},{19,3},{3,19},{20,4},{4,... | collective-permute-start | bytes 3145736 | tf_op jit(solution)/shard_map/ppermute | solution.py:18
  85.9 7.7 %copy-start.3 = (f32[1,128,16,128]{3,2,1,0:T(8,128)}, f32[1,128,16,128]{3,2,1,0:T(8,128)S(1)}, u32[]{:S(2)}) copy-start(f32[1,128,16,128]{3,2,1,0:T(8,128)S(1)} %collective-permute-done.7) | copy-start | bytes 3145732
  85.9 4.6 %collective-permute-start.8 = (f32[10,1,16,128]{3,2,1,0:T(8,128)S(1)}, f32[10,1,16,128]{3,2,1,0:T(8,128)S(1)}, u32[]{:S(2)}, u32[]{:S(2)}) collective-permute-start(f32[10,1,16,128]{3,2,1,0:T(8,128)S(1)} %get-tuple-element.64), channel_id=1, source_target_pairs={{0,4},{4,8},{8,12},{12,0},{1,5},{5,9},{9,13},{13,1},{2,6},{6,10},{... | collective-permute-start | bytes 245768 | tf_op jit(solution)/shard_map/ppermute | solution.py:16
  87.4 4.3 %collective-permute-start.9 = (f32[10,1,16,128]{3,2,1,0:T(8,128)S(1)}, f32[10,1,16,128]{3,2,1,0:T(8,128)S(1)}, u32[]{:S(2)}, u32[]{:S(2)}) collective-permute-start(f32[10,1,16,128]{3,2,1,0:T(8,128)S(1)} %get-tuple-element.65), channel_id=1, source_target_pairs={{4,0},{8,4},{12,8},{0,12},{5,1},{9,5},{13,9},{1,13},{6,2},{10,6},{... | collective-permute-start | bytes 245768 | tf_op jit(solution)/shard_map/ppermute | solution.py:18
  93.6 18.0 %collective-permute-start.11 = (f32[10,130,1,128]{3,1,2,0:T(8,128)S(1)}, f32[10,130,1,128]{3,1,2,0:T(8,128)S(1)}, u32[]{:S(2)}, u32[]{:S(2)}) collective-permute-start(f32[10,130,1,128]{3,1,2,0:T(8,128)S(1)} %copy.29), channel_id=1, source_target_pairs={{1,0},{2,1},{3,2},{0,3},{5,4},{6,5},{7,6},{4,7},{9,8},{10,9},{11,1... | collective-permute-start | bytes 1996808 | tf_op jit(solution)/shard_map/ppermute | solution.py:18
  93.9 32.4 %collective-permute-start.10 = (f32[10,130,1,128]{3,1,2,0:T(8,128)S(1)}, f32[10,130,1,128]{3,1,2,0:T(8,128)S(1)}, u32[]{:S(2)}, u32[]{:S(2)}) collective-permute-start(f32[10,130,1,128]{3,1,2,0:T(8,128)S(1)} %copy.27), channel_id=1, source_target_pairs={{0,1},{1,2},{2,3},{3,0},{4,5},{5,6},{6,7},{7,4},{8,9},{9,10},{10,1... | collective-permute-start | bytes 1996808 | tf_op jit(solution)/shard_map/ppermute | solution.py:16
  143.8 14.1 %copy-start = (f32[8,128,16,128]{3,2,1,0:T(8,128)S(1)}, f32[8,128,16,128]{3,2,1,0:T(8,128)}, u32[]{:S(2)}) copy-start(f32[8,128,16,128]{3,2,1,0:T(8,128)} %fusion.22) | copy-start | bytes 25165828
  145.6 3.7 %collective-permute-start.12 = (f32[1,128,16,128]{3,2,1,0:T(8,128)S(1)}, f32[1,128,16,128]{3,2,1,0:T(8,128)S(1)}, u32[]{:S(2)}, u32[]{:S(2)}) collective-permute-start(f32[1,128,16,128]{3,2,1,0:T(8,128)S(1)} %get-tuple-element.70), channel_id=1, source_target_pairs={{0,16},{16,0},{1,17},{17,1},{2,18},{18,2},{3,19},{19,3},{4,20},{20... | collective-permute-start | bytes 3145736 | tf_op jit(solution)/shard_map/ppermute | solution.py:16
  147.0 3.8 %collective-permute-start.13 = (f32[1,128,16,128]{3,2,1,0:T(8,128)S(1)}, f32[1,128,16,128]{3,2,1,0:T(8,128)S(1)}, u32[]{:S(2)}, u32[]{:S(2)}) collective-permute-start(f32[1,128,16,128]{3,2,1,0:T(8,128)S(1)} %get-tuple-element.71), channel_id=1, source_target_pairs={{16,0},{0,16},{17,1},{1,17},{18,2},{2,18},{19,3},{3,19},{20,4},{4,... | collective-permute-start | bytes 3145736 | tf_op jit(solution)/shard_map/ppermute | solution.py:18
  150.8 8.9 %copy-start.4 = (f32[1,128,16,128]{3,2,1,0:T(8,128)}, f32[1,128,16,128]{3,2,1,0:T(8,128)S(1)}, u32[]{:S(2)}) copy-start(f32[1,128,16,128]{3,2,1,0:T(8,128)S(1)} %collective-permute-done.13) | copy-start | bytes 3145732
  151.8 4.6 %collective-permute-start.14 = (f32[10,1,16,128]{3,2,1,0:T(8,128)S(1)}, f32[10,1,16,128]{3,2,1,0:T(8,128)S(1)}, u32[]{:S(2)}, u32[]{:S(2)}) collective-permute-start(f32[10,1,16,128]{3,2,1,0:T(8,128)S(1)} %get-tuple-element.62), channel_id=1, source_target_pairs={{0,4},{4,8},{8,12},{12,0},{1,5},{5,9},{9,13},{13,1},{2,6},{6,10},{... | collective-permute-start | bytes 245768 | tf_op jit(solution)/shard_map/ppermute | solution.py:16
  153.2 4.7 %collective-permute-start.15 = (f32[10,1,16,128]{3,2,1,0:T(8,128)S(1)}, f32[10,1,16,128]{3,2,1,0:T(8,128)S(1)}, u32[]{:S(2)}, u32[]{:S(2)}) collective-permute-start(f32[10,1,16,128]{3,2,1,0:T(8,128)S(1)} %get-tuple-element.63), channel_id=1, source_target_pairs={{4,0},{8,4},{12,8},{0,12},{5,1},{9,5},{13,9},{1,13},{6,2},{10,6},{... | collective-permute-start | bytes 245768 | tf_op jit(solution)/shard_map/ppermute | solution.py:18
  159.8 17.8 %collective-permute-start.17 = (f32[10,130,1,128]{3,1,2,0:T(8,128)S(1)}, f32[10,130,1,128]{3,1,2,0:T(8,128)S(1)}, u32[]{:S(2)}, u32[]{:S(2)}) collective-permute-start(f32[10,130,1,128]{3,1,2,0:T(8,128)S(1)} %copy.33), channel_id=1, source_target_pairs={{1,0},{2,1},{3,2},{0,3},{5,4},{6,5},{7,6},{4,7},{9,8},{10,9},{11,1... | collective-permute-start | bytes 1996808 | tf_op jit(solution)/shard_map/ppermute | solution.py:18
  161.1 32.2 %collective-permute-start.16 = (f32[10,130,1,128]{3,1,2,0:T(8,128)S(1)}, f32[10,130,1,128]{3,1,2,0:T(8,128)S(1)}, u32[]{:S(2)}, u32[]{:S(2)}) collective-permute-start(f32[10,130,1,128]{3,1,2,0:T(8,128)S(1)} %copy.31), channel_id=1, source_target_pairs={{0,1},{1,2},{2,3},{3,0},{4,5},{5,6},{6,7},{7,4},{8,9},{9,10},{10,1... | collective-permute-start | bytes 1996808 | tf_op jit(solution)/shard_map/ppermute | solution.py:16
  210.8 13.6 %copy-start.1 = (f32[8,128,16,128]{3,2,1,0:T(8,128)S(1)}, f32[8,128,16,128]{3,2,1,0:T(8,128)}, u32[]{:S(2)}) copy-start(f32[8,128,16,128]{3,2,1,0:T(8,128)} %fusion.13) | copy-start | bytes 25165828
  212.6 3.3 collective-permute-start.18
  213.7 3.8 %collective-permute-start.19 = (f32[1,128,16,128]{3,2,1,0:T(8,128)S(1)}, f32[1,128,16,128]{3,2,1,0:T(8,128)S(1)}, u32[]{:S(2)}, u32[]{:S(2)}) collective-permute-start(f32[1,128,16,128]{3,2,1,0:T(8,128)S(1)} %get-tuple-element.69), channel_id=1, source_target_pairs={{16,0},{0,16},{17,1},{1,17},{18,2},{2,18},{19,3},{3,19},{20,4},{4,... | collective-permute-start | bytes 3145736 | tf_op jit(solution)/shard_map/ppermute | solution.py:18
  217.4 8.9 %copy-start.5 = (f32[1,128,16,128]{3,2,1,0:T(8,128)}, f32[1,128,16,128]{3,2,1,0:T(8,128)S(1)}, u32[]{:S(2)}) copy-start(f32[1,128,16,128]{3,2,1,0:T(8,128)S(1)} %collective-permute-done.19) | copy-start | bytes 3145732
  218.4 4.6 %collective-permute-start.20 = (f32[10,1,16,128]{3,2,1,0:T(8,128)S(1)}, f32[10,1,16,128]{3,2,1,0:T(8,128)S(1)}, u32[]{:S(2)}, u32[]{:S(2)}) collective-permute-start(f32[10,1,16,128]{3,2,1,0:T(8,128)S(1)} %get-tuple-element.60), channel_id=1, source_target_pairs={{0,4},{4,8},{8,12},{12,0},{1,5},{5,9},{9,13},{13,1},{2,6},{6,10},{... | collective-permute-start | bytes 245768 | tf_op jit(solution)/shard_map/ppermute | solution.py:16
  219.9 4.5 %collective-permute-start.21 = (f32[10,1,16,128]{3,2,1,0:T(8,128)S(1)}, f32[10,1,16,128]{3,2,1,0:T(8,128)S(1)}, u32[]{:S(2)}, u32[]{:S(2)}) collective-permute-start(f32[10,1,16,128]{3,2,1,0:T(8,128)S(1)} %get-tuple-element.61), channel_id=1, source_target_pairs={{4,0},{8,4},{12,8},{0,12},{5,1},{9,5},{13,9},{1,13},{6,2},{10,6},{... | collective-permute-start | bytes 245768 | tf_op jit(solution)/shard_map/ppermute | solution.py:18
  226.4 17.9 %collective-permute-start.23 = (f32[10,130,1,128]{3,1,2,0:T(8,128)S(1)}, f32[10,130,1,128]{3,1,2,0:T(8,128)S(1)}, u32[]{:S(2)}, u32[]{:S(2)}) collective-permute-start(f32[10,130,1,128]{3,1,2,0:T(8,128)S(1)} %copy.37), channel_id=1, source_target_pairs={{1,0},{2,1},{3,2},{0,3},{5,4},{6,5},{7,6},{4,7},{9,8},{10,9},{11,1... | collective-permute-start | bytes 1996808 | tf_op jit(solution)/shard_map/ppermute | solution.py:18
  227.2 33.4 %collective-permute-start.22 = (f32[10,130,1,128]{3,1,2,0:T(8,128)S(1)}, f32[10,130,1,128]{3,1,2,0:T(8,128)S(1)}, u32[]{:S(2)}, u32[]{:S(2)}) collective-permute-start(f32[10,130,1,128]{3,1,2,0:T(8,128)S(1)} %copy.35), channel_id=1, source_target_pairs={{0,1},{1,2},{2,3},{3,0},{4,5},{5,6},{6,7},{7,4},{8,9},{9,10},{10,1... | collective-permute-start | bytes 1996808 | tf_op jit(solution)/shard_map/ppermute | solution.py:16
Sparse Core Ops, SparseCore 0:
  291.8 44.6 all-gather.2
where the time goes:
time: 362 us
  waiting for transfers between devices  185 us (51%)
  other arithmetic  98.8 us (27%)
  local copies, waits for them, and re-layouts  34.1 us (9%)
  starting transfers between devices  29.1 us (8%)
  between operations  14.3 us (4%)
    add x4, other arithmetic, march_step(): return middle + 0.1 * spread + 0.2 * middle * (1.0 - middle * crowding)  72.4 us
    ppermute x12, waiting for transfers between devices, with_halo(): lax.ppermute(tail, axis, [(i, (i + 1) % count) for i in range(count)])  72.1 us
    ppermute x12, waiting for transfers between devices, with_halo(): lax.ppermute(head, axis, [((i + 1) % count, i) for i in range(count)])  67.8 us
    all_gather x1, waiting for transfers between devices, entering(): gathered = lax.all_gather(part, axis)  44.8 us
    ppermute x12, starting transfers between devices, with_halo(): lax.ppermute(tail, axis, [(i, (i + 1) % count) for i in range(count)])  22.3 us
    unnamed x15, local copies, waits for them, and re-layouts  12.2 us
    another operation x1, other arithmetic, per_device(): here = jnp.cumsum(field_values, axis=2)  11.6 us
    slice x7, other arithmetic, with_halo(): lax.slice_in_dim(cells, cells.shape[dim] - width, cells.shape[dim], axis=...  8.7 us
  transfers between devices with their start and end apart: 25, of which 24 were waited for; matrix products, arithmetic and copies ran while one was open for 3% of the time, Pallas kernels for 0%

commit v1 on v0

v1 whole, which is shorter than its diff:
```python
import functools

import jax
import jax.numpy as jnp
from jax import lax
from jax.experimental import pallas as pl
from jax.experimental.pallas import tpu as pltpu
from jax.sharding import PartitionSpec as P

STEPS = 4
TILE = 8
PARTS = 2
MIB = 1024 * 1024


CHUNKS = 8
VMEM = pl.BlockSpec(memory_space=pltpu.VMEM)
HBM = pl.BlockSpec(memory_space=pltpu.HBM)


def ups(count):
    return [(i, (i + 1) % count) for i in range(count)]


def downs(count):
    return [((i + 1) % count, i) for i in range(count)]


def like(shape, array):
    return jax.ShapeDtypeStruct(shape, array.dtype)


def add_faces(cells, low, high):
    depth = cells.shape[-2]
    layer = lax.broadcasted_iota(jnp.int32, cells.shape, cells.ndim - 2)
    cells = jnp.where(layer == 0, jnp.expand_dims(low, -2), cells)
    return jnp.where(layer == depth - 1, jnp.expand_dims(high, -2), cells)


def peel_kernel(f_ref, h_ref, low_ref, high_ref, both_ref, first_ref, final_ref, ground_ref, sems):
    ground_ref[...] = jnp.full(ground_ref.shape, jnp.where(lax.axis_index("lev") == 0, 1.0, 0.0), ground_ref.dtype)
    rows, span, depth, _ = h_ref.shape
    chunk = span // CHUNKS
    copies = []
    for k in range(CHUNKS):
        part = pl.ds(k * chunk, chunk)
        copies.append(pltpu.make_async_copy(f_ref.at[:, part], h_ref.at[:, part], sems.at[k]))
        copies[-1].start()

    def one(at, _):
        for row in range(rows):
            low_ref[row, pl.ds(at, 1), :] = h_ref[row, at, pl.ds(0, 1), :]
            high_ref[row, pl.ds(at, 1), :] = h_ref[row, at, pl.ds(depth - 1, 1), :]
        both_ref[0, at] = h_ref[0, at]
        both_ref[1, at] = h_ref[rows - 1, at]
        return 0

    for k in range(CHUNKS):
        copies[k].wait()
        lax.fori_loop(k * chunk, (k + 1) * chunk, one, 0)
    for row in range(rows):
        first_ref[row] = h_ref[row, 0]
        final_ref[row] = h_ref[row, span - 1]


def peel(field):
    rows, span, depth, lanes = field.shape
    face = like((rows, span, lanes), field)
    edge = like((rows, depth, lanes), field)
    return pl.pallas_call(
        peel_kernel,
        in_specs=[HBM],
        out_specs=[VMEM] * 7,
        out_shape=[like(field.shape, field), face, face, like((2, span, depth, lanes), field), edge, edge, like((1, 1, lanes), field)],
        scratch_shapes=[pltpu.SemaphoreType.DMA((CHUNKS,))],
        compiler_params=pltpu.CompilerParams(vmem_limit_bytes=2 * MIB),
        cost_estimate=pl.CostEstimate(flops=4 * field.size, bytes_accessed=field.size, transcendentals=0),
        name="peel",
    )(field)


def march_kernel(fixed, last, ylow_at, yhigh_at, *refs):
    refs = list(refs)
    h_ref = refs.pop(0)
    low_ref, high_ref = (refs.pop(0), refs.pop(0)) if fixed else (None, None)
    xlow_ref, xhigh_ref, ylow_ref, yhigh_ref, c_ref, out_ref = refs[:6]
    refs = refs[6:]
    rows, span, depth, lanes = h_ref.shape
    tiles = depth // TILE
    sub = lax.broadcasted_iota(jnp.int32, (TILE, lanes), 0)
    first, final = sub == 0, sub == TILE - 1

    def tile(t):
        return pl.ds(t * TILE, TILE)

    def cells_at(at):
        out = []
        for row in range(rows):
            cells = [h_ref[row, at, tile(t), :] for t in range(tiles)]
            if fixed:
                cells[0] = jnp.where(first, low_ref[row, pl.ds(at, 1), :], cells[0])
                cells[-1] = jnp.where(final, high_ref[row, pl.ds(at, 1), :], cells[-1])
            out.append(cells)
        return out

    def edge(ref):
        return [[ref[row, tile(t), :] for t in range(tiles)] for row in range(rows)]

    def one(at, before, here, after):
        for row in range(rows):
            mids = here[row]
            down = [pltpu.roll(m, 1, 0) for m in mids]
            up = [pltpu.roll(m, TILE - 1, 0) for m in mids]
            news = []
            for t in range(tiles):
                ylow = ylow_ref[ylow_at, at, tile(t), :] if row == 0 else here[row - 1][t]
                yhigh = yhigh_ref[yhigh_at, at, tile(t), :] if row == rows - 1 else here[row + 1][t]
                around = (ylow + yhigh) + (before[row][t] + after[row][t])
                around = around + jnp.where(first, down[t - 1] if t else 0.0, down[t])
                around = around + jnp.where(final, up[t + 1] if t < tiles - 1 else 0.0, up[t])
                mid = mids[t]
                new = mid * (0.6 - 0.2 * (mid * c_ref[row, at, tile(t), :])) + 0.1 * around
                out_ref[row, at, tile(t), :] = new
                news.append(new)
            if last:
                total = functools.reduce(jnp.add, news)
                refs[0][row, pl.ds(at, 1), :] = jnp.sum(total, axis=0, keepdims=True)
            else:
                refs[0][row, pl.ds(at, 1), :] = news[0][:1]
                refs[1][row, pl.ds(at, 1), :] = news[-1][TILE - 1 :]

    def step(at, carry):
        before, here = carry
        after = cells_at(at + 1)
        one(at, before, here, after)
        return here, after

    before, here = lax.fori_loop(0, span - 1, step, (edge(xlow_ref), cells_at(0)))
    one(span - 1, before, here, edge(xhigh_ref))


def march(h, faces, xlow, xhigh, ylow, yhigh, crowding, last):
    rows, span, _, lanes = h.shape
    face = like((rows, span, lanes), h)
    count = 1 if last else 2
    operands = [h, *(faces or ()), xlow, xhigh, ylow[0], yhigh[0], crowding]
    return pl.pallas_call(
        functools.partial(march_kernel, faces is not None, last, ylow[1], yhigh[1]),
        in_specs=[VMEM] * len(operands),
        out_specs=[VMEM] * (1 + count),
        out_shape=[like(h.shape, h)] + [face] * count,
        input_output_aliases={0: 0},
        compiler_params=pltpu.CompilerParams(vmem_limit_bytes=2 * MIB),
        cost_estimate=pl.CostEstimate(flops=16 * h.size, bytes_accessed=12 * h.size, transcendentals=0),
        name="march",
    )(*operands)


def end_kernel(h_ref, low_ref, high_ref, end_ref, sum_ref, stage, sems):
    rows, span, depth, lanes = h_ref.shape
    tiles = depth // TILE
    chunk = span // CHUNKS
    sub = lax.broadcasted_iota(jnp.int32, (TILE, lanes), 0)

    def copy(k):
        return pltpu.make_async_copy(stage.at[k % 2], end_ref.at[:, pl.ds(k * chunk, chunk)], sems.at[k])

    for k in range(CHUNKS):
        if k >= 2:
            copy(k - 2).wait()

        def one(step, _):
            at = step + k * chunk
            held = [[h_ref[row, at, pl.ds(t * TILE, TILE), :] for t in range(tiles)] for row in range(rows)]
            for row in range(rows):
                carry = None
                for t in range(tiles):
                    part = pl.ds(t * TILE, TILE)
                    cells = held[row][t]
                    end = cells
                    if t == 0:
                        end = end + jnp.where(sub == 0, low_ref[row, pl.ds(at, 1), :], 0.0)
                    if t == tiles - 1:
                        end = end + jnp.where(sub == TILE - 1, high_ref[row, pl.ds(at, 1), :], 0.0)
                    stage[k % 2, row, step, part, :] = end
                    shift = 1
                    while shift < TILE:
                        cells = cells + jnp.where(sub >= shift, pltpu.roll(cells, shift, 0), 0.0)
                        shift *= 2
                    held[row][t] = cells if carry is None else cells + carry
                    carry = held[row][t][TILE - 1 :]
            for row in range(rows):
                for t in range(tiles):
                    sum_ref[row, at, pl.ds(t * TILE, TILE), :] = held[row][t]
            return 0

        lax.fori_loop(0, chunk, one, 0)
        copy(k).start()
    for k in (CHUNKS - 2, CHUNKS - 1):
        copy(k).wait()


def end(h, low, high):
    rows, span, depth, lanes = h.shape
    return pl.pallas_call(
        end_kernel,
        in_specs=[VMEM] * 3,
        out_specs=[HBM, VMEM],
        out_shape=[like(h.shape, h)] * 2,
        scratch_shapes=[pltpu.VMEM((2, rows, span // CHUNKS, depth, lanes), h.dtype), pltpu.SemaphoreType.DMA((CHUNKS,))],
        input_output_aliases={0: 1},
        compiler_params=pltpu.CompilerParams(vmem_limit_bytes=4 * MIB),
        cost_estimate=pl.CostEstimate(flops=12 * h.size, bytes_accessed=12 * h.size, transcendentals=0),
        name="end",
    )(h, low, high)


def potential_kernel(scale, offset, sum_ref, prior_ref, got_ref, rest_ref, high_ref, *refs):
    pot_ref, stage, sems = refs[-3:]
    rows, span, depth, lanes = stage.shape
    chunk = span // CHUNKS
    layer = lax.broadcasted_iota(jnp.int32, (depth, lanes), 0)

    def one(at, _):
        for row in range(rows):
            base = prior_ref[row, pl.ds(at, 1), :] + got_ref[row, pl.ds(at, 1), :]
            base = base + rest_ref[row + offset, pl.ds(at, 1), :]
            high = high_ref[row + offset, pl.ds(at, 1), :]
            cells = sum_ref[row + offset, at] + base
            stage[row, at] = (cells + jnp.where(layer == depth - 1, high, 0.0)) * scale
        return 0

    copies = []
    for k in range(CHUNKS):
        lax.fori_loop(k * chunk, (k + 1) * chunk, one, 0)
        part = pl.ds(k * chunk, chunk)
        copies.append(pltpu.make_async_copy(stage.at[:, part], pot_ref.at[pl.ds(offset, rows), part], sems.at[k]))
        copies[-1].start()
    for copy in copies:
        copy.wait()


def potential(sums, prior, got, rest, high, scale, part, made):
    _, span, depth, lanes = sums.shape
    some = got.shape[0]
    return pl.pallas_call(
        functools.partial(potential_kernel, scale, part * some),
        in_specs=[VMEM] * 5 + ([] if made is None else [HBM]),
        out_specs=HBM,
        out_shape=like(sums.shape, sums),
        scratch_shapes=[pltpu.VMEM((some, span, depth, lanes), sums.dtype), pltpu.SemaphoreType.DMA((CHUNKS,))],
        input_output_aliases={} if made is None else {5: 0},
        compiler_params=pltpu.CompilerParams(vmem_limit_bytes=(2 + 8 // PARTS) * MIB),
        cost_estimate=pl.CostEstimate(flops=2 * sums.size, bytes_accessed=8 * sums.size // PARTS, transcendentals=0),
        name="potential",
    )(sums, prior, got, rest, high, *(() if made is None else (made,)))


def side_halos(both, first, final):
    lats, lons = lax.axis_size("lat"), lax.axis_size("lon")
    if lats == 2:
        swapped = lax.ppermute(both, "lat", [(0, 1), (1, 0)])
        ylow, yhigh = (swapped, 1), (swapped, 0)
    else:
        ylow = (lax.ppermute(both[1:], "lat", ups(lats)), 0)
        yhigh = (lax.ppermute(both[:1], "lat", downs(lats)), 0)
    xlow = lax.ppermute(final, "lon", ups(lons))
    xhigh = lax.ppermute(first, "lon", downs(lons))
    return xlow, xhigh, ylow, yhigh


def edges(h, low, high):
    rows, span = h.shape[:2]
    both = jnp.stack([add_faces(h[y], low[y], high[y]) for y in (0, rows - 1)])
    first, final = (add_faces(h[:, x], low[:, x], high[:, x]) for x in (0, span - 1))
    return both, first, final


def steps(field, crowding):
    levs = lax.axis_size("lev")
    depth = field.shape[2]
    faces = None
    h, low, high, both, first, final, ground = peel(field)
    for step in range(STEPS):
        last = step == STEPS - 1
        above = lax.ppermute(low, "lev", downs(levs))
        below = lax.ppermute(high, "lev", ups(levs))
        halos = side_halos(both, first, final)
        outs = march(h, faces, *halos, crowding, last)
        h = outs[0]
        if not last:
            low = outs[1] + 0.1 * below
            high = outs[2] + 0.1 * above
            faces = (low, high)
            both, first, final = edges(h, low, high)
    rest = 0.1 * jnp.where(ground > 0.0, below, low)
    own = outs[1] + 0.1 * high + rest
    top = 0.1 * above
    field_end, sums = end(h, 0.1 * below, top)
    rows = own.shape[0] // PARTS
    made = None
    for part in range(PARTS):
        mine = own[part * rows : (part + 1) * rows]
        before, got = jnp.zeros_like(mine), jnp.zeros_like(mine)
        for hop in range(levs - 1):
            before = before + got
            got = lax.ppermute(before + mine, "lev", [(hop, hop + 1)])
        made = potential(sums, before, got, rest, top, 1.0 / (depth * levs), part, made)
    return made, field_end


def solution(mesh):
    return jax.shard_map(
        steps,
        mesh=mesh,
        in_specs=(P("lat", "lon", "lev", None), P("lat", "lon", "lev", None)),
        out_specs=(P("lat", "lon", "lev", None), P("lat", "lon", "lev", None)),
        check_vma=False,
    )
```

time: 362 us -> 156 us (0.43)
  the two profiles are of different devices: /device:TPU:25 before, /device:TPU:23 now
where the time goes in v1:
time: 156 us; the launch traced here: 155 us
  waiting for transfers between devices  83 us (53%)
  Pallas kernels  38.5 us (25%)
  starting transfers between devices  26.7 us (17%)
  local copies, waits for them, and re-layouts  3.51 us (2%)
  other arithmetic  2.72 us (2%)
    ppermute x4, waiting for transfers between devices, steps(): below = lax.ppermute(high, 'lev', ups(levs))  40.3 us
    ppermute x6, waiting for transfers between devices, steps(): got = lax.ppermute(before + mine, 'lev', [(hop, hop + 1)])  28.3 us
    pallas_call x4, Pallas kernels, march(): pl.pallas_call(functools.partial(march_kernel, faces is not None, last, y...  24.1 us
    ppermute x4, waiting for transfers between devices, steps(): above = lax.ppermute(low, 'lev', downs(levs))  7.71 us
    ppermute x6, starting transfers between devices, steps(): got = lax.ppermute(before + mine, 'lev', [(hop, hop + 1)])  6.54 us
    pallas_call x1, Pallas kernels, end(): pl.pallas_call(end_kernel, in_specs=[VMEM] * 3, out_specs=[HBM, VMEM], ou...  6.54 us
    ppermute x4, starting transfers between devices, side_halos(): xlow = lax.ppermute(final, 'lon', ups(lons))  6.19 us
    pallas_call x2, Pallas kernels, potential(): pl.pallas_call(functools.partial(potential_kernel, scale, part * some), i...  5.79 us
  transfers between devices with their start and end apart: 26, of which 17 were waited for; matrix products, arithmetic and copies ran while one was open for 0% of the time, Pallas kernels for 22%

profile of v1, /device:TPU:23, one launch (start us, length us, event | category | flops | bytes accessed | tf_op | source)
XLA Modules:
  0.0 155.4 jit_solution(15708673485771447707)
XLA Ops:
  0.6 3.4 %copy-done.1 = f32[8,128,16,128]{3,2,1,0:T(8,128)S(1)} copy-done((f32[8,128,16,128]{3,2,1,0:T(8,128)S(1)}, f32[8,128,16,128]{3,2,1,0:T(8,128)}, u32[]{:S(2)}) %copy-start.1) | copy-done | bytes 8388632
  4.0 2.1 %peel.1 = (f32[8,128,16,128]{3,2,1,0:T(8,128)S(1)}, f32[8,128,128]{2,1,0:T(8,128)S(1)}, f32[8,128,128]{2,1,0:T(8,128)S(1)}, f32[2,128,16,128]{3,2,1,0:T(8,128)S(...) custom-call(f32[8,128,16,128]{3,2,1,0:T(8,128)S(1)} %copy-done.1), custom_call_target="tpu_custom_call" | custom-call | flops 8388608 | bytes 2097152 | tf_op jit(solution)/shard_map/peel/pallas_call | solution.py:70
  6.1 0.7 collective-permute-start.2
  6.9 0.2 collective-permute-start.4
  7.0 0.2 collective-permute-start
  7.2 1.3 collective-permute-start.1
  8.5 1.3 collective-permute-start.3
  9.8 0.6 collective-permute-done.refs_1_
  10.4 1.2 collective-permute-done.1.refs_2_
  11.6 5.1 %march.4 = (f32[8,128,16,128]{3,2,1,0:T(8,128)S(1)}, f32[8,128,128]{2,1,0:T(8,128)S(1)}, f32[8,128,128]{2,1,0:T(8,128)S(1)}) custom-call(f32[8,128,16,128]{3,2,1,0:T(8,128)S(1)} %get-tuple-element.22.refs_0_, f32[8,16,128]{2,1,0:T(8,128)S(1)} %collective-permute-done.refs_1_, ...), custom_call_target="tpu_custom_call", output_to_operand_aliasing={{0}: (0, {})} | custom-call | flops 33554432 | bytes 25165824 | tf_op jit(solution)/shard_map/march/pallas_call | solution.py:147
  16.7 3.5 %collective-permute-done.4 = f32[8,128,128]{2,1,0:T(8,128)S(1)} collective-permute-done((f32[8,128,128]{2,1,0:T(8,128)S(1)}, f32[8,128,128]{2,1,0:T(8,128)S(1)}, u32[]{:S(2)}, u32[]{:S(2)}) %collective-permute-start.4) | collective-permute-done | bytes 524320 | tf_op jit(solution)/shard_map/ppermute | solution.py:286
  20.4 12.9 %collective-permute-done.3 = f32[8,128,128]{2,1,0:T(8,128)S(1)} collective-permute-done((f32[8,128,128]{2,1,0:T(8,128)S(1)}, f32[8,128,128]{2,1,0:T(8,128)S(1)}, u32[]{:S(2)}, u32[]{:S(2)}) %collective-permute-start.3) | collective-permute-done | bytes 524320 | tf_op jit(solution)/shard_map/ppermute | solution.py:287
  33.4 0.4 select_select_fusion.5
  33.8 0.1 pad_maximum_fusion
  33.9 0.8 collective-permute-start.7
  34.8 0.6 collective-permute-start.9
  35.4 0.1 fusion.9
  35.5 0.3 collective-permute-start.6
  35.8 2.1 %collective-permute-start.5 = (f32[8,16,128]{2,1,0:T(8,128)S(1)}, f32[8,16,128]{2,1,0:T(8,128)S(1)}, u32[]{:S(2)}, u32[]{:S(2)}) collective-permute-start(f32[8,16,128]{2,1,0:T(8,128)S(1)} %get-tuple-element.59), channel_id=1, source_target_pairs={{0,4},{4,8},{8,12},{12,0},{1,5},{5,9},{9,13},{13,1},{2,6},{6,10},{... | collective-permute-start | bytes 196616 | tf_op jit(solution)/shard_map/ppermute | solution.py:267
  37.9 0.9 collective-permute-start.8
  38.8 0.8 collective-permute-done.6.refs_4_
  39.6 0.6 collective-permute-done.5.refs_3_
  40.2 6.0 %march.5 = (f32[8,128,16,128]{3,2,1,0:T(8,128)S(1)}, f32[8,128,128]{2,1,0:T(8,128)S(1)}, f32[8,128,128]{2,1,0:T(8,128)S(1)}) custom-call(f32[8,128,16,128]{3,2,1,0:T(8,128)S(1)} %get-tuple-element.26.refs_0_, f32[8,128,128]{2,1,0:T(8,128)S(1)} %multiply_add_fusion.5.refs_1_, ...), custom_call_target="tpu_custom_call", output_to_operand_aliasing={{0}: (0, {})} | custom-call | flops 33554432 | bytes 25165824 | tf_op jit(solution)/shard_map/march/pallas_call | solution.py:147
  46.2 1.9 %collective-permute-done.9 = f32[8,128,128]{2,1,0:T(8,128)S(1)} collective-permute-done((f32[8,128,128]{2,1,0:T(8,128)S(1)}, f32[8,128,128]{2,1,0:T(8,128)S(1)}, u32[]{:S(2)}, u32[]{:S(2)}) %collective-permute-start.9) | collective-permute-done | bytes 524320 | tf_op jit(solution)/shard_map/ppermute | solution.py:286
  48.3 13.5 %collective-permute-done.8 = f32[8,128,128]{2,1,0:T(8,128)S(1)} collective-permute-done((f32[8,128,128]{2,1,0:T(8,128)S(1)}, f32[8,128,128]{2,1,0:T(8,128)S(1)}, u32[]{:S(2)}, u32[]{:S(2)}) %collective-permute-start.8) | collective-permute-done | bytes 524320 | tf_op jit(solution)/shard_map/ppermute | solution.py:287
  61.8 0.1 multiply_add_fusion.3.refs_1_
  61.9 0.4 select_select_fusion.3
  62.3 0.1 pad_maximum_fusion.1
  62.4 0.6 collective-permute-start.12
  63.0 0.3 collective-permute-start.14
  63.3 0.1 fusion.5
  63.4 0.5 collective-permute-start.11
  63.9 1.9 %collective-permute-start.10 = (f32[8,16,128]{2,1,0:T(8,128)S(1)}, f32[8,16,128]{2,1,0:T(8,128)S(1)}, u32[]{:S(2)}, u32[]{:S(2)}) collective-permute-start(f32[8,16,128]{2,1,0:T(8,128)S(1)} %get-tuple-element.55), channel_id=1, source_target_pairs={{0,4},{4,8},{8,12},{12,0},{1,5},{5,9},{9,13},{13,1},{2,6},{6,10},{... | collective-permute-start | bytes 196616 | tf_op jit(solution)/shard_map/ppermute | solution.py:267
  65.8 1.1 collective-permute-start.13
  67.0 0.5 collective-permute-done.11.refs_4_
  67.5 0.6 collective-permute-done.10.refs_3_
  68.1 6.0 %march.6 = (f32[8,128,16,128]{3,2,1,0:T(8,128)S(1)}, f32[8,128,128]{2,1,0:T(8,128)S(1)}, f32[8,128,128]{2,1,0:T(8,128)S(1)}) custom-call(f32[8,128,16,128]{3,2,1,0:T(8,128)S(1)} %get-tuple-element.31.refs_0_, f32[8,128,128]{2,1,0:T(8,128)S(1)} %multiply_add_fusion.3.refs_1_, ...), custom_call_target="tpu_custom_call", output_to_operand_aliasing={{0}: (0, {})} | custom-call | flops 33554432 | bytes 25165824 | tf_op jit(solution)/shard_map/march/pallas_call | solution.py:147
  74.2 2.2 %collective-permute-done.14 = f32[8,128,128]{2,1,0:T(8,128)S(1)} collective-permute-done((f32[8,128,128]{2,1,0:T(8,128)S(1)}, f32[8,128,128]{2,1,0:T(8,128)S(1)}, u32[]{:S(2)}, u32[]{:S(2)}) %collective-permute-start.14) | collective-permute-done | bytes 524320 | tf_op jit(solution)/shard_map/ppermute | solution.py:286
  76.5 13.4 %collective-permute-done.13 = f32[8,128,128]{2,1,0:T(8,128)S(1)} collective-permute-done((f32[8,128,128]{2,1,0:T(8,128)S(1)}, f32[8,128,128]{2,1,0:T(8,128)S(1)}, u32[]{:S(2)}, u32[]{:S(2)}) %collective-permute-start.13) | collective-permute-done | bytes 524320 | tf_op jit(solution)/shard_map/ppermute | solution.py:287
  89.9 0.4 select_select_fusion.1
  90.3 0.1 pad_maximum_fusion.2
  90.5 0.6 collective-permute-start.17
  91.0 1.2 collective-permute-start.18
  92.3 0.1 fusion.1
  92.3 0.5 collective-permute-start.16
  92.8 1.9 %collective-permute-start.15 = (f32[8,16,128]{2,1,0:T(8,128)S(1)}, f32[8,16,128]{2,1,0:T(8,128)S(1)}, u32[]{:S(2)}, u32[]{:S(2)}) collective-permute-start(f32[8,16,128]{2,1,0:T(8,128)S(1)} %get-tuple-element.51), channel_id=1, source_target_pairs={{0,4},{4,8},{8,12},{12,0},{1,5},{5,9},{9,13},{13,1},{2,6},{6,10},{... | collective-permute-start | bytes 196616 | tf_op jit(solution)/shard_map/ppermute | solution.py:267
  94.8 1.6 %collective-permute-done.16.refs_4_ = f32[8,16,128]{2,1,0:T(8,128)S(1)} collective-permute-done((f32[8,16,128]{2,1,0:T(8,128)S(1)}, f32[8,16,128]{2,1,0:T(8,128)S(1)}, u32[]{:S(2)}, u32[]{:S(2)}) %collective-permute-start.16) | collective-permute-done | bytes 65568 | tf_op jit(solution)/shard_map/ppermute | solution.py:268
  96.4 0.6 collective-permute-done.15.refs_3_
  97.1 6.9 %march.7 = (f32[8,128,16,128]{3,2,1,0:T(8,128)S(1)}, f32[8,128,128]{2,1,0:T(8,128)S(1)}) custom-call(f32[8,128,16,128]{3,2,1,0:T(8,128)S(1)} %get-tuple-element.34.refs_0_, f32[8,128,128]{2,1,0:T(8,128)S(1)} %multiply_add_fusion.1.refs_1_, f32[8,128,128]{2,1,0:T(8,128)S(1)} %multiply_add_fusion.refs_2_, ...), custom_call_target="tpu_custom_call", output_to_operand_aliasing={{0}: (0, {})} | custom-call | flops 33554432 | bytes 25165824 | tf_op jit(solution)/shard_map/march/pallas_call | solution.py:147
  104.0 0.5 collective-permute-done.18
  104.5 0.2 add_add_fusion
  104.7 0.7 collective-permute-start.23
  105.4 1.3 collective-permute-start.24
  106.7 0.7 collective-permute-start.20
  107.4 12.7 %collective-permute-done.24 = f32[4,128,128]{2,1,0:T(8,128)S(1)} collective-permute-done((f32[4,128,128]{2,1,0:T(8,128)S(1)}, f32[4,128,128]{2,1,0:T(8,128)S(1)}, u32[]{:S(2)}, u32[]{:S(2)}) %collective-permute-start.24) | collective-permute-done | bytes 262176 | tf_op jit(solution)/shard_map/ppermute | solution.py:307
  120.1 0.1 slice_add_fusion
  120.2 1.3 collective-permute-start.21
  121.5 3.2 %collective-permute-start.19 = (f32[8,128,128]{2,1,0:T(8,128)S(1)}, f32[8,128,128]{2,1,0:T(8,128)S(1)}, u32[]{:S(2)}, u32[]{:S(2)}) collective-permute-start(f32[8,128,128]{2,1,0:T(8,128)S(1)} %multiply_add_fusion.1.refs_1_), channel_id=1, source_target_pairs={{1,0},{2,1},{3,2},{0,3},{5,4},{6,5},{7,6},{4,7},{9,8},{10,9},{11,1... | collective-permute-start | bytes 1572872 | tf_op jit(solution)/shard_map/ppermute | solution.py:286
  124.7 1.3 collective-permute-start.25
  126.0 15.7 %collective-permute-done.21 = f32[4,128,128]{2,1,0:T(8,128)S(1)} collective-permute-done((f32[4,128,128]{2,1,0:T(8,128)S(1)}, f32[4,128,128]{2,1,0:T(8,128)S(1)}, u32[]{:S(2)}, u32[]{:S(2)}) %collective-permute-start.21) | collective-permute-done | bytes 262176 | tf_op jit(solution)/shard_map/ppermute | solution.py:307
  141.7 1.3 collective-permute-start.22
  143.1 6.5 %end.1 = (f32[8,128,16,128]{3,2,1,0:T(8,128)}, f32[8,128,16,128]{3,2,1,0:T(8,128)S(1)}) custom-call(f32[8,128,16,128]{3,2,1,0:T(8,128)S(1)} %get-tuple-element.37.h_ref, f32[8,128,128]{2,1,0:T(8,128)S(1)} %get-tuple-element.63.low_ref, f32[8,128,128]{2,1,0:T(8,128)S(1)} %broadcast_multiply_fusion.high_ref), custom_call_target="tpu_custom_call", output_to_operand_aliasing={{1}: (0, {})} | custom-call | flops 25165824 | bytes 25165824 | tf_op jit(solution)/shard_map/end/pallas_call | solution.py:205
  149.6 2.9 %potential.2.refs_0_ = f32[8,128,16,128]{3,2,1,0:T(8,128)} custom-call(f32[8,128,16,128]{3,2,1,0:T(8,128)S(1)} %get-tuple-element.38.sum_ref, f32[4,128,128]{2,1,0:T(8,128)S(1)} %get-tuple-element.43.prior_ref, f32[4,128,128]{2,1,0:T(8,128)S(1)} %collective-permute-done.25.got_ref, f32[8,128,128]{2,1,0:T(8,128)S(1)} %get-tuple-element.47.rest_ref, ...), custom_call_target="tpu_custom_call" | custom-call | flops 4194304 | bytes 8388608 | tf_op jit(solution)/shard_map/potential/pallas_call | solution.py:246
  152.5 2.9 %potential.3 = f32[8,128,16,128]{3,2,1,0:T(8,128)} custom-call(f32[8,128,16,128]{3,2,1,0:T(8,128)S(1)} %get-tuple-element.38.sum_ref, f32[4,128,128]{2,1,0:T(8,128)S(1)} %get-tuple-element.45.prior_ref, f32[4,128,128]{2,1,0:T(8,128)S(1)} %collective-permute-done.22.got_ref, ...), custom_call_target="tpu_custom_call", output_to_operand_aliasing={{}: (5, {})} | custom-call | flops 4194304 | bytes 8388608 | tf_op jit(solution)/shard_map/potential/pallas_call | solution.py:246
  (35 shorter events, 0.7 us)
Async XLA Ops:
  0.6 3.4 %copy-start.1 = (f32[8,128,16,128]{3,2,1,0:T(8,128)S(1)}, f32[8,128,16,128]{3,2,1,0:T(8,128)}, u32[]{:S(2)}) copy-start(f32[8,128,16,128]{3,2,1,0:T(8,128)} %f_ref.1) | copy-start | bytes 25165828
  4.0 7.6 %copy-start = (f32[8,128,16,128]{3,2,1,0:T(8,128)S(1)}, f32[8,128,16,128]{3,2,1,0:T(8,128)}, u32[]{:S(2)}) copy-start(f32[8,128,16,128]{3,2,1,0:T(8,128)} %refs_7_.5) | copy-start | bytes 25165828
  6.1 5.5 %collective-permute-start.2 = (f32[2,128,16,128]{3,2,1,0:T(8,128)S(1)}, f32[2,128,16,128]{3,2,1,0:T(8,128)S(1)}, u32[]{:S(2)}, u32[]{:S(2)}) collective-permute-start(f32[2,128,16,128]{3,2,1,0:T(8,128)S(1)} %get-tuple-element.25), channel_id=1, source_target_pairs={{0,16},{16,0},{1,17},{17,1},{2,18},{18,2},{3,19},{19,3},{4,20},{20... | collective-permute-start | bytes 6291464 | tf_op jit(solution)/shard_map/ppermute | solution.py:262
  6.9 13.4 %collective-permute-start.4 = (f32[8,128,128]{2,1,0:T(8,128)S(1)}, f32[8,128,128]{2,1,0:T(8,128)S(1)}, u32[]{:S(2)}, u32[]{:S(2)}) collective-permute-start(f32[8,128,128]{2,1,0:T(8,128)S(1)} %get-tuple-element.30), channel_id=1, source_target_pairs={{1,0},{2,1},{3,2},{0,3},{5,4},{6,5},{7,6},{4,7},{9,8},{10,9},{11,1... | collective-permute-start | bytes 1572872 | tf_op jit(solution)/shard_map/ppermute | solution.py:286
  7.0 3.4 %collective-permute-start = (f32[8,16,128]{2,1,0:T(8,128)S(1)}, f32[8,16,128]{2,1,0:T(8,128)S(1)}, u32[]{:S(2)}, u32[]{:S(2)}) collective-permute-start(f32[8,16,128]{2,1,0:T(8,128)S(1)} %get-tuple-element.23), channel_id=1, source_target_pairs={{0,4},{4,8},{8,12},{12,0},{1,5},{5,9},{9,13},{13,1},{2,6},{6,10},{... | collective-permute-start | bytes 196616 | tf_op jit(solution)/shard_map/ppermute | solution.py:267
  7.2 4.4 %collective-permute-start.1 = (f32[8,16,128]{2,1,0:T(8,128)S(1)}, f32[8,16,128]{2,1,0:T(8,128)S(1)}, u32[]{:S(2)}, u32[]{:S(2)}) collective-permute-start(f32[8,16,128]{2,1,0:T(8,128)S(1)} %get-tuple-element.24), channel_id=1, source_target_pairs={{4,0},{8,4},{12,8},{0,12},{5,1},{9,5},{13,9},{1,13},{6,2},{10,6},{... | collective-permute-start | bytes 196616 | tf_op jit(solution)/shard_map/ppermute | solution.py:268
  8.5 24.8 %collective-permute-start.3 = (f32[8,128,128]{2,1,0:T(8,128)S(1)}, f32[8,128,128]{2,1,0:T(8,128)S(1)}, u32[]{:S(2)}, u32[]{:S(2)}) collective-permute-start(f32[8,128,128]{2,1,0:T(8,128)S(1)} %get-tuple-element.28), channel_id=1, source_target_pairs={{0,1},{1,2},{2,3},{3,0},{4,5},{5,6},{6,7},{7,4},{8,9},{9,10},{10,1... | collective-permute-start | bytes 1572872 | tf_op jit(solution)/shard_map/ppermute | solution.py:287
  33.9 6.3 %collective-permute-start.7 = (f32[2,128,16,128]{3,2,1,0:T(8,128)S(1)}, f32[2,128,16,128]{3,2,1,0:T(8,128)S(1)}, u32[]{:S(2)}, u32[]{:S(2)}) collective-permute-start(f32[2,128,16,128]{3,2,1,0:T(8,128)S(1)} %pad_maximum_fusion), channel_id=1, source_target_pairs={{0,16},{16,0},{1,17},{17,1},{2,18},{18,2},{3,19},{19,3},{4,20},{20... | collective-permute-start | bytes 6291464 | tf_op jit(solution)/shard_map/ppermute | solution.py:262
  34.8 13.4 %collective-permute-start.9 = (f32[8,128,128]{2,1,0:T(8,128)S(1)}, f32[8,128,128]{2,1,0:T(8,128)S(1)}, u32[]{:S(2)}, u32[]{:S(2)}) collective-permute-start(f32[8,128,128]{2,1,0:T(8,128)S(1)} %multiply_add_fusion.5.refs_1_), channel_id=1, source_target_pairs={{1,0},{2,1},{3,2},{0,3},{5,4},{6,5},{7,6},{4,7},{9,8},{10,9},{11,1... | collective-permute-start | bytes 1572872 | tf_op jit(solution)/shard_map/ppermute | solution.py:286
  35.5 4.1 %collective-permute-start.6 = (f32[8,16,128]{2,1,0:T(8,128)S(1)}, f32[8,16,128]{2,1,0:T(8,128)S(1)}, u32[]{:S(2)}, u32[]{:S(2)}) collective-permute-start(f32[8,16,128]{2,1,0:T(8,128)S(1)} %get-tuple-element.58), channel_id=1, source_target_pairs={{4,0},{8,4},{12,8},{0,12},{5,1},{9,5},{13,9},{1,13},{6,2},{10,6},{... | collective-permute-start | bytes 196616 | tf_op jit(solution)/shard_map/ppermute | solution.py:268
  35.8 4.4 %collective-permute-start.5 = (f32[8,16,128]{2,1,0:T(8,128)S(1)}, f32[8,16,128]{2,1,0:T(8,128)S(1)}, u32[]{:S(2)}, u32[]{:S(2)}) collective-permute-start(f32[8,16,128]{2,1,0:T(8,128)S(1)} %get-tuple-element.59), channel_id=1, source_target_pairs={{0,4},{4,8},{8,12},{12,0},{1,5},{5,9},{9,13},{13,1},{2,6},{6,10},{... | collective-permute-start | bytes 196616 | tf_op jit(solution)/shard_map/ppermute | solution.py:267
  37.9 23.8 %collective-permute-start.8 = (f32[8,128,128]{2,1,0:T(8,128)S(1)}, f32[8,128,128]{2,1,0:T(8,128)S(1)}, u32[]{:S(2)}, u32[]{:S(2)}) collective-permute-start(f32[8,128,128]{2,1,0:T(8,128)S(1)} %multiply_add_fusion.4.refs_2_), channel_id=1, source_target_pairs={{0,1},{1,2},{2,3},{3,0},{4,5},{5,6},{6,7},{7,4},{8,9},{9,10},{10,1... | collective-permute-start | bytes 1572872 | tf_op jit(solution)/shard_map/ppermute | solution.py:287
  62.4 5.7 %collective-permute-start.12 = (f32[2,128,16,128]{3,2,1,0:T(8,128)S(1)}, f32[2,128,16,128]{3,2,1,0:T(8,128)S(1)}, u32[]{:S(2)}, u32[]{:S(2)}) collective-permute-start(f32[2,128,16,128]{3,2,1,0:T(8,128)S(1)} %pad_maximum_fusion.1), channel_id=1, source_target_pairs={{0,16},{16,0},{1,17},{17,1},{2,18},{18,2},{3,19},{19,3},{4,20},{20... | collective-permute-start | bytes 6291464 | tf_op jit(solution)/shard_map/ppermute | solution.py:262
  63.0 13.4 %collective-permute-start.14 = (f32[8,128,128]{2,1,0:T(8,128)S(1)}, f32[8,128,128]{2,1,0:T(8,128)S(1)}, u32[]{:S(2)}, u32[]{:S(2)}) collective-permute-start(f32[8,128,128]{2,1,0:T(8,128)S(1)} %multiply_add_fusion.3.refs_1_), channel_id=1, source_target_pairs={{1,0},{2,1},{3,2},{0,3},{5,4},{6,5},{7,6},{4,7},{9,8},{10,9},{11,1... | collective-permute-start | bytes 1572872 | tf_op jit(solution)/shard_map/ppermute | solution.py:286
  63.4 4.1 %collective-permute-start.11 = (f32[8,16,128]{2,1,0:T(8,128)S(1)}, f32[8,16,128]{2,1,0:T(8,128)S(1)}, u32[]{:S(2)}, u32[]{:S(2)}) collective-permute-start(f32[8,16,128]{2,1,0:T(8,128)S(1)} %get-tuple-element.54), channel_id=1, source_target_pairs={{4,0},{8,4},{12,8},{0,12},{5,1},{9,5},{13,9},{1,13},{6,2},{10,6},{... | collective-permute-start | bytes 196616 | tf_op jit(solution)/shard_map/ppermute | solution.py:268
  63.9 4.2 %collective-permute-start.10 = (f32[8,16,128]{2,1,0:T(8,128)S(1)}, f32[8,16,128]{2,1,0:T(8,128)S(1)}, u32[]{:S(2)}, u32[]{:S(2)}) collective-permute-start(f32[8,16,128]{2,1,0:T(8,128)S(1)} %get-tuple-element.55), channel_id=1, source_target_pairs={{0,4},{4,8},{8,12},{12,0},{1,5},{5,9},{9,13},{13,1},{2,6},{6,10},{... | collective-permute-start | bytes 196616 | tf_op jit(solution)/shard_map/ppermute | solution.py:267
  65.8 24.0 %collective-permute-start.13 = (f32[8,128,128]{2,1,0:T(8,128)S(1)}, f32[8,128,128]{2,1,0:T(8,128)S(1)}, u32[]{:S(2)}, u32[]{:S(2)}) collective-permute-start(f32[8,128,128]{2,1,0:T(8,128)S(1)} %multiply_add_fusion.2.refs_2_), channel_id=1, source_target_pairs={{0,1},{1,2},{2,3},{3,0},{4,5},{5,6},{6,7},{7,4},{8,9},{9,10},{10,1... | collective-permute-start | bytes 1572872 | tf_op jit(solution)/shard_map/ppermute | solution.py:287
  90.5 6.6 %collective-permute-start.17 = (f32[2,128,16,128]{3,2,1,0:T(8,128)S(1)}, f32[2,128,16,128]{3,2,1,0:T(8,128)S(1)}, u32[]{:S(2)}, u32[]{:S(2)}) collective-permute-start(f32[2,128,16,128]{3,2,1,0:T(8,128)S(1)} %pad_maximum_fusion.2), channel_id=1, source_target_pairs={{0,16},{16,0},{1,17},{17,1},{2,18},{18,2},{3,19},{19,3},{4,20},{20... | collective-permute-start | bytes 6291464 | tf_op jit(solution)/shard_map/ppermute | solution.py:262
  91.0 13.4 %collective-permute-start.18 = (f32[8,128,128]{2,1,0:T(8,128)S(1)}, f32[8,128,128]{2,1,0:T(8,128)S(1)}, u32[]{:S(2)}, u32[]{:S(2)}) collective-permute-start(f32[8,128,128]{2,1,0:T(8,128)S(1)} %multiply_add_fusion.refs_2_), channel_id=1, source_target_pairs={{0,1},{1,2},{2,3},{3,0},{4,5},{5,6},{6,7},{7,4},{8,9},{9,10},{10,1... | collective-permute-start | bytes 1572872 | tf_op jit(solution)/shard_map/ppermute | solution.py:287
  92.3 4.1 %collective-permute-start.16 = (f32[8,16,128]{2,1,0:T(8,128)S(1)}, f32[8,16,128]{2,1,0:T(8,128)S(1)}, u32[]{:S(2)}, u32[]{:S(2)}) collective-permute-start(f32[8,16,128]{2,1,0:T(8,128)S(1)} %get-tuple-element.50), channel_id=1, source_target_pairs={{4,0},{8,4},{12,8},{0,12},{5,1},{9,5},{13,9},{1,13},{6,2},{10,6},{... | collective-permute-start | bytes 196616 | tf_op jit(solution)/shard_map/ppermute | solution.py:268
  92.8 4.2 %collective-permute-start.15 = (f32[8,16,128]{2,1,0:T(8,128)S(1)}, f32[8,16,128]{2,1,0:T(8,128)S(1)}, u32[]{:S(2)}, u32[]{:S(2)}) collective-permute-start(f32[8,16,128]{2,1,0:T(8,128)S(1)} %get-tuple-element.51), channel_id=1, source_target_pairs={{0,4},{4,8},{8,12},{12,0},{1,5},{5,9},{9,13},{13,1},{2,6},{6,10},{... | collective-permute-start | bytes 196616 | tf_op jit(solution)/shard_map/ppermute | solution.py:267
  104.7 0.7 collective-permute-start.23
  105.4 14.6 %collective-permute-start.24 = (f32[4,128,128]{2,1,0:T(8,128)S(1)}, f32[4,128,128]{2,1,0:T(8,128)S(1)}, u32[]{:S(2)}, u32[]{:S(2)}) collective-permute-start(f32[4,128,128]{2,1,0:T(8,128)S(1)} %get-tuple-element.61), channel_id=1, source_target_pairs={{1,2},{5,6},{9,10},{13,14},{17,18},{21,22},{25,26},{29,30}} | collective-permute-start | bytes 786440 | tf_op jit(solution)/shard_map/ppermute | solution.py:307
  106.7 13.3 %collective-permute-start.20 = (f32[4,128,128]{2,1,0:T(8,128)S(1)}, f32[4,128,128]{2,1,0:T(8,128)S(1)}, u32[]{:S(2)}, u32[]{:S(2)}) collective-permute-start(f32[4,128,128]{2,1,0:T(8,128)S(1)} %get-tuple-element.62), channel_id=1, source_target_pairs={{0,1},{4,5},{8,9},{12,13},{16,17},{20,21},{24,25},{28,29}} | collective-permute-start | bytes 786440 | tf_op jit(solution)/shard_map/ppermute | solution.py:307
  120.2 21.4 %collective-permute-start.21 = (f32[4,128,128]{2,1,0:T(8,128)S(1)}, f32[4,128,128]{2,1,0:T(8,128)S(1)}, u32[]{:S(2)}, u32[]{:S(2)}) collective-permute-start(f32[4,128,128]{2,1,0:T(8,128)S(1)} %get-tuple-element.60), channel_id=1, source_target_pairs={{1,2},{5,6},{9,10},{13,14},{17,18},{21,22},{25,26},{29,30}} | collective-permute-start | bytes 786440 | tf_op jit(solution)/shard_map/ppermute | solution.py:307
  121.5 21.5 %collective-permute-start.19 = (f32[8,128,128]{2,1,0:T(8,128)S(1)}, f32[8,128,128]{2,1,0:T(8,128)S(1)}, u32[]{:S(2)}, u32[]{:S(2)}) collective-permute-start(f32[8,128,128]{2,1,0:T(8,128)S(1)} %multiply_add_fusion.1.refs_1_), channel_id=1, source_target_pairs={{1,0},{2,1},{3,2},{0,3},{5,4},{6,5},{7,6},{4,7},{9,8},{10,9},{11,1... | collective-permute-start | bytes 1572872 | tf_op jit(solution)/shard_map/ppermute | solution.py:286
  124.7 25.0 %collective-permute-start.25 = (f32[4,128,128]{2,1,0:T(8,128)S(1)}, f32[4,128,128]{2,1,0:T(8,128)S(1)}, u32[]{:S(2)}, u32[]{:S(2)}) collective-permute-start(f32[4,128,128]{2,1,0:T(8,128)S(1)} %get-tuple-element.42), channel_id=1, source_target_pairs={{2,3},{6,7},{10,11},{14,15},{18,19},{22,23},{26,27},{30,31}} | collective-permute-start | bytes 786440 | tf_op jit(solution)/shard_map/ppermute | solution.py:307
  141.7 10.8 %collective-permute-start.22 = (f32[4,128,128]{2,1,0:T(8,128)S(1)}, f32[4,128,128]{2,1,0:T(8,128)S(1)}, u32[]{:S(2)}, u32[]{:S(2)}) collective-permute-start(f32[4,128,128]{2,1,0:T(8,128)S(1)} %get-tuple-element.44), channel_id=1, source_target_pairs={{2,3},{6,7},{10,11},{14,15},{18,19},{22,23},{26,27},{30,31}} | collective-permute-start | bytes 786440 | tf_op jit(solution)/shard_map/ppermute | solution.py:307

commit v2 on v1

--- a/solution.py
+++ b/solution.py
@@ -9,11 +9,12 @@
 
 STEPS = 4
 TILE = 8
-PARTS = 2
+PARTS = 4
 MIB = 1024 * 1024
 
 
 CHUNKS = 8
+SLOTS = 4
 VMEM = pl.BlockSpec(memory_space=pltpu.VMEM)
 HBM = pl.BlockSpec(memory_space=pltpu.HBM)
 
@@ -57,7 +58,7 @@
 
     for k in range(CHUNKS):
         copies[k].wait()
-        lax.fori_loop(k * chunk, (k + 1) * chunk, one, 0)
+        lax.fori_loop(k * chunk, (k + 1) * chunk, one, 0, unroll=4)
     for row in range(rows):
         first_ref[row] = h_ref[row, 0]
         final_ref[row] = h_ref[row, span - 1]
@@ -73,7 +74,7 @@
         out_specs=[VMEM] * 7,
         out_shape=[like(field.shape, field), face, face, like((2, span, depth, lanes), field), edge, edge, like((1, 1, lanes), field)],
         scratch_shapes=[pltpu.SemaphoreType.DMA((CHUNKS,))],
-        compiler_params=pltpu.CompilerParams(vmem_limit_bytes=2 * MIB),
+        compiler_params=pltpu.CompilerParams(vmem_limit_bytes=42 * MIB),
         cost_estimate=pl.CostEstimate(flops=4 * field.size, bytes_accessed=field.size, transcendentals=0),
         name="peel",
     )(field)
@@ -156,66 +157,107 @@
     )(*operands)
 
 
-def end_kernel(h_ref, low_ref, high_ref, end_ref, sum_ref, stage, sems):
+def sums_kernel(h_ref, sum_ref):
+    rows, span, depth, lanes = h_ref.shape
+    sub = lax.broadcasted_iota(jnp.int32, (TILE, lanes), 0)
+
+    def one(at, _):
+        for row in range(rows):
+            carry = None
+            for t in range(depth // TILE):
+                cells = h_ref[row, at, pl.ds(t * TILE, TILE), :]
+                shift = 1
+                while shift < TILE:
+                    cells = cells + jnp.where(sub >= shift, pltpu.roll(cells, shift, 0), 0.0)
+                    shift *= 2
+                cells = cells if carry is None else cells + carry
+                sum_ref[row, at, pl.ds(t * TILE, TILE), :] = cells
+                carry = cells[TILE - 1 :]
+        return 0
+
+    lax.fori_loop(0, span, one, 0, unroll=2)
+
+
+def running_sums(h):
+    return pl.pallas_call(
+        sums_kernel,
+        in_specs=[VMEM],
+        out_specs=VMEM,
+        out_shape=like(h.shape, h),
+        compiler_params=pltpu.CompilerParams(vmem_limit_bytes=2 * MIB),
+        cost_estimate=pl.CostEstimate(flops=8 * h.size, bytes_accessed=8 * h.size, transcendentals=0),
+        name="sums",
+    )(h)
+
+
+def ending_kernel(h_ref, low_ref, high_ref, end_ref, stage, sems):
     rows, span, depth, lanes = h_ref.shape
     tiles = depth // TILE
     chunk = span // CHUNKS
     sub = lax.broadcasted_iota(jnp.int32, (TILE, lanes), 0)
 
     def copy(k):
-        return pltpu.make_async_copy(stage.at[k % 2], end_ref.at[:, pl.ds(k * chunk, chunk)], sems.at[k])
+        return pltpu.make_async_copy(stage.at[k % SLOTS], end_ref.at[:, pl.ds(k * chunk, chunk)], sems.at[k])
 
     for k in range(CHUNKS):
-        if k >= 2:
-            copy(k - 2).wait()
+        if k >= SLOTS:
+            copy(k - SLOTS).wait()
 
         def one(step, _):
             at = step + k * chunk
-            held = [[h_ref[row, at, pl.ds(t * TILE, TILE), :] for t in range(tiles)] for row in range(rows)]
-            for row in range(rows):
-                carry = None
-                for t in range(tiles):
-                    part = pl.ds(t * TILE, TILE)
-                    cells = held[row][t]
-                    end = cells
-                    if t == 0:
-                        end = end + jnp.where(sub == 0, low_ref[row, pl.ds(at, 1), :], 0.0)
-                    if t == tiles - 1:
-                        end = end + jnp.where(sub == TILE - 1, high_ref[row, pl.ds(at, 1), :], 0.0)
-                    stage[k % 2, row, step, part, :] = end
-                    shift = 1
-                    while shift < TILE:
-                        cells = cells + jnp.where(sub >= shift, pltpu.roll(cells, shift, 0), 0.0)
-                        shift *= 2
-                    held[row][t] = cells if carry is None else cells + carry
-                    carry = held[row][t][TILE - 1 :]
             for row in range(rows):
                 for t in range(tiles):
-                    sum_ref[row, at, pl.ds(t * TILE, TILE), :] = held[row][t]
+                    cells = h_ref[row, at, pl.ds(t * TILE, TILE), :]
+                    if t == 0:
+                        cells = cells + jnp.where(sub == 0, low_ref[row, pl.ds(at, 1), :], 0.0)
+                    if t == tiles - 1:
+                        cells = cells + jnp.where(sub == TILE - 1, high_ref[row, pl.ds(at, 1), :], 0.0)
+                    stage[k % SLOTS, row, step, pl.ds(t * TILE, TILE), :] = cells
             return 0
 
-        lax.fori_loop(0, chunk, one, 0)
+        lax.fori_loop(0, chunk, one, 0, unroll=2)
         copy(k).start()
-    for k in (CHUNKS - 2, CHUNKS - 1):
+    for k in range(CHUNKS - SLOTS, CHUNKS):
         copy(k).wait()
 
 
-def end(h, low, high):
+def ending(h, low, high):
     rows, span, depth, lanes = h.shape
     return pl.pallas_call(
-        end_kernel,
+        ending_kernel,
         in_specs=[VMEM] * 3,
-        out_specs=[HBM, VMEM],
-        out_shape=[like(h.shape, h)] * 2,
-        scratch_shapes=[pltpu.VMEM((2, rows, span // CHUNKS, depth, lanes), h.dtype), pltpu.SemaphoreType.DMA((CHUNKS,))],
-        input_output_aliases={0: 1},
-        compiler_params=pltpu.CompilerParams(vmem_limit_bytes=4 * MIB),
-        cost_estimate=pl.CostEstimate(flops=12 * h.size, bytes_accessed=12 * h.size, transcendentals=0),
-        name="end",
+        out_specs=HBM,
+        out_shape=like(h.shape, h),
+        scratch_shapes=[pltpu.VMEM((SLOTS, rows, span // CHUNKS, depth, lanes), h.dtype), pltpu.SemaphoreType.DMA((CHUNKS,))],
+        compiler_params=pltpu.CompilerParams(vmem_limit_bytes=8 * MIB),
+        cost_estimate=pl.CostEstimate(flops=2 * h.size, bytes_accessed=8 * h.size, transcendentals=0),
+        name="ending",
     )(h, low, high)
 
 
-def potential_kernel(scale, offset, sum_ref, prior_ref, got_ref, rest_ref, high_ref, *refs):
+def relay_kernel(offset, got_ref, *refs):
+    prior_ref, (own_ref, before_ref, next_ref) = refs[0], refs[-3:]
+    rows = got_ref.shape[0]
+    before = got_ref[...] if len(refs) == 3 else prior_ref[...] + got_ref[...]
+    before_ref[...] = before
+    next_ref[...] = before + own_ref[pl.ds(offset, rows)]
+
+
+def relay(prior, got, own, part):
+    operands = [got] + ([] if prior is None else [prior]) + [own]
+    return pl.pallas_call(
+        functools.partial(relay_kernel, part * got.shape[0]),
+        in_specs=[VMEM] * len(operands),
+        out_specs=[VMEM] * 2,
+        out_shape=[like(got.shape, got)] * 2,
+        compiler_params=pltpu.CompilerParams(vmem_limit_bytes=2 * MIB),
+        cost_estimate=pl.CostEstimate(flops=2 * got.size, bytes_accessed=16 * got.size, transcendentals=0),
+        name="relay",
+    )(*operands)
+
+
+def potential_kernel(scale, offset, given, sum_ref, got_ref, rest_ref, high_ref, *refs):
+    prior_ref = refs[0] if given else None
     pot_ref, stage, sems = refs[-3:]
     rows, span, depth, lanes = stage.shape
     chunk = span // CHUNKS
@@ -223,7 +265,8 @@
 
     def one(at, _):
         for row in range(rows):
-            base = prior_ref[row, pl.ds(at, 1), :] + got_ref[row, pl.ds(at, 1), :]
+            base = got_ref[row, pl.ds(at, 1), :]
+            base = base if prior_ref is None else base + prior_ref[row, pl.ds(at, 1), :]
             base = base + rest_ref[row + offset, pl.ds(at, 1), :]
             high = high_ref[row + offset, pl.ds(at, 1), :]
             cells = sum_ref[row + offset, at] + base
@@ -232,7 +275,7 @@
 
     copies = []
     for k in range(CHUNKS):
-        lax.fori_loop(k * chunk, (k + 1) * chunk, one, 0)
+        lax.fori_loop(k * chunk, (k + 1) * chunk, one, 0, unroll=4)
         part = pl.ds(k * chunk, chunk)
         copies.append(pltpu.make_async_copy(stage.at[:, part], pot_ref.at[pl.ds(offset, rows), part], sems.at[k]))
         copies[-1].start()
@@ -243,17 +286,18 @@
 def potential(sums, prior, got, rest, high, scale, part, made):
     _, span, depth, lanes = sums.shape
     some = got.shape[0]
-    return pl.pallas_call(
-        functools.partial(potential_kernel, scale, part * some),
-        in_specs=[VMEM] * 5 + ([] if made is None else [HBM]),
+    operands = [sums, got, rest, high] + ([] if prior is None else [prior])
+    return pl.pallas_call(
+        functools.partial(potential_kernel, scale, part * some, prior is not None),
+        in_specs=[VMEM] * len(operands) + [HBM] * (made is not None),
         out_specs=HBM,
         out_shape=like(sums.shape, sums),
         scratch_shapes=[pltpu.VMEM((some, span, depth, lanes), sums.dtype), pltpu.SemaphoreType.DMA((CHUNKS,))],
-        input_output_aliases={} if made is None else {5: 0},
+        input_output_aliases={} if made is None else {len(operands): 0},
         compiler_params=pltpu.CompilerParams(vmem_limit_bytes=(2 + 8 // PARTS) * MIB),
         cost_estimate=pl.CostEstimate(flops=2 * sums.size, bytes_accessed=8 * sums.size // PARTS, transcendentals=0),
         name="potential",
-    )(sums, prior, got, rest, high, *(() if made is None else (made,)))
+    )(*operands, *(() if made is None else (made,)))
 
 
 def side_halos(both, first, final):
@@ -296,16 +340,19 @@
     rest = 0.1 * jnp.where(ground > 0.0, below, low)
     own = outs[1] + 0.1 * high + rest
     top = 0.1 * above
-    field_end, sums = end(h, 0.1 * below, top)
+    sums = running_sums(h)
+    field_end = ending(h, 0.1 * below, top)
     rows = own.shape[0] // PARTS
+    nexts = [own[part * rows : (part + 1) * rows] for part in range(PARTS)]
+    befores, gots = [None] * PARTS, [jnp.zeros_like(one) for one in nexts]
+    for hop in range(levs - 1):
+        for part in range(PARTS):
+            if hop:
+                befores[part], nexts[part] = relay(befores[part], gots[part], own, part)
+            gots[part] = lax.ppermute(nexts[part], "lev", [(hop, hop + 1)])
     made = None
     for part in range(PARTS):
-        mine = own[part * rows : (part + 1) * rows]
-        before, got = jnp.zeros_like(mine), jnp.zeros_like(mine)
-        for hop in range(levs - 1):
-            before = before + got
-            got = lax.ppermute(before + mine, "lev", [(hop, hop + 1)])
-        made = potential(sums, before, got, rest, top, 1.0 / (depth * levs), part, made)
+        made = potential(sums, befores[part], gots[part], rest, top, 1.0 / (depth * levs), part, made)
     return made, field_end
 
 

time: 156 us -> 145 us (0.929)
  the two profiles are of different devices: /device:TPU:23 before, /device:TPU:16 now
where the time goes in v2:
time: 145 us
  waiting for transfers between devices  69 us (48%)
  Pallas kernels  40.6 us (28%)
  starting transfers between devices  31.5 us (22%)
  other arithmetic  2.53 us (2%)
    ppermute x4, waiting for transfers between devices, steps(): below = lax.ppermute(high, 'lev', ups(levs))  37.4 us
    pallas_call x4, Pallas kernels, march(): pl.pallas_call(functools.partial(march_kernel, faces is not None, last, y...  24.2 us
    ppermute x12, waiting for transfers between devices, steps(): gots[part] = lax.ppermute(nexts[part], 'lev', [(hop, hop + 1)])  13.9 us
    ppermute x12, starting transfers between devices, steps(): gots[part] = lax.ppermute(nexts[part], 'lev', [(hop, hop + 1)])  13 us
    ppermute x4, waiting for transfers between devices, side_halos(): xlow = lax.ppermute(final, 'lon', ups(lons))  9.24 us
    ppermute x4, starting transfers between devices, side_halos(): xhigh = lax.ppermute(first, 'lon', downs(lons))  8.6 us
    pallas_call x4, Pallas kernels, potential(): pl.pallas_call(functools.partial(potential_kernel, scale, part * some, pr...  5.8 us
    ppermute x4, starting transfers between devices, steps(): below = lax.ppermute(high, 'lev', ups(levs))  5.65 us
  transfers between devices with their start and end apart: 32, of which 18 were waited for; matrix products, arithmetic and copies ran while one was open for 1% of the time, Pallas kernels for 24%

profile of v2, /device:TPU:16, one launch (start us, length us, event | category | flops | bytes accessed | tf_op | source)
XLA Modules:
  0.0 144.9 jit_solution(2559958956922267249)
XLA Ops:
  0.6 3.7 %peel.1 = (f32[8,128,16,128]{3,2,1,0:T(8,128)S(1)}, f32[8,128,128]{2,1,0:T(8,128)S(1)}, f32[8,128,128]{2,1,0:T(8,128)S(1)}, f32[2,128,16,128]{3,2,1,0:T(8,128)S(...) custom-call(f32[8,128,16,128]{3,2,1,0:T(8,128)} %f_ref.1), custom_call_target="tpu_custom_call" | custom-call | flops 8388608 | bytes 2097152 | tf_op jit(solution)/shard_map/peel/pallas_call | solution.py:71
  4.5 0.5 collective-permute-start.4
  5.0 1.5 %collective-permute-start = (f32[8,16,128]{2,1,0:T(8,128)S(1)}, f32[8,16,128]{2,1,0:T(8,128)S(1)}, u32[]{:S(2)}, u32[]{:S(2)}) collective-permute-start(f32[8,16,128]{2,1,0:T(8,128)S(1)} %get-tuple-element.37), channel_id=1, source_target_pairs={{0,4},{4,8},{8,12},{12,0},{1,5},{5,9},{9,13},{13,1},{2,6},{6,10},{... | collective-permute-start | bytes 196616 | tf_op jit(solution)/shard_map/ppermute | solution.py:311
  6.5 1.4 collective-permute-start.1
  7.9 1.6 %collective-permute-start.3 = (f32[8,128,128]{2,1,0:T(8,128)S(1)}, f32[8,128,128]{2,1,0:T(8,128)S(1)}, u32[]{:S(2)}, u32[]{:S(2)}) collective-permute-start(f32[8,128,128]{2,1,0:T(8,128)S(1)} %get-tuple-element.42), channel_id=1, source_target_pairs={{0,1},{1,2},{2,3},{3,0},{4,5},{5,6},{6,7},{7,4},{8,9},{9,10},{10,1... | collective-permute-start | bytes 1572872 | tf_op jit(solution)/shard_map/ppermute | solution.py:331
  9.5 0.9 collective-permute-done.refs_1_
  10.4 1.1 collective-permute-done.1.refs_2_
  11.5 5.2 %march.4 = (f32[8,128,16,128]{3,2,1,0:T(8,128)S(1)}, f32[8,128,128]{2,1,0:T(8,128)S(1)}, f32[8,128,128]{2,1,0:T(8,128)S(1)}) custom-call(f32[8,128,16,128]{3,2,1,0:T(8,128)S(1)} %get-tuple-element.36.refs_0_, f32[8,16,128]{2,1,0:T(8,128)S(1)} %collective-permute-done.refs_1_, ...), custom_call_target="tpu_custom_call", output_to_operand_aliasing={{0}: (0, {})} | custom-call | flops 33554432 | bytes 25165824 | tf_op jit(solution)/shard_map/march/pallas_call | solution.py:148
  16.7 2.6 %collective-permute-done.4 = f32[8,128,128]{2,1,0:T(8,128)S(1)} collective-permute-done((f32[8,128,128]{2,1,0:T(8,128)S(1)}, f32[8,128,128]{2,1,0:T(8,128)S(1)}, u32[]{:S(2)}, u32[]{:S(2)}) %collective-permute-start.4) | collective-permute-done | bytes 524320 | tf_op jit(solution)/shard_map/ppermute | solution.py:330
  19.4 12.5 %collective-permute-done.3 = f32[8,128,128]{2,1,0:T(8,128)S(1)} collective-permute-done((f32[8,128,128]{2,1,0:T(8,128)S(1)}, f32[8,128,128]{2,1,0:T(8,128)S(1)}, u32[]{:S(2)}, u32[]{:S(2)}) %collective-permute-start.3) | collective-permute-done | bytes 524320 | tf_op jit(solution)/shard_map/ppermute | solution.py:331
  32.0 0.4 select_select_fusion.5
  32.4 0.1 pad_maximum_fusion
  32.6 0.7 collective-permute-start.9
  33.3 0.1 fusion.9
  33.4 2.5 %collective-permute-start.6 = (f32[8,16,128]{2,1,0:T(8,128)S(1)}, f32[8,16,128]{2,1,0:T(8,128)S(1)}, u32[]{:S(2)}, u32[]{:S(2)}) collective-permute-start(f32[8,16,128]{2,1,0:T(8,128)S(1)} %get-tuple-element.82), channel_id=1, source_target_pairs={{4,0},{8,4},{12,8},{0,12},{5,1},{9,5},{13,9},{1,13},{6,2},{10,6},{... | collective-permute-start | bytes 196616 | tf_op jit(solution)/shard_map/ppermute | solution.py:312
  35.9 1.1 collective-permute-start.8
  37.1 1.2 collective-permute-done.6.refs_4_
  38.3 2.8 %collective-permute-done.5.refs_3_ = f32[8,16,128]{2,1,0:T(8,128)S(1)} collective-permute-done((f32[8,16,128]{2,1,0:T(8,128)S(1)}, f32[8,16,128]{2,1,0:T(8,128)S(1)}, u32[]{:S(2)}, u32[]{:S(2)}) %collective-permute-start.5) | collective-permute-done | bytes 65568 | tf_op jit(solution)/shard_map/ppermute | solution.py:311
  41.1 6.1 %march.5 = (f32[8,128,16,128]{3,2,1,0:T(8,128)S(1)}, f32[8,128,128]{2,1,0:T(8,128)S(1)}, f32[8,128,128]{2,1,0:T(8,128)S(1)}) custom-call(f32[8,128,16,128]{3,2,1,0:T(8,128)S(1)} %get-tuple-element.40.refs_0_, f32[8,128,128]{2,1,0:T(8,128)S(1)} %multiply_add_fusion.5.refs_1_, ...), custom_call_target="tpu_custom_call", output_to_operand_aliasing={{0}: (0, {})} | custom-call | flops 33554432 | bytes 25165824 | tf_op jit(solution)/shard_map/march/pallas_call | solution.py:148
  47.2 0.3 collective-permute-done.9
  47.6 12.4 %collective-permute-done.8 = f32[8,128,128]{2,1,0:T(8,128)S(1)} collective-permute-done((f32[8,128,128]{2,1,0:T(8,128)S(1)}, f32[8,128,128]{2,1,0:T(8,128)S(1)}, u32[]{:S(2)}, u32[]{:S(2)}) %collective-permute-start.8) | collective-permute-done | bytes 524320 | tf_op jit(solution)/shard_map/ppermute | solution.py:331
  60.1 0.4 select_select_fusion.3
  60.5 0.1 pad_maximum_fusion.1
  60.7 0.7 collective-permute-start.14
  61.5 2.3 %collective-permute-start.11 = (f32[8,16,128]{2,1,0:T(8,128)S(1)}, f32[8,16,128]{2,1,0:T(8,128)S(1)}, u32[]{:S(2)}, u32[]{:S(2)}) collective-permute-start(f32[8,16,128]{2,1,0:T(8,128)S(1)} %get-tuple-element.78), channel_id=1, source_target_pairs={{4,0},{8,4},{12,8},{0,12},{5,1},{9,5},{13,9},{1,13},{6,2},{10,6},{... | collective-permute-start | bytes 196616 | tf_op jit(solution)/shard_map/ppermute | solution.py:312
  63.8 1.4 collective-permute-start.13
  65.2 1.0 collective-permute-done.11.refs_4_
  66.2 2.8 %collective-permute-done.10.refs_3_ = f32[8,16,128]{2,1,0:T(8,128)S(1)} collective-permute-done((f32[8,16,128]{2,1,0:T(8,128)S(1)}, f32[8,16,128]{2,1,0:T(8,128)S(1)}, u32[]{:S(2)}, u32[]{:S(2)}) %collective-permute-start.10) | collective-permute-done | bytes 65568 | tf_op jit(solution)/shard_map/ppermute | solution.py:311
  69.0 6.1 %march.6 = (f32[8,128,16,128]{3,2,1,0:T(8,128)S(1)}, f32[8,128,128]{2,1,0:T(8,128)S(1)}, f32[8,128,128]{2,1,0:T(8,128)S(1)}) custom-call(f32[8,128,16,128]{3,2,1,0:T(8,128)S(1)} %get-tuple-element.45.refs_0_, f32[8,128,128]{2,1,0:T(8,128)S(1)} %multiply_add_fusion.3.refs_1_, ...), custom_call_target="tpu_custom_call", output_to_operand_aliasing={{0}: (0, {})} | custom-call | flops 33554432 | bytes 25165824 | tf_op jit(solution)/shard_map/march/pallas_call | solution.py:148
  75.1 0.5 collective-permute-done.14
  75.7 12.4 %collective-permute-done.13 = f32[8,128,128]{2,1,0:T(8,128)S(1)} collective-permute-done((f32[8,128,128]{2,1,0:T(8,128)S(1)}, f32[8,128,128]{2,1,0:T(8,128)S(1)}, u32[]{:S(2)}, u32[]{:S(2)}) %collective-permute-start.13) | collective-permute-done | bytes 524320 | tf_op jit(solution)/shard_map/ppermute | solution.py:331
  88.1 0.1 multiply_add_fusion.1.refs_1_
  88.2 0.4 select_select_fusion.1
  88.6 0.1 pad_maximum_fusion.2
  88.8 1.5 %collective-permute-start.18 = (f32[8,128,128]{2,1,0:T(8,128)S(1)}, f32[8,128,128]{2,1,0:T(8,128)S(1)}, u32[]{:S(2)}, u32[]{:S(2)}) collective-permute-start(f32[8,128,128]{2,1,0:T(8,128)S(1)} %multiply_add_fusion.refs_2_), channel_id=1, source_target_pairs={{0,1},{1,2},{2,3},{3,0},{4,5},{5,6},{6,7},{7,4},{8,9},{9,10},{10,1... | collective-permute-start | bytes 1572872 | tf_op jit(solution)/shard_map/ppermute | solution.py:331
  90.3 0.1 fusion.1
  90.4 2.3 %collective-permute-start.16 = (f32[8,16,128]{2,1,0:T(8,128)S(1)}, f32[8,16,128]{2,1,0:T(8,128)S(1)}, u32[]{:S(2)}, u32[]{:S(2)}) collective-permute-start(f32[8,16,128]{2,1,0:T(8,128)S(1)} %get-tuple-element.74), channel_id=1, source_target_pairs={{4,0},{8,4},{12,8},{0,12},{5,1},{9,5},{13,9},{1,13},{6,2},{10,6},{... | collective-permute-start | bytes 196616 | tf_op jit(solution)/shard_map/ppermute | solution.py:312
  92.8 0.6 collective-permute-start.22
  93.4 1.8 %collective-permute-done.16.refs_4_ = f32[8,16,128]{2,1,0:T(8,128)S(1)} collective-permute-done((f32[8,16,128]{2,1,0:T(8,128)S(1)}, f32[8,16,128]{2,1,0:T(8,128)S(1)}, u32[]{:S(2)}, u32[]{:S(2)}) %collective-permute-start.16) | collective-permute-done | bytes 65568 | tf_op jit(solution)/shard_map/ppermute | solution.py:312
  95.1 2.8 %collective-permute-done.15.refs_3_ = f32[8,16,128]{2,1,0:T(8,128)S(1)} collective-permute-done((f32[8,16,128]{2,1,0:T(8,128)S(1)}, f32[8,16,128]{2,1,0:T(8,128)S(1)}, u32[]{:S(2)}, u32[]{:S(2)}) %collective-permute-start.15) | collective-permute-done | bytes 65568 | tf_op jit(solution)/shard_map/ppermute | solution.py:311
  97.9 6.9 %march.7 = (f32[8,128,16,128]{3,2,1,0:T(8,128)S(1)}, f32[8,128,128]{2,1,0:T(8,128)S(1)}) custom-call(f32[8,128,16,128]{3,2,1,0:T(8,128)S(1)} %get-tuple-element.48.refs_0_, f32[8,128,128]{2,1,0:T(8,128)S(1)} %multiply_add_fusion.1.refs_1_, f32[8,128,128]{2,1,0:T(8,128)S(1)} %multiply_add_fusion.refs_2_, ...), custom_call_target="tpu_custom_call", output_to_operand_aliasing={{0}: (0, {})} | custom-call | flops 33554432 | bytes 25165824 | tf_op jit(solution)/shard_map/march/pallas_call | solution.py:148
  104.8 0.2 add_add_fusion
  105.1 0.7 collective-permute-start.29
  105.7 0.7 collective-permute-start.26
  106.4 0.7 collective-permute-start.23
  107.1 0.7 collective-permute-start.19
  107.8 1.3 collective-permute-start.30
  109.1 1.3 collective-permute-start.27
  110.5 1.3 collective-permute-start.24
  111.8 1.3 collective-permute-start.20
  113.1 9.6 %collective-permute-done.30.got_ref = f32[2,128,128]{2,1,0:T(8,128)S(1)} collective-permute-done((f32[2,128,128]{2,1,0:T(8,128)S(1)}, f32[2,128,128]{2,1,0:T(8,128)S(1)}, u32[]{:S(2)}, u32[]{:S(2)}) %collective-permute-start.30) | collective-permute-done | bytes 131104 | tf_op jit(solution)/shard_map/ppermute | solution.py:352
  122.8 1.3 collective-permute-start.31
  124.1 1.5 %collective-permute-done.27.got_ref = f32[2,128,128]{2,1,0:T(8,128)S(1)} collective-permute-done((f32[2,128,128]{2,1,0:T(8,128)S(1)}, f32[2,128,128]{2,1,0:T(8,128)S(1)}, u32[]{:S(2)}, u32[]{:S(2)}) %collective-permute-start.27) | collective-permute-done | bytes 131104 | tf_op jit(solution)/shard_map/ppermute | solution.py:352
  125.6 1.3 collective-permute-start.28
  126.9 1.5 %collective-permute-done.24.got_ref = f32[2,128,128]{2,1,0:T(8,128)S(1)} collective-permute-done((f32[2,128,128]{2,1,0:T(8,128)S(1)}, f32[2,128,128]{2,1,0:T(8,128)S(1)}, u32[]{:S(2)}, u32[]{:S(2)}) %collective-permute-start.24) | collective-permute-done | bytes 131104 | tf_op jit(solution)/shard_map/ppermute | solution.py:352
  128.4 1.3 collective-permute-start.25
  129.7 1.3 collective-permute-done.20.got_ref
  131.0 1.3 collective-permute-start.21
  132.3 3.5 %ending.1 = f32[8,128,16,128]{3,2,1,0:T(8,128)} custom-call(f32[8,128,16,128]{3,2,1,0:T(8,128)S(1)} %get-tuple-element.51.h_ref, f32[8,128,128]{2,1,0:T(8,128)S(1)} %get-tuple-element.84.low_ref, f32[8,128,128]{2,1,0:T(8,128)S(1)} %broadcast_multiply_fusion.1.high_ref), custom_call_target="tpu_custom_call" | custom-call | flops 4194304 | bytes 16777216 | tf_op jit(solution)/shard_map/ending/pallas_call | solution.py:226
  135.9 3.1 %sums.1.sum_ref = f32[8,128,16,128]{3,2,1,0:T(8,128)S(1)} custom-call(f32[8,128,16,128]{3,2,1,0:T(8,128)S(1)} %get-tuple-element.51.h_ref), custom_call_target="tpu_custom_call" | custom-call | flops 16777216 | bytes 16777216 | tf_op jit(solution)/shard_map/sums/pallas_call | solution.py:182
  139.0 1.4 potential.4.refs_1_
  140.5 1.5 %potential.5.refs_1_ = f32[8,128,16,128]{3,2,1,0:T(8,128)} custom-call(f32[8,128,16,128]{3,2,1,0:T(8,128)S(1)} %sums.1.sum_ref, f32[2,128,128]{2,1,0:T(8,128)S(1)} %collective-permute-done.28.got_ref, f32[8,128,128]{2,1,0:T(8,128)S(1)} %get-tuple-element.71.rest_ref, ...), custom_call_target="tpu_custom_call", output_to_operand_aliasing={{}: (5, {})} | custom-call | flops 4194304 | bytes 4194304 | tf_op jit(solution)/shard_map/potential/pallas_call | solution.py:290
  142.0 1.5 %potential.6.refs_1_ = f32[8,128,16,128]{3,2,1,0:T(8,128)} custom-call(f32[8,128,16,128]{3,2,1,0:T(8,128)S(1)} %sums.1.sum_ref, f32[2,128,128]{2,1,0:T(8,128)S(1)} %collective-permute-done.25.got_ref, f32[8,128,128]{2,1,0:T(8,128)S(1)} %get-tuple-element.71.rest_ref, ...), custom_call_target="tpu_custom_call", output_to_operand_aliasing={{}: (5, {})} | custom-call | flops 4194304 | bytes 4194304 | tf_op jit(solution)/shard_map/potential/pallas_call | solution.py:290
  143.5 1.5 %potential.7 = f32[8,128,16,128]{3,2,1,0:T(8,128)} custom-call(f32[8,128,16,128]{3,2,1,0:T(8,128)S(1)} %sums.1.sum_ref, f32[2,128,128]{2,1,0:T(8,128)S(1)} %collective-permute-done.21.got_ref, f32[8,128,128]{2,1,0:T(8,128)S(1)} %get-tuple-element.71.rest_ref, f32[8,128,128]{2,1,0:T(8,128)S(1)} %broadcast_multiply_fusion.1.high_ref, ...), custom_call_target="tpu_custom_call", output_to_operand_aliasing={{}: (5, {})} | custom-call | flops 4194304 | bytes 4194304 | tf_op jit(solution)/shard_map/potential/pallas_call | solution.py:290
  (53 shorter events, 1.2 us)
Async XLA Ops:
  0.6 10.9 %copy-start = (f32[8,128,16,128]{3,2,1,0:T(8,128)S(1)}, f32[8,128,16,128]{3,2,1,0:T(8,128)}, u32[]{:S(2)}) copy-start(f32[8,128,16,128]{3,2,1,0:T(8,128)} %refs_7_.5) | copy-start | bytes 25165828
  4.4 7.1 %collective-permute-start.2 = (f32[2,128,16,128]{3,2,1,0:T(8,128)S(1)}, f32[2,128,16,128]{3,2,1,0:T(8,128)S(1)}, u32[]{:S(2)}, u32[]{:S(2)}) collective-permute-start(f32[2,128,16,128]{3,2,1,0:T(8,128)S(1)} %get-tuple-element.39), channel_id=1, source_target_pairs={{0,16},{16,0},{1,17},{17,1},{2,18},{18,2},{3,19},{19,3},{4,20},{20... | collective-permute-start | bytes 6291464 | tf_op jit(solution)/shard_map/ppermute | solution.py:306
  4.5 14.8 %collective-permute-start.4 = (f32[8,128,128]{2,1,0:T(8,128)S(1)}, f32[8,128,128]{2,1,0:T(8,128)S(1)}, u32[]{:S(2)}, u32[]{:S(2)}) collective-permute-start(f32[8,128,128]{2,1,0:T(8,128)S(1)} %get-tuple-element.44), channel_id=1, source_target_pairs={{1,0},{2,1},{3,2},{0,3},{5,4},{6,5},{7,6},{4,7},{9,8},{10,9},{11,1... | collective-permute-start | bytes 1572872 | tf_op jit(solution)/shard_map/ppermute | solution.py:330
  5.0 5.4 %collective-permute-start = (f32[8,16,128]{2,1,0:T(8,128)S(1)}, f32[8,16,128]{2,1,0:T(8,128)S(1)}, u32[]{:S(2)}, u32[]{:S(2)}) collective-permute-start(f32[8,16,128]{2,1,0:T(8,128)S(1)} %get-tuple-element.37), channel_id=1, source_target_pairs={{0,4},{4,8},{8,12},{12,0},{1,5},{5,9},{9,13},{13,1},{2,6},{6,10},{... | collective-permute-start | bytes 196616 | tf_op jit(solution)/shard_map/ppermute | solution.py:311
  6.5 5.0 %collective-permute-start.1 = (f32[8,16,128]{2,1,0:T(8,128)S(1)}, f32[8,16,128]{2,1,0:T(8,128)S(1)}, u32[]{:S(2)}, u32[]{:S(2)}) collective-permute-start(f32[8,16,128]{2,1,0:T(8,128)S(1)} %get-tuple-element.38), channel_id=1, source_target_pairs={{4,0},{8,4},{12,8},{0,12},{5,1},{9,5},{13,9},{1,13},{6,2},{10,6},{... | collective-permute-start | bytes 196616 | tf_op jit(solution)/shard_map/ppermute | solution.py:312
  7.9 24.0 %collective-permute-start.3 = (f32[8,128,128]{2,1,0:T(8,128)S(1)}, f32[8,128,128]{2,1,0:T(8,128)S(1)}, u32[]{:S(2)}, u32[]{:S(2)}) collective-permute-start(f32[8,128,128]{2,1,0:T(8,128)S(1)} %get-tuple-element.42), channel_id=1, source_target_pairs={{0,1},{1,2},{2,3},{3,0},{4,5},{5,6},{6,7},{7,4},{8,9},{9,10},{10,1... | collective-permute-start | bytes 1572872 | tf_op jit(solution)/shard_map/ppermute | solution.py:331
  32.6 8.5 %collective-permute-start.7 = (f32[2,128,16,128]{3,2,1,0:T(8,128)S(1)}, f32[2,128,16,128]{3,2,1,0:T(8,128)S(1)}, u32[]{:S(2)}, u32[]{:S(2)}) collective-permute-start(f32[2,128,16,128]{3,2,1,0:T(8,128)S(1)} %pad_maximum_fusion), channel_id=1, source_target_pairs={{0,16},{16,0},{1,17},{17,1},{2,18},{18,2},{3,19},{19,3},{4,20},{20... | collective-permute-start | bytes 6291464 | tf_op jit(solution)/shard_map/ppermute | solution.py:306
  32.6 14.8 %collective-permute-start.9 = (f32[8,128,128]{2,1,0:T(8,128)S(1)}, f32[8,128,128]{2,1,0:T(8,128)S(1)}, u32[]{:S(2)}, u32[]{:S(2)}) collective-permute-start(f32[8,128,128]{2,1,0:T(8,128)S(1)} %multiply_add_fusion.5.refs_1_), channel_id=1, source_target_pairs={{1,0},{2,1},{3,2},{0,3},{5,4},{6,5},{7,6},{4,7},{9,8},{10,9},{11,1... | collective-permute-start | bytes 1572872 | tf_op jit(solution)/shard_map/ppermute | solution.py:330
  33.4 4.9 %collective-permute-start.6 = (f32[8,16,128]{2,1,0:T(8,128)S(1)}, f32[8,16,128]{2,1,0:T(8,128)S(1)}, u32[]{:S(2)}, u32[]{:S(2)}) collective-permute-start(f32[8,16,128]{2,1,0:T(8,128)S(1)} %get-tuple-element.82), channel_id=1, source_target_pairs={{4,0},{8,4},{12,8},{0,12},{5,1},{9,5},{13,9},{1,13},{6,2},{10,6},{... | collective-permute-start | bytes 196616 | tf_op jit(solution)/shard_map/ppermute | solution.py:312
  35.9 5.2 %collective-permute-start.5 = (f32[8,16,128]{2,1,0:T(8,128)S(1)}, f32[8,16,128]{2,1,0:T(8,128)S(1)}, u32[]{:S(2)}, u32[]{:S(2)}) collective-permute-start(f32[8,16,128]{2,1,0:T(8,128)S(1)} %get-tuple-element.83), channel_id=1, source_target_pairs={{0,4},{4,8},{8,12},{12,0},{1,5},{5,9},{9,13},{13,1},{2,6},{6,10},{... | collective-permute-start | bytes 196616 | tf_op jit(solution)/shard_map/ppermute | solution.py:311
  35.9 24.1 %collective-permute-start.8 = (f32[8,128,128]{2,1,0:T(8,128)S(1)}, f32[8,128,128]{2,1,0:T(8,128)S(1)}, u32[]{:S(2)}, u32[]{:S(2)}) collective-permute-start(f32[8,128,128]{2,1,0:T(8,128)S(1)} %multiply_add_fusion.4.refs_2_), channel_id=1, source_target_pairs={{0,1},{1,2},{2,3},{3,0},{4,5},{5,6},{6,7},{7,4},{8,9},{9,10},{10,1... | collective-permute-start | bytes 1572872 | tf_op jit(solution)/shard_map/ppermute | solution.py:331
  60.6 8.4 %collective-permute-start.12 = (f32[2,128,16,128]{3,2,1,0:T(8,128)S(1)}, f32[2,128,16,128]{3,2,1,0:T(8,128)S(1)}, u32[]{:S(2)}, u32[]{:S(2)}) collective-permute-start(f32[2,128,16,128]{3,2,1,0:T(8,128)S(1)} %pad_maximum_fusion.1), channel_id=1, source_target_pairs={{0,16},{16,0},{1,17},{17,1},{2,18},{18,2},{3,19},{19,3},{4,20},{20... | collective-permute-start | bytes 6291464 | tf_op jit(solution)/shard_map/ppermute | solution.py:306
  60.7 14.8 %collective-permute-start.14 = (f32[8,128,128]{2,1,0:T(8,128)S(1)}, f32[8,128,128]{2,1,0:T(8,128)S(1)}, u32[]{:S(2)}, u32[]{:S(2)}) collective-permute-start(f32[8,128,128]{2,1,0:T(8,128)S(1)} %multiply_add_fusion.3.refs_1_), channel_id=1, source_target_pairs={{1,0},{2,1},{3,2},{0,3},{5,4},{6,5},{7,6},{4,7},{9,8},{10,9},{11,1... | collective-permute-start | bytes 1572872 | tf_op jit(solution)/shard_map/ppermute | solution.py:330
  61.5 4.7 %collective-permute-start.11 = (f32[8,16,128]{2,1,0:T(8,128)S(1)}, f32[8,16,128]{2,1,0:T(8,128)S(1)}, u32[]{:S(2)}, u32[]{:S(2)}) collective-permute-start(f32[8,16,128]{2,1,0:T(8,128)S(1)} %get-tuple-element.78), channel_id=1, source_target_pairs={{4,0},{8,4},{12,8},{0,12},{5,1},{9,5},{13,9},{1,13},{6,2},{10,6},{... | collective-permute-start | bytes 196616 | tf_op jit(solution)/shard_map/ppermute | solution.py:312
  63.8 5.2 %collective-permute-start.10 = (f32[8,16,128]{2,1,0:T(8,128)S(1)}, f32[8,16,128]{2,1,0:T(8,128)S(1)}, u32[]{:S(2)}, u32[]{:S(2)}) collective-permute-start(f32[8,16,128]{2,1,0:T(8,128)S(1)} %get-tuple-element.79), channel_id=1, source_target_pairs={{0,4},{4,8},{8,12},{12,0},{1,5},{5,9},{9,13},{13,1},{2,6},{6,10},{... | collective-permute-start | bytes 196616 | tf_op jit(solution)/shard_map/ppermute | solution.py:311
  63.8 24.2 %collective-permute-start.13 = (f32[8,128,128]{2,1,0:T(8,128)S(1)}, f32[8,128,128]{2,1,0:T(8,128)S(1)}, u32[]{:S(2)}, u32[]{:S(2)}) collective-permute-start(f32[8,128,128]{2,1,0:T(8,128)S(1)} %multiply_add_fusion.2.refs_2_), channel_id=1, source_target_pairs={{0,1},{1,2},{2,3},{3,0},{4,5},{5,6},{6,7},{7,4},{8,9},{9,10},{10,1... | collective-permute-start | bytes 1572872 | tf_op jit(solution)/shard_map/ppermute | solution.py:331
  88.7 9.2 %collective-permute-start.17 = (f32[2,128,16,128]{3,2,1,0:T(8,128)S(1)}, f32[2,128,16,128]{3,2,1,0:T(8,128)S(1)}, u32[]{:S(2)}, u32[]{:S(2)}) collective-permute-start(f32[2,128,16,128]{3,2,1,0:T(8,128)S(1)} %pad_maximum_fusion.2), channel_id=1, source_target_pairs={{0,16},{16,0},{1,17},{17,1},{2,18},{18,2},{3,19},{19,3},{4,20},{20... | collective-permute-start | bytes 6291464 | tf_op jit(solution)/shard_map/ppermute | solution.py:306
  88.8 16.0 %collective-permute-start.18 = (f32[8,128,128]{2,1,0:T(8,128)S(1)}, f32[8,128,128]{2,1,0:T(8,128)S(1)}, u32[]{:S(2)}, u32[]{:S(2)}) collective-permute-start(f32[8,128,128]{2,1,0:T(8,128)S(1)} %multiply_add_fusion.refs_2_), channel_id=1, source_target_pairs={{0,1},{1,2},{2,3},{3,0},{4,5},{5,6},{6,7},{7,4},{8,9},{9,10},{10,1... | collective-permute-start | bytes 1572872 | tf_op jit(solution)/shard_map/ppermute | solution.py:331
  90.4 4.7 %collective-permute-start.16 = (f32[8,16,128]{2,1,0:T(8,128)S(1)}, f32[8,16,128]{2,1,0:T(8,128)S(1)}, u32[]{:S(2)}, u32[]{:S(2)}) collective-permute-start(f32[8,16,128]{2,1,0:T(8,128)S(1)} %get-tuple-element.74), channel_id=1, source_target_pairs={{4,0},{8,4},{12,8},{0,12},{5,1},{9,5},{13,9},{1,13},{6,2},{10,6},{... | collective-permute-start | bytes 196616 | tf_op jit(solution)/shard_map/ppermute | solution.py:312
  92.7 5.2 %collective-permute-start.15 = (f32[8,16,128]{2,1,0:T(8,128)S(1)}, f32[8,16,128]{2,1,0:T(8,128)S(1)}, u32[]{:S(2)}, u32[]{:S(2)}) collective-permute-start(f32[8,16,128]{2,1,0:T(8,128)S(1)} %get-tuple-element.75), channel_id=1, source_target_pairs={{0,4},{4,8},{8,12},{12,0},{1,5},{5,9},{9,13},{13,1},{2,6},{6,10},{... | collective-permute-start | bytes 196616 | tf_op jit(solution)/shard_map/ppermute | solution.py:311
  92.8 39.5 %collective-permute-start.22 = (f32[8,128,128]{2,1,0:T(8,128)S(1)}, f32[8,128,128]{2,1,0:T(8,128)S(1)}, u32[]{:S(2)}, u32[]{:S(2)}) collective-permute-start(f32[8,128,128]{2,1,0:T(8,128)S(1)} %multiply_add_fusion.1.refs_1_), channel_id=1, source_target_pairs={{1,0},{2,1},{3,2},{0,3},{5,4},{6,5},{7,6},{4,7},{9,8},{10,9},{11,1... | collective-permute-start | bytes 1572872 | tf_op jit(solution)/shard_map/ppermute | solution.py:330
  105.1 2.7 %collective-permute-start.29 = (f32[2,128,128]{2,1,0:T(8,128)S(1)}, f32[2,128,128]{2,1,0:T(8,128)S(1)}, u32[]{:S(2)}, u32[]{:S(2)}) collective-permute-start(f32[2,128,128]{2,1,0:T(8,128)S(1)} %get-tuple-element.85), channel_id=1, source_target_pairs={{0,1},{4,5},{8,9},{12,13},{16,17},{20,21},{24,25},{28,29}} | collective-permute-start | bytes 393224 | tf_op jit(solution)/shard_map/ppermute | solution.py:352
  105.7 3.4 %collective-permute-start.26 = (f32[2,128,128]{2,1,0:T(8,128)S(1)}, f32[2,128,128]{2,1,0:T(8,128)S(1)}, u32[]{:S(2)}, u32[]{:S(2)}) collective-permute-start(f32[2,128,128]{2,1,0:T(8,128)S(1)} %get-tuple-element.86), channel_id=1, source_target_pairs={{0,1},{4,5},{8,9},{12,13},{16,17},{20,21},{24,25},{28,29}} | collective-permute-start | bytes 393224 | tf_op jit(solution)/shard_map/ppermute | solution.py:352
  106.4 4.0 %collective-permute-start.23 = (f32[2,128,128]{2,1,0:T(8,128)S(1)}, f32[2,128,128]{2,1,0:T(8,128)S(1)}, u32[]{:S(2)}, u32[]{:S(2)}) collective-permute-start(f32[2,128,128]{2,1,0:T(8,128)S(1)} %get-tuple-element.87), channel_id=1, source_target_pairs={{0,1},{4,5},{8,9},{12,13},{16,17},{20,21},{24,25},{28,29}} | collective-permute-start | bytes 393224 | tf_op jit(solution)/shard_map/ppermute | solution.py:352
  107.1 4.7 %collective-permute-start.19 = (f32[2,128,128]{2,1,0:T(8,128)S(1)}, f32[2,128,128]{2,1,0:T(8,128)S(1)}, u32[]{:S(2)}, u32[]{:S(2)}) collective-permute-start(f32[2,128,128]{2,1,0:T(8,128)S(1)} %get-tuple-element.88), channel_id=1, source_target_pairs={{0,1},{4,5},{8,9},{12,13},{16,17},{20,21},{24,25},{28,29}} | collective-permute-start | bytes 393224 | tf_op jit(solution)/shard_map/ppermute | solution.py:352
  107.8 14.9 %collective-permute-start.30 = (f32[2,128,128]{2,1,0:T(8,128)S(1)}, f32[2,128,128]{2,1,0:T(8,128)S(1)}, u32[]{:S(2)}, u32[]{:S(2)}) collective-permute-start(f32[2,128,128]{2,1,0:T(8,128)S(1)} %get-tuple-element.66), channel_id=1, source_target_pairs={{1,2},{5,6},{9,10},{13,14},{17,18},{21,22},{25,26},{29,30}} | collective-permute-start | bytes 393224 | tf_op jit(solution)/shard_map/ppermute | solution.py:352
  109.1 16.4 %collective-permute-start.27 = (f32[2,128,128]{2,1,0:T(8,128)S(1)}, f32[2,128,128]{2,1,0:T(8,128)S(1)}, u32[]{:S(2)}, u32[]{:S(2)}) collective-permute-start(f32[2,128,128]{2,1,0:T(8,128)S(1)} %get-tuple-element.62), channel_id=1, source_target_pairs={{1,2},{5,6},{9,10},{13,14},{17,18},{21,22},{25,26},{29,30}} | collective-permute-start | bytes 393224 | tf_op jit(solution)/shard_map/ppermute | solution.py:352
  110.5 17.9 %collective-permute-start.24 = (f32[2,128,128]{2,1,0:T(8,128)S(1)}, f32[2,128,128]{2,1,0:T(8,128)S(1)}, u32[]{:S(2)}, u32[]{:S(2)}) collective-permute-start(f32[2,128,128]{2,1,0:T(8,128)S(1)} %get-tuple-element.58), channel_id=1, source_target_pairs={{1,2},{5,6},{9,10},{13,14},{17,18},{21,22},{25,26},{29,30}} | collective-permute-start | bytes 393224 | tf_op jit(solution)/shard_map/ppermute | solution.py:352
  111.8 19.1 %collective-permute-start.20 = (f32[2,128,128]{2,1,0:T(8,128)S(1)}, f32[2,128,128]{2,1,0:T(8,128)S(1)}, u32[]{:S(2)}, u32[]{:S(2)}) collective-permute-start(f32[2,128,128]{2,1,0:T(8,128)S(1)} %get-tuple-element.54), channel_id=1, source_target_pairs={{1,2},{5,6},{9,10},{13,14},{17,18},{21,22},{25,26},{29,30}} | collective-permute-start | bytes 393224 | tf_op jit(solution)/shard_map/ppermute | solution.py:352
  122.8 16.3 %collective-permute-start.31 = (f32[2,128,128]{2,1,0:T(8,128)S(1)}, f32[2,128,128]{2,1,0:T(8,128)S(1)}, u32[]{:S(2)}, u32[]{:S(2)}) collective-permute-start(f32[2,128,128]{2,1,0:T(8,128)S(1)} %get-tuple-element.68), channel_id=1, source_target_pairs={{2,3},{6,7},{10,11},{14,15},{18,19},{22,23},{26,27},{30,31}} | collective-permute-start | bytes 393224 | tf_op jit(solution)/shard_map/ppermute | solution.py:352
  125.6 14.9 %collective-permute-start.28 = (f32[2,128,128]{2,1,0:T(8,128)S(1)}, f32[2,128,128]{2,1,0:T(8,128)S(1)}, u32[]{:S(2)}, u32[]{:S(2)}) collective-permute-start(f32[2,128,128]{2,1,0:T(8,128)S(1)} %get-tuple-element.64), channel_id=1, source_target_pairs={{2,3},{6,7},{10,11},{14,15},{18,19},{22,23},{26,27},{30,31}} | collective-permute-start | bytes 393224 | tf_op jit(solution)/shard_map/ppermute | solution.py:352
  128.4 13.6 %collective-permute-start.25 = (f32[2,128,128]{2,1,0:T(8,128)S(1)}, f32[2,128,128]{2,1,0:T(8,128)S(1)}, u32[]{:S(2)}, u32[]{:S(2)}) collective-permute-start(f32[2,128,128]{2,1,0:T(8,128)S(1)} %get-tuple-element.60), channel_id=1, source_target_pairs={{2,3},{6,7},{10,11},{14,15},{18,19},{22,23},{26,27},{30,31}} | collective-permute-start | bytes 393224 | tf_op jit(solution)/shard_map/ppermute | solution.py:352
  131.0 12.5 %collective-permute-start.21 = (f32[2,128,128]{2,1,0:T(8,128)S(1)}, f32[2,128,128]{2,1,0:T(8,128)S(1)}, u32[]{:S(2)}, u32[]{:S(2)}) collective-permute-start(f32[2,128,128]{2,1,0:T(8,128)S(1)} %get-tuple-element.56), channel_id=1, source_target_pairs={{2,3},{6,7},{10,11},{14,15},{18,19},{22,23},{26,27},{30,31}} | collective-permute-start | bytes 393224 | tf_op jit(solution)/shard_map/ppermute | solution.py:352

commit v3 on v2

--- a/solution.py
+++ b/solution.py
@@ -14,6 +14,7 @@
 
 
 CHUNKS = 8
+GRANT = 40
 SLOTS = 4
 VMEM = pl.BlockSpec(memory_space=pltpu.VMEM)
 HBM = pl.BlockSpec(memory_space=pltpu.HBM)
@@ -38,9 +39,34 @@
     return jnp.where(layer == depth - 1, jnp.expand_dims(high, -2), cells)
 
 
-def peel_kernel(f_ref, h_ref, low_ref, high_ref, both_ref, first_ref, final_ref, ground_ref, sems):
+def layers_kernel(f_ref, low_ref, high_ref, sems):
+    rows, _, depth, _ = f_ref.shape
+    copies = []
+    for side, (layer, face_ref) in enumerate(((0, low_ref), (depth - 1, high_ref))):
+        for row in range(rows):
+            copies.append(pltpu.make_async_copy(f_ref.at[row, :, layer], face_ref.at[row], sems.at[side, row]))
+            copies[-1].start()
+    for copy in copies:
+        copy.wait()
+
+
+def layers(field):
+    rows, span, _, lanes = field.shape
+    return pl.pallas_call(
+        layers_kernel,
+        in_specs=[HBM],
+        out_specs=[VMEM] * 2,
+        out_shape=[like((rows, span, lanes), field)] * 2,
+        scratch_shapes=[pltpu.SemaphoreType.DMA((2, rows))],
+        compiler_params=pltpu.CompilerParams(vmem_limit_bytes=50 * MIB),
+        cost_estimate=pl.CostEstimate(flops=field.size, bytes_accessed=field.size, transcendentals=0),
+        name="layers",
+    )(field)
+
+
+def peel_kernel(f_ref, h_ref, both_ref, first_ref, final_ref, ground_ref, sems):
     ground_ref[...] = jnp.full(ground_ref.shape, jnp.where(lax.axis_index("lev") == 0, 1.0, 0.0), ground_ref.dtype)
-    rows, span, depth, _ = h_ref.shape
+    rows, span, _, _ = h_ref.shape
     chunk = span // CHUNKS
     copies = []
     for k in range(CHUNKS):
@@ -49,9 +75,6 @@
         copies[-1].start()
 
     def one(at, _):
-        for row in range(rows):
-            low_ref[row, pl.ds(at, 1), :] = h_ref[row, at, pl.ds(0, 1), :]
-            high_ref[row, pl.ds(at, 1), :] = h_ref[row, at, pl.ds(depth - 1, 1), :]
         both_ref[0, at] = h_ref[0, at]
         both_ref[1, at] = h_ref[rows - 1, at]
         return 0
@@ -66,15 +89,14 @@
 
 def peel(field):
     rows, span, depth, lanes = field.shape
-    face = like((rows, span, lanes), field)
     edge = like((rows, depth, lanes), field)
     return pl.pallas_call(
         peel_kernel,
         in_specs=[HBM],
-        out_specs=[VMEM] * 7,
-        out_shape=[like(field.shape, field), face, face, like((2, span, depth, lanes), field), edge, edge, like((1, 1, lanes), field)],
+        out_specs=[VMEM] * 5,
+        out_shape=[like(field.shape, field), like((2, span, depth, lanes), field), edge, edge, like((1, 1, lanes), field)],
         scratch_shapes=[pltpu.SemaphoreType.DMA((CHUNKS,))],
-        compiler_params=pltpu.CompilerParams(vmem_limit_bytes=42 * MIB),
+        compiler_params=pltpu.CompilerParams(vmem_limit_bytes=GRANT * MIB),
         cost_estimate=pl.CostEstimate(flops=4 * field.size, bytes_accessed=field.size, transcendentals=0),
         name="peel",
     )(field)
@@ -324,17 +346,21 @@
     levs = lax.axis_size("lev")
     depth = field.shape[2]
     faces = None
-    h, low, high, both, first, final, ground = peel(field)
+    h, both, first, final, ground = peel(field)
+    low, high = layers(field)
+    raw_low, raw_high = low, high
     for step in range(STEPS):
         last = step == STEPS - 1
-        above = lax.ppermute(low, "lev", downs(levs))
-        below = lax.ppermute(high, "lev", ups(levs))
+        below = lax.ppermute(raw_high, "lev", ups(levs))
+        above = lax.ppermute(raw_low, "lev", downs(levs))
+        if step:
+            below, above = below + 0.1 * older[0], above + 0.1 * older[1]
         halos = side_halos(both, first, final)
         outs = march(h, faces, *halos, crowding, last)
-        h = outs[0]
+        h, older = outs[0], (low, high)
         if not last:
-            low = outs[1] + 0.1 * below
-            high = outs[2] + 0.1 * above
+            raw_low, raw_high = outs[1], outs[2]
+            low, high = raw_low + 0.1 * below, raw_high + 0.1 * above
             faces = (low, high)
             both, first, final = edges(h, low, high)
     rest = 0.1 * jnp.where(ground > 0.0, below, low)

time: 145 us -> 146 us (level)
  waiting for transfers between devices: 69 us -> 60.2 us
  local copies, waits for them, and re-layouts: 0.16 us -> 6.93 us
    ppermute x8, waiting for transfers between devices: 40.8 us -> 28.8 us  [the longest x4 20 us: steps(): above = lax.ppermute(raw_low, 'lev', downs(levs))]
    unnamed x2 -> x6, local copies, waits for them, and re-layouts: 0.01 us -> 6.77 us
    ppermute x4, waiting for transfers between devices: 9.24 us -> 11 us  [side_halos(): xlow = lax.ppermute(final, 'lon', ups(lons))]
    ppermute x12, waiting for transfers between devices: 13.9 us -> 15.4 us  [steps(): gots[part] = lax.ppermute(nexts[part], 'lev', [(hop, hop + 1)])]
    pallas_call x1 -> x2, Pallas kernels: 3.74 us -> 5.01 us  [the longest x1 3.51 us: peel(): pl.pallas_call(peel_kernel, in_specs=[HBM], out_specs=[VMEM] * 5, out_sha...]
  transfers between devices with their start and end apart: 32 -> 32, of which waited for: 18 -> 15; matrix products, arithmetic and copies ran while one was open for 1% -> 1% of each run, Pallas kernels for 24% -> 25%
where the time goes in v3:
time: 146 us; the launch traced here: 145 us
  waiting for transfers between devices  60.2 us (41%)
  Pallas kernels  41.8 us (29%)
  starting transfers between devices  32.4 us (22%)
  local copies, waits for them, and re-layouts  6.93 us (5%)
  other arithmetic  2.79 us (2%)
    pallas_call x4, Pallas kernels, march(): pl.pallas_call(functools.partial(march_kernel, faces is not None, last, y...  24.1 us
    ppermute x4, waiting for transfers between devices, steps(): above = lax.ppermute(raw_low, 'lev', downs(levs))  20 us
    ppermute x12, waiting for transfers between devices, steps(): gots[part] = lax.ppermute(nexts[part], 'lev', [(hop, hop + 1)])  15.4 us
    ppermute x12, starting transfers between devices, steps(): gots[part] = lax.ppermute(nexts[part], 'lev', [(hop, hop + 1)])  13 us
    ppermute x4, waiting for transfers between devices, side_halos(): xlow = lax.ppermute(final, 'lon', ups(lons))  11 us
    ppermute x4, starting transfers between devices, side_halos(): xhigh = lax.ppermute(first, 'lon', downs(lons))  8.93 us
    ppermute x4, waiting for transfers between devices, steps(): below = lax.ppermute(raw_high, 'lev', ups(levs))  8.79 us
    unnamed x6, local copies, waits for them, and re-layouts  6.77 us
  transfers between devices with their start and end apart: 32, of which 15 were waited for; matrix products, arithmetic and copies ran while one was open for 1% of the time, Pallas kernels for 25%

profile of v3, /device:TPU:16, one launch (start us, length us, event | category | flops | bytes accessed | tf_op | source)
XLA Modules:
  0.0 145.3 jit_solution(4469868611133509905)
XLA Ops:
  0.6 3.5 %peel.1 = (f32[8,128,16,128]{3,2,1,0:T(8,128)S(1)}, f32[2,128,16,128]{3,2,1,0:T(8,128)S(1)}, f32[8,16,128]{2,1,0:T(8,128)S(1)}, f32[8,16,128]{2,1,0:T(8,128)S(1)}, f32[1,1,128]{2,1,0:T(1,128)S(1)}) custom-call(f32[8,128,16,128]{3,2,1,0:T(8,128)} %f_ref.3), custom_call_target="tpu_custom_call" | custom-call | flops 8388608 | bytes 2097152 | tf_op jit(solution)/shard_map/peel/pallas_call | solution.py:93
  4.2 1.5 %layers.1 = (f32[8,128,128]{2,1,0:T(8,128)S(1)}, f32[8,128,128]{2,1,0:T(8,128)S(1)}) custom-call(f32[8,128,16,128]{3,2,1,0:T(8,128)} %f_ref.3), custom_call_target="tpu_custom_call" | custom-call | flops 2097152 | bytes 2097152 | tf_op jit(solution)/shard_map/layers/pallas_call | solution.py:55
  5.7 0.5 collective-permute-start.4
  6.2 1.6 %collective-permute-start.3 = (f32[8,128,128]{2,1,0:T(8,128)S(1)}, f32[8,128,128]{2,1,0:T(8,128)S(1)}, u32[]{:S(2)}, u32[]{:S(2)}) collective-permute-start(f32[8,128,128]{2,1,0:T(8,128)S(1)} %get-tuple-element.42), channel_id=1, source_target_pairs={{0,1},{1,2},{2,3},{3,0},{4,5},{5,6},{6,7},{7,4},{8,9},{9,10},{10,1... | collective-permute-start | bytes 1572872 | tf_op jit(solution)/shard_map/ppermute | solution.py:354
  7.8 1.5 %collective-permute-start = (f32[8,16,128]{2,1,0:T(8,128)S(1)}, f32[8,16,128]{2,1,0:T(8,128)S(1)}, u32[]{:S(2)}, u32[]{:S(2)}) collective-permute-start(f32[8,16,128]{2,1,0:T(8,128)S(1)} %get-tuple-element.37), channel_id=1, source_target_pairs={{0,4},{4,8},{8,12},{12,0},{1,5},{5,9},{9,13},{13,1},{2,6},{6,10},{... | collective-permute-start | bytes 196616 | tf_op jit(solution)/shard_map/ppermute | solution.py:333
  9.3 1.4 collective-permute-start.1
  10.7 2.7 %collective-permute-done.refs_1_ = f32[8,16,128]{2,1,0:T(8,128)S(1)} collective-permute-done((f32[8,16,128]{2,1,0:T(8,128)S(1)}, f32[8,16,128]{2,1,0:T(8,128)S(1)}, u32[]{:S(2)}, u32[]{:S(2)}) %collective-permute-start) | collective-permute-done | bytes 65568 | tf_op jit(solution)/shard_map/ppermute | solution.py:333
  13.4 0.7 collective-permute-done.1.refs_2_
  14.1 3.4 %copy-done = f32[8,128,16,128]{3,2,1,0:T(8,128)S(1)} copy-done((f32[8,128,16,128]{3,2,1,0:T(8,128)S(1)}, f32[8,128,16,128]{3,2,1,0:T(8,128)}, u32[]{:S(2)}) %copy-start) | copy-done | bytes 8388632
  17.5 5.1 %march.4 = (f32[8,128,16,128]{3,2,1,0:T(8,128)S(1)}, f32[8,128,128]{2,1,0:T(8,128)S(1)}, f32[8,128,128]{2,1,0:T(8,128)S(1)}) custom-call(f32[8,128,16,128]{3,2,1,0:T(8,128)S(1)} %get-tuple-element.36.refs_0_, f32[8,16,128]{2,1,0:T(8,128)S(1)} %collective-permute-done.refs_1_, ...), custom_call_target="tpu_custom_call", output_to_operand_aliasing={{0}: (0, {})} | custom-call | flops 33554432 | bytes 25165824 | tf_op jit(solution)/shard_map/march/pallas_call | solution.py:170
  22.7 8.8 %collective-permute-done.3 = f32[8,128,128]{2,1,0:T(8,128)S(1)} collective-permute-done((f32[8,128,128]{2,1,0:T(8,128)S(1)}, f32[8,128,128]{2,1,0:T(8,128)S(1)}, u32[]{:S(2)}, u32[]{:S(2)}) %collective-permute-start.3) | collective-permute-done | bytes 524320 | tf_op jit(solution)/shard_map/ppermute | solution.py:354
  31.6 0.4 select_select_fusion.5
  32.0 0.1 pad_maximum_fusion
  32.2 1.6 %collective-permute-start.8 = (f32[8,128,128]{2,1,0:T(8,128)S(1)}, f32[8,128,128]{2,1,0:T(8,128)S(1)}, u32[]{:S(2)}, u32[]{:S(2)}) collective-permute-start(f32[8,128,128]{2,1,0:T(8,128)S(1)} %get-tuple-element.43), channel_id=1, source_target_pairs={{0,1},{1,2},{2,3},{3,0},{4,5},{5,6},{6,7},{7,4},{8,9},{9,10},{10,1... | collective-permute-start | bytes 1572872 | tf_op jit(solution)/shard_map/ppermute | solution.py:354
  33.9 2.5 %collective-permute-start.6 = (f32[8,16,128]{2,1,0:T(8,128)S(1)}, f32[8,16,128]{2,1,0:T(8,128)S(1)}, u32[]{:S(2)}, u32[]{:S(2)}) collective-permute-start(f32[8,16,128]{2,1,0:T(8,128)S(1)} %get-tuple-element.82), channel_id=1, source_target_pairs={{4,0},{8,4},{12,8},{0,12},{5,1},{9,5},{13,9},{1,13},{6,2},{10,6},{... | collective-permute-start | bytes 196616 | tf_op jit(solution)/shard_map/ppermute | solution.py:334
  36.5 0.8 collective-permute-start.9
  37.2 1.6 %collective-permute-done.6.refs_4_ = f32[8,16,128]{2,1,0:T(8,128)S(1)} collective-permute-done((f32[8,16,128]{2,1,0:T(8,128)S(1)}, f32[8,16,128]{2,1,0:T(8,128)S(1)}, u32[]{:S(2)}, u32[]{:S(2)}) %collective-permute-start.6) | collective-permute-done | bytes 65568 | tf_op jit(solution)/shard_map/ppermute | solution.py:334
  38.8 2.8 %collective-permute-done.5.refs_3_ = f32[8,16,128]{2,1,0:T(8,128)S(1)} collective-permute-done((f32[8,16,128]{2,1,0:T(8,128)S(1)}, f32[8,16,128]{2,1,0:T(8,128)S(1)}, u32[]{:S(2)}, u32[]{:S(2)}) %collective-permute-start.5) | collective-permute-done | bytes 65568 | tf_op jit(solution)/shard_map/ppermute | solution.py:333
  41.6 3.4 %copy-done.1 = f32[8,128,16,128]{3,2,1,0:T(8,128)S(1)} copy-done((f32[8,128,16,128]{3,2,1,0:T(8,128)S(1)}, f32[8,128,16,128]{3,2,1,0:T(8,128)}, u32[]{:S(2)}) %copy-start.1) | copy-done | bytes 8388632
  45.0 6.0 %march.5 = (f32[8,128,16,128]{3,2,1,0:T(8,128)S(1)}, f32[8,128,128]{2,1,0:T(8,128)S(1)}, f32[8,128,128]{2,1,0:T(8,128)S(1)}) custom-call(f32[8,128,16,128]{3,2,1,0:T(8,128)S(1)} %get-tuple-element.40.refs_0_, f32[8,128,128]{2,1,0:T(8,128)S(1)} %multiply_add_fusion.6.refs_1_, ...), custom_call_target="tpu_custom_call", output_to_operand_aliasing={{0}: (0, {})} | custom-call | flops 33554432 | bytes 25165824 | tf_op jit(solution)/shard_map/march/pallas_call | solution.py:170
  51.1 0.1 multiply_add_fusion.4.refs_1_
  51.2 8.2 %collective-permute-done.9 = f32[8,128,128]{2,1,0:T(8,128)S(1)} collective-permute-done((f32[8,128,128]{2,1,0:T(8,128)S(1)}, f32[8,128,128]{2,1,0:T(8,128)S(1)}, u32[]{:S(2)}, u32[]{:S(2)}) %collective-permute-start.9) | collective-permute-done | bytes 524320 | tf_op jit(solution)/shard_map/ppermute | solution.py:355
  59.4 0.1 multiply_add_fusion.3.refs_2_
  59.6 0.4 select_select_fusion.3
  60.0 0.1 pad_maximum_fusion.1
  60.2 1.6 %collective-permute-start.13 = (f32[8,128,128]{2,1,0:T(8,128)S(1)}, f32[8,128,128]{2,1,0:T(8,128)S(1)}, u32[]{:S(2)}, u32[]{:S(2)}) collective-permute-start(f32[8,128,128]{2,1,0:T(8,128)S(1)} %get-tuple-element.47), channel_id=1, source_target_pairs={{0,1},{1,2},{2,3},{3,0},{4,5},{5,6},{6,7},{7,4},{8,9},{9,10},{10,1... | collective-permute-start | bytes 1572872 | tf_op jit(solution)/shard_map/ppermute | solution.py:354
  61.9 2.5 %collective-permute-start.11 = (f32[8,16,128]{2,1,0:T(8,128)S(1)}, f32[8,16,128]{2,1,0:T(8,128)S(1)}, u32[]{:S(2)}, u32[]{:S(2)}) collective-permute-start(f32[8,16,128]{2,1,0:T(8,128)S(1)} %get-tuple-element.78), channel_id=1, source_target_pairs={{4,0},{8,4},{12,8},{0,12},{5,1},{9,5},{13,9},{1,13},{6,2},{10,6},{... | collective-permute-start | bytes 196616 | tf_op jit(solution)/shard_map/ppermute | solution.py:334
  64.4 0.4 collective-permute-start.14
  64.9 1.9 %collective-permute-done.11.refs_4_ = f32[8,16,128]{2,1,0:T(8,128)S(1)} collective-permute-done((f32[8,16,128]{2,1,0:T(8,128)S(1)}, f32[8,16,128]{2,1,0:T(8,128)S(1)}, u32[]{:S(2)}, u32[]{:S(2)}) %collective-permute-start.11) | collective-permute-done | bytes 65568 | tf_op jit(solution)/shard_map/ppermute | solution.py:334
  66.8 2.8 %collective-permute-done.10.refs_3_ = f32[8,16,128]{2,1,0:T(8,128)S(1)} collective-permute-done((f32[8,16,128]{2,1,0:T(8,128)S(1)}, f32[8,16,128]{2,1,0:T(8,128)S(1)}, u32[]{:S(2)}, u32[]{:S(2)}) %collective-permute-start.10) | collective-permute-done | bytes 65568 | tf_op jit(solution)/shard_map/ppermute | solution.py:333
  69.6 6.0 %march.6 = (f32[8,128,16,128]{3,2,1,0:T(8,128)S(1)}, f32[8,128,128]{2,1,0:T(8,128)S(1)}, f32[8,128,128]{2,1,0:T(8,128)S(1)}) custom-call(f32[8,128,16,128]{3,2,1,0:T(8,128)S(1)} %get-tuple-element.45.refs_0_, f32[8,128,128]{2,1,0:T(8,128)S(1)} %multiply_add_fusion.4.refs_1_, ...), custom_call_target="tpu_custom_call", output_to_operand_aliasing={{0}: (0, {})} | custom-call | flops 33554432 | bytes 25165824 | tf_op jit(solution)/shard_map/march/pallas_call | solution.py:170
  75.8 11.8 %collective-permute-done.14 = f32[8,128,128]{2,1,0:T(8,128)S(1)} collective-permute-done((f32[8,128,128]{2,1,0:T(8,128)S(1)}, f32[8,128,128]{2,1,0:T(8,128)S(1)}, u32[]{:S(2)}, u32[]{:S(2)}) %collective-permute-start.14) | collective-permute-done | bytes 524320 | tf_op jit(solution)/shard_map/ppermute | solution.py:355
  87.6 0.1 multiply_add_fusion.1.refs_2_
  87.7 0.4 select_select_fusion.1
  88.1 0.1 pad_maximum_fusion.2
  88.3 0.5 collective-permute-start.18
  89.0 2.5 %collective-permute-start.16 = (f32[8,16,128]{2,1,0:T(8,128)S(1)}, f32[8,16,128]{2,1,0:T(8,128)S(1)}, u32[]{:S(2)}, u32[]{:S(2)}) collective-permute-start(f32[8,16,128]{2,1,0:T(8,128)S(1)} %get-tuple-element.74), channel_id=1, source_target_pairs={{4,0},{8,4},{12,8},{0,12},{5,1},{9,5},{13,9},{1,13},{6,2},{10,6},{... | collective-permute-start | bytes 196616 | tf_op jit(solution)/shard_map/ppermute | solution.py:334
  91.5 1.6 %collective-permute-start.22 = (f32[8,128,128]{2,1,0:T(8,128)S(1)}, f32[8,128,128]{2,1,0:T(8,128)S(1)}, u32[]{:S(2)}, u32[]{:S(2)}) collective-permute-start(f32[8,128,128]{2,1,0:T(8,128)S(1)} %get-tuple-element.49), channel_id=1, source_target_pairs={{1,0},{2,1},{3,2},{0,3},{5,4},{6,5},{7,6},{4,7},{9,8},{10,9},{11,1... | collective-permute-start | bytes 1572872 | tf_op jit(solution)/shard_map/ppermute | solution.py:355
  93.1 0.8 collective-permute-done.16.refs_4_
  93.9 2.8 %collective-permute-done.15.refs_3_ = f32[8,16,128]{2,1,0:T(8,128)S(1)} collective-permute-done((f32[8,16,128]{2,1,0:T(8,128)S(1)}, f32[8,16,128]{2,1,0:T(8,128)S(1)}, u32[]{:S(2)}, u32[]{:S(2)}) %collective-permute-start.15) | collective-permute-done | bytes 65568 | tf_op jit(solution)/shard_map/ppermute | solution.py:333
  96.7 6.9 %march.7 = (f32[8,128,16,128]{3,2,1,0:T(8,128)S(1)}, f32[8,128,128]{2,1,0:T(8,128)S(1)}) custom-call(f32[8,128,16,128]{3,2,1,0:T(8,128)S(1)} %get-tuple-element.48.refs_0_, f32[8,128,128]{2,1,0:T(8,128)S(1)} %multiply_add_fusion.2.refs_1_, f32[8,128,128]{2,1,0:T(8,128)S(1)} %multiply_add_fusion.1.refs_2_, ...), custom_call_target="tpu_custom_call", output_to_operand_aliasing={{0}: (0, {})} | custom-call | flops 33554432 | bytes 25165824 | tf_op jit(solution)/shard_map/march/pallas_call | solution.py:170
  103.6 0.2 add_add_fusion
  103.9 0.7 collective-permute-start.29
  104.5 0.7 collective-permute-start.26
  105.2 0.7 collective-permute-start.23
  105.9 0.7 collective-permute-start.19
  106.6 1.3 collective-permute-start.30
  108.0 1.3 collective-permute-start.27
  109.3 1.3 collective-permute-start.24
  110.6 1.3 collective-permute-start.20
  111.9 11.2 %collective-permute-done.30.got_ref = f32[2,128,128]{2,1,0:T(8,128)S(1)} collective-permute-done((f32[2,128,128]{2,1,0:T(8,128)S(1)}, f32[2,128,128]{2,1,0:T(8,128)S(1)}, u32[]{:S(2)}, u32[]{:S(2)}) %collective-permute-start.30) | collective-permute-done | bytes 131104 | tf_op jit(solution)/shard_map/ppermute | solution.py:378
  123.1 1.3 collective-permute-start.31
  124.4 1.5 %collective-permute-done.27.got_ref = f32[2,128,128]{2,1,0:T(8,128)S(1)} collective-permute-done((f32[2,128,128]{2,1,0:T(8,128)S(1)}, f32[2,128,128]{2,1,0:T(8,128)S(1)}, u32[]{:S(2)}, u32[]{:S(2)}) %collective-permute-start.27) | collective-permute-done | bytes 131104 | tf_op jit(solution)/shard_map/ppermute | solution.py:378
  125.9 1.3 collective-permute-start.28
  127.3 1.5 %collective-permute-done.24.got_ref = f32[2,128,128]{2,1,0:T(8,128)S(1)} collective-permute-done((f32[2,128,128]{2,1,0:T(8,128)S(1)}, f32[2,128,128]{2,1,0:T(8,128)S(1)}, u32[]{:S(2)}, u32[]{:S(2)}) %collective-permute-start.24) | collective-permute-done | bytes 131104 | tf_op jit(solution)/shard_map/ppermute | solution.py:378
  128.8 1.3 collective-permute-start.25
  130.1 1.3 collective-permute-done.20.got_ref
  131.3 1.3 collective-permute-start.21
  132.8 3.5 %ending.1 = f32[8,128,16,128]{3,2,1,0:T(8,128)} custom-call(f32[8,128,16,128]{3,2,1,0:T(8,128)S(1)} %get-tuple-element.51.h_ref, f32[8,128,128]{2,1,0:T(8,128)S(1)} %get-tuple-element.84.low_ref, f32[8,128,128]{2,1,0:T(8,128)S(1)} %add_multiply_fusion.high_ref), custom_call_target="tpu_custom_call" | custom-call | flops 4194304 | bytes 16777216 | tf_op jit(solution)/shard_map/ending/pallas_call | solution.py:248
  136.3 3.1 %sums.1.sum_ref = f32[8,128,16,128]{3,2,1,0:T(8,128)S(1)} custom-call(f32[8,128,16,128]{3,2,1,0:T(8,128)S(1)} %get-tuple-element.51.h_ref), custom_call_target="tpu_custom_call" | custom-call | flops 16777216 | bytes 16777216 | tf_op jit(solution)/shard_map/sums/pallas_call | solution.py:204
  139.5 1.4 potential.4.refs_1_
  140.9 1.5 potential.5.refs_1_
  142.4 1.5 potential.6.refs_1_
  143.9 1.5 potential.7
  (58 shorter events, 1.3 us)
Async XLA Ops:
  4.1 10.0 %collective-permute-start.2 = (f32[2,128,16,128]{3,2,1,0:T(8,128)S(1)}, f32[2,128,16,128]{3,2,1,0:T(8,128)S(1)}, u32[]{:S(2)}, u32[]{:S(2)}) collective-permute-start(f32[2,128,16,128]{3,2,1,0:T(8,128)S(1)} %get-tuple-element.39), channel_id=1, source_target_pairs={{0,16},{16,0},{1,17},{17,1},{2,18},{18,2},{3,19},{19,3},{4,20},{20... | collective-permute-start | bytes 6291464 | tf_op jit(solution)/shard_map/ppermute | solution.py:328
  5.7 16.9 %collective-permute-start.4 = (f32[8,128,128]{2,1,0:T(8,128)S(1)}, f32[8,128,128]{2,1,0:T(8,128)S(1)}, u32[]{:S(2)}, u32[]{:S(2)}) collective-permute-start(f32[8,128,128]{2,1,0:T(8,128)S(1)} %get-tuple-element.44), channel_id=1, source_target_pairs={{1,0},{2,1},{3,2},{0,3},{5,4},{6,5},{7,6},{4,7},{9,8},{10,9},{11,1... | collective-permute-start | bytes 1572872 | tf_op jit(solution)/shard_map/ppermute | solution.py:355
  6.2 25.3 %collective-permute-start.3 = (f32[8,128,128]{2,1,0:T(8,128)S(1)}, f32[8,128,128]{2,1,0:T(8,128)S(1)}, u32[]{:S(2)}, u32[]{:S(2)}) collective-permute-start(f32[8,128,128]{2,1,0:T(8,128)S(1)} %get-tuple-element.42), channel_id=1, source_target_pairs={{0,1},{1,2},{2,3},{3,0},{4,5},{5,6},{6,7},{7,4},{8,9},{9,10},{10,1... | collective-permute-start | bytes 1572872 | tf_op jit(solution)/shard_map/ppermute | solution.py:354
  7.8 5.6 %collective-permute-start = (f32[8,16,128]{2,1,0:T(8,128)S(1)}, f32[8,16,128]{2,1,0:T(8,128)S(1)}, u32[]{:S(2)}, u32[]{:S(2)}) collective-permute-start(f32[8,16,128]{2,1,0:T(8,128)S(1)} %get-tuple-element.37), channel_id=1, source_target_pairs={{0,4},{4,8},{8,12},{12,0},{1,5},{5,9},{9,13},{13,1},{2,6},{6,10},{... | collective-permute-start | bytes 196616 | tf_op jit(solution)/shard_map/ppermute | solution.py:333
  9.3 4.8 %collective-permute-start.1 = (f32[8,16,128]{2,1,0:T(8,128)S(1)}, f32[8,16,128]{2,1,0:T(8,128)S(1)}, u32[]{:S(2)}, u32[]{:S(2)}) collective-permute-start(f32[8,16,128]{2,1,0:T(8,128)S(1)} %get-tuple-element.38), channel_id=1, source_target_pairs={{4,0},{8,4},{12,8},{0,12},{5,1},{9,5},{13,9},{1,13},{6,2},{10,6},{... | collective-permute-start | bytes 196616 | tf_op jit(solution)/shard_map/ppermute | solution.py:334
  14.1 3.4 %copy-start = (f32[8,128,16,128]{3,2,1,0:T(8,128)S(1)}, f32[8,128,16,128]{3,2,1,0:T(8,128)}, u32[]{:S(2)}) copy-start(f32[8,128,16,128]{3,2,1,0:T(8,128)} %refs_7_.5) | copy-start | bytes 25165828
  32.1 9.5 %collective-permute-start.7 = (f32[2,128,16,128]{3,2,1,0:T(8,128)S(1)}, f32[2,128,16,128]{3,2,1,0:T(8,128)S(1)}, u32[]{:S(2)}, u32[]{:S(2)}) collective-permute-start(f32[2,128,16,128]{3,2,1,0:T(8,128)S(1)} %pad_maximum_fusion), channel_id=1, source_target_pairs={{0,16},{16,0},{1,17},{17,1},{2,18},{18,2},{3,19},{19,3},{4,20},{20... | collective-permute-start | bytes 6291464 | tf_op jit(solution)/shard_map/ppermute | solution.py:328
  32.2 18.9 %collective-permute-start.8 = (f32[8,128,128]{2,1,0:T(8,128)S(1)}, f32[8,128,128]{2,1,0:T(8,128)S(1)}, u32[]{:S(2)}, u32[]{:S(2)}) collective-permute-start(f32[8,128,128]{2,1,0:T(8,128)S(1)} %get-tuple-element.43), channel_id=1, source_target_pairs={{0,1},{1,2},{2,3},{3,0},{4,5},{5,6},{6,7},{7,4},{8,9},{9,10},{10,1... | collective-permute-start | bytes 1572872 | tf_op jit(solution)/shard_map/ppermute | solution.py:354
  33.9 4.9 %collective-permute-start.6 = (f32[8,16,128]{2,1,0:T(8,128)S(1)}, f32[8,16,128]{2,1,0:T(8,128)S(1)}, u32[]{:S(2)}, u32[]{:S(2)}) collective-permute-start(f32[8,16,128]{2,1,0:T(8,128)S(1)} %get-tuple-element.82), channel_id=1, source_target_pairs={{4,0},{8,4},{12,8},{0,12},{5,1},{9,5},{13,9},{1,13},{6,2},{10,6},{... | collective-permute-start | bytes 196616 | tf_op jit(solution)/shard_map/ppermute | solution.py:334
  36.4 5.2 %collective-permute-start.5 = (f32[8,16,128]{2,1,0:T(8,128)S(1)}, f32[8,16,128]{2,1,0:T(8,128)S(1)}, u32[]{:S(2)}, u32[]{:S(2)}) collective-permute-start(f32[8,16,128]{2,1,0:T(8,128)S(1)} %get-tuple-element.83), channel_id=1, source_target_pairs={{0,4},{4,8},{8,12},{12,0},{1,5},{5,9},{9,13},{13,1},{2,6},{6,10},{... | collective-permute-start | bytes 196616 | tf_op jit(solution)/shard_map/ppermute | solution.py:333
  36.5 23.0 %collective-permute-start.9 = (f32[8,128,128]{2,1,0:T(8,128)S(1)}, f32[8,128,128]{2,1,0:T(8,128)S(1)}, u32[]{:S(2)}, u32[]{:S(2)}) collective-permute-start(f32[8,128,128]{2,1,0:T(8,128)S(1)} %get-tuple-element.41), channel_id=1, source_target_pairs={{1,0},{2,1},{3,2},{0,3},{5,4},{6,5},{7,6},{4,7},{9,8},{10,9},{11,1... | collective-permute-start | bytes 1572872 | tf_op jit(solution)/shard_map/ppermute | solution.py:355
  41.6 3.4 %copy-start.1 = (f32[8,128,16,128]{3,2,1,0:T(8,128)S(1)}, f32[8,128,16,128]{3,2,1,0:T(8,128)}, u32[]{:S(2)}) copy-start(f32[8,128,16,128]{3,2,1,0:T(8,128)} %refs_7_.5) | copy-start | bytes 25165828
  51.0 18.6 %copy-start.2 = (f32[8,128,16,128]{3,2,1,0:T(8,128)S(1)}, f32[8,128,16,128]{3,2,1,0:T(8,128)}, u32[]{:S(2)}) copy-start(f32[8,128,16,128]{3,2,1,0:T(8,128)} %refs_7_.5) | copy-start | bytes 25165828
  60.1 9.5 %collective-permute-start.12 = (f32[2,128,16,128]{3,2,1,0:T(8,128)S(1)}, f32[2,128,16,128]{3,2,1,0:T(8,128)S(1)}, u32[]{:S(2)}, u32[]{:S(2)}) collective-permute-start(f32[2,128,16,128]{3,2,1,0:T(8,128)S(1)} %pad_maximum_fusion.1), channel_id=1, source_target_pairs={{0,16},{16,0},{1,17},{17,1},{2,18},{18,2},{3,19},{19,3},{4,20},{20... | collective-permute-start | bytes 6291464 | tf_op jit(solution)/shard_map/ppermute | solution.py:328
  60.2 15.5 %collective-permute-start.13 = (f32[8,128,128]{2,1,0:T(8,128)S(1)}, f32[8,128,128]{2,1,0:T(8,128)S(1)}, u32[]{:S(2)}, u32[]{:S(2)}) collective-permute-start(f32[8,128,128]{2,1,0:T(8,128)S(1)} %get-tuple-element.47), channel_id=1, source_target_pairs={{0,1},{1,2},{2,3},{3,0},{4,5},{5,6},{6,7},{7,4},{8,9},{9,10},{10,1... | collective-permute-start | bytes 1572872 | tf_op jit(solution)/shard_map/ppermute | solution.py:354
  61.9 4.9 %collective-permute-start.11 = (f32[8,16,128]{2,1,0:T(8,128)S(1)}, f32[8,16,128]{2,1,0:T(8,128)S(1)}, u32[]{:S(2)}, u32[]{:S(2)}) collective-permute-start(f32[8,16,128]{2,1,0:T(8,128)S(1)} %get-tuple-element.78), channel_id=1, source_target_pairs={{4,0},{8,4},{12,8},{0,12},{5,1},{9,5},{13,9},{1,13},{6,2},{10,6},{... | collective-permute-start | bytes 196616 | tf_op jit(solution)/shard_map/ppermute | solution.py:334
  64.4 5.2 %collective-permute-start.10 = (f32[8,16,128]{2,1,0:T(8,128)S(1)}, f32[8,16,128]{2,1,0:T(8,128)S(1)}, u32[]{:S(2)}, u32[]{:S(2)}) collective-permute-start(f32[8,16,128]{2,1,0:T(8,128)S(1)} %get-tuple-element.79), channel_id=1, source_target_pairs={{0,4},{4,8},{8,12},{12,0},{1,5},{5,9},{9,13},{13,1},{2,6},{6,10},{... | collective-permute-start | bytes 196616 | tf_op jit(solution)/shard_map/ppermute | solution.py:333
  64.4 23.1 %collective-permute-start.14 = (f32[8,128,128]{2,1,0:T(8,128)S(1)}, f32[8,128,128]{2,1,0:T(8,128)S(1)}, u32[]{:S(2)}, u32[]{:S(2)}) collective-permute-start(f32[8,128,128]{2,1,0:T(8,128)S(1)} %get-tuple-element.46), channel_id=1, source_target_pairs={{1,0},{2,1},{3,2},{0,3},{5,4},{6,5},{7,6},{4,7},{9,8},{10,9},{11,1... | collective-permute-start | bytes 1572872 | tf_op jit(solution)/shard_map/ppermute | solution.py:355
  88.3 8.4 %collective-permute-start.17 = (f32[2,128,16,128]{3,2,1,0:T(8,128)S(1)}, f32[2,128,16,128]{3,2,1,0:T(8,128)S(1)}, u32[]{:S(2)}, u32[]{:S(2)}) collective-permute-start(f32[2,128,16,128]{3,2,1,0:T(8,128)S(1)} %pad_maximum_fusion.2), channel_id=1, source_target_pairs={{0,16},{16,0},{1,17},{17,1},{2,18},{18,2},{3,19},{19,3},{4,20},{20... | collective-permute-start | bytes 6291464 | tf_op jit(solution)/shard_map/ppermute | solution.py:328
  88.3 15.2 %collective-permute-start.18 = (f32[8,128,128]{2,1,0:T(8,128)S(1)}, f32[8,128,128]{2,1,0:T(8,128)S(1)}, u32[]{:S(2)}, u32[]{:S(2)}) collective-permute-start(f32[8,128,128]{2,1,0:T(8,128)S(1)} %get-tuple-element.50), channel_id=1, source_target_pairs={{0,1},{1,2},{2,3},{3,0},{4,5},{5,6},{6,7},{7,4},{8,9},{9,10},{10,1... | collective-permute-start | bytes 1572872 | tf_op jit(solution)/shard_map/ppermute | solution.py:354
  89.0 4.9 %collective-permute-start.16 = (f32[8,16,128]{2,1,0:T(8,128)S(1)}, f32[8,16,128]{2,1,0:T(8,128)S(1)}, u32[]{:S(2)}, u32[]{:S(2)}) collective-permute-start(f32[8,16,128]{2,1,0:T(8,128)S(1)} %get-tuple-element.74), channel_id=1, source_target_pairs={{4,0},{8,4},{12,8},{0,12},{5,1},{9,5},{13,9},{1,13},{6,2},{10,6},{... | collective-permute-start | bytes 196616 | tf_op jit(solution)/shard_map/ppermute | solution.py:334
  91.5 5.2 %collective-permute-start.15 = (f32[8,16,128]{2,1,0:T(8,128)S(1)}, f32[8,16,128]{2,1,0:T(8,128)S(1)}, u32[]{:S(2)}, u32[]{:S(2)}) collective-permute-start(f32[8,16,128]{2,1,0:T(8,128)S(1)} %get-tuple-element.75), channel_id=1, source_target_pairs={{0,4},{4,8},{8,12},{12,0},{1,5},{5,9},{9,13},{13,1},{2,6},{6,10},{... | collective-permute-start | bytes 196616 | tf_op jit(solution)/shard_map/ppermute | solution.py:333
  91.5 41.1 %collective-permute-start.22 = (f32[8,128,128]{2,1,0:T(8,128)S(1)}, f32[8,128,128]{2,1,0:T(8,128)S(1)}, u32[]{:S(2)}, u32[]{:S(2)}) collective-permute-start(f32[8,128,128]{2,1,0:T(8,128)S(1)} %get-tuple-element.49), channel_id=1, source_target_pairs={{1,0},{2,1},{3,2},{0,3},{5,4},{6,5},{7,6},{4,7},{9,8},{10,9},{11,1... | collective-permute-start | bytes 1572872 | tf_op jit(solution)/shard_map/ppermute | solution.py:355
  103.9 2.7 %collective-permute-start.29 = (f32[2,128,128]{2,1,0:T(8,128)S(1)}, f32[2,128,128]{2,1,0:T(8,128)S(1)}, u32[]{:S(2)}, u32[]{:S(2)}) collective-permute-start(f32[2,128,128]{2,1,0:T(8,128)S(1)} %get-tuple-element.85), channel_id=1, source_target_pairs={{0,1},{4,5},{8,9},{12,13},{16,17},{20,21},{24,25},{28,29}} | collective-permute-start | bytes 393224 | tf_op jit(solution)/shard_map/ppermute | solution.py:378
  104.5 3.4 %collective-permute-start.26 = (f32[2,128,128]{2,1,0:T(8,128)S(1)}, f32[2,128,128]{2,1,0:T(8,128)S(1)}, u32[]{:S(2)}, u32[]{:S(2)}) collective-permute-start(f32[2,128,128]{2,1,0:T(8,128)S(1)} %get-tuple-element.86), channel_id=1, source_target_pairs={{0,1},{4,5},{8,9},{12,13},{16,17},{20,21},{24,25},{28,29}} | collective-permute-start | bytes 393224 | tf_op jit(solution)/shard_map/ppermute | solution.py:378
  105.2 4.0 %collective-permute-start.23 = (f32[2,128,128]{2,1,0:T(8,128)S(1)}, f32[2,128,128]{2,1,0:T(8,128)S(1)}, u32[]{:S(2)}, u32[]{:S(2)}) collective-permute-start(f32[2,128,128]{2,1,0:T(8,128)S(1)} %get-tuple-element.87), channel_id=1, source_target_pairs={{0,1},{4,5},{8,9},{12,13},{16,17},{20,21},{24,25},{28,29}} | collective-permute-start | bytes 393224 | tf_op jit(solution)/shard_map/ppermute | solution.py:378
  105.9 4.7 %collective-permute-start.19 = (f32[2,128,128]{2,1,0:T(8,128)S(1)}, f32[2,128,128]{2,1,0:T(8,128)S(1)}, u32[]{:S(2)}, u32[]{:S(2)}) collective-permute-start(f32[2,128,128]{2,1,0:T(8,128)S(1)} %get-tuple-element.88), channel_id=1, source_target_pairs={{0,1},{4,5},{8,9},{12,13},{16,17},{20,21},{24,25},{28,29}} | collective-permute-start | bytes 393224 | tf_op jit(solution)/shard_map/ppermute | solution.py:378
  106.6 16.5 %collective-permute-start.30 = (f32[2,128,128]{2,1,0:T(8,128)S(1)}, f32[2,128,128]{2,1,0:T(8,128)S(1)}, u32[]{:S(2)}, u32[]{:S(2)}) collective-permute-start(f32[2,128,128]{2,1,0:T(8,128)S(1)} %get-tuple-element.66), channel_id=1, source_target_pairs={{1,2},{5,6},{9,10},{13,14},{17,18},{21,22},{25,26},{29,30}} | collective-permute-start | bytes 393224 | tf_op jit(solution)/shard_map/ppermute | solution.py:378
  108.0 18.0 %collective-permute-start.27 = (f32[2,128,128]{2,1,0:T(8,128)S(1)}, f32[2,128,128]{2,1,0:T(8,128)S(1)}, u32[]{:S(2)}, u32[]{:S(2)}) collective-permute-start(f32[2,128,128]{2,1,0:T(8,128)S(1)} %get-tuple-element.62), channel_id=1, source_target_pairs={{1,2},{5,6},{9,10},{13,14},{17,18},{21,22},{25,26},{29,30}} | collective-permute-start | bytes 393224 | tf_op jit(solution)/shard_map/ppermute | solution.py:378
  109.3 19.4 %collective-permute-start.24 = (f32[2,128,128]{2,1,0:T(8,128)S(1)}, f32[2,128,128]{2,1,0:T(8,128)S(1)}, u32[]{:S(2)}, u32[]{:S(2)}) collective-permute-start(f32[2,128,128]{2,1,0:T(8,128)S(1)} %get-tuple-element.58), channel_id=1, source_target_pairs={{1,2},{5,6},{9,10},{13,14},{17,18},{21,22},{25,26},{29,30}} | collective-permute-start | bytes 393224 | tf_op jit(solution)/shard_map/ppermute | solution.py:378
  110.6 20.7 %collective-permute-start.20 = (f32[2,128,128]{2,1,0:T(8,128)S(1)}, f32[2,128,128]{2,1,0:T(8,128)S(1)}, u32[]{:S(2)}, u32[]{:S(2)}) collective-permute-start(f32[2,128,128]{2,1,0:T(8,128)S(1)} %get-tuple-element.54), channel_id=1, source_target_pairs={{1,2},{5,6},{9,10},{13,14},{17,18},{21,22},{25,26},{29,30}} | collective-permute-start | bytes 393224 | tf_op jit(solution)/shard_map/ppermute | solution.py:378
  123.1 16.3 %collective-permute-start.31 = (f32[2,128,128]{2,1,0:T(8,128)S(1)}, f32[2,128,128]{2,1,0:T(8,128)S(1)}, u32[]{:S(2)}, u32[]{:S(2)}) collective-permute-start(f32[2,128,128]{2,1,0:T(8,128)S(1)} %get-tuple-element.68), channel_id=1, source_target_pairs={{2,3},{6,7},{10,11},{14,15},{18,19},{22,23},{26,27},{30,31}} | collective-permute-start | bytes 393224 | tf_op jit(solution)/shard_map/ppermute | solution.py:378
  125.9 15.0 %collective-permute-start.28 = (f32[2,128,128]{2,1,0:T(8,128)S(1)}, f32[2,128,128]{2,1,0:T(8,128)S(1)}, u32[]{:S(2)}, u32[]{:S(2)}) collective-permute-start(f32[2,128,128]{2,1,0:T(8,128)S(1)} %get-tuple-element.64), channel_id=1, source_target_pairs={{2,3},{6,7},{10,11},{14,15},{18,19},{22,23},{26,27},{30,31}} | collective-permute-start | bytes 393224 | tf_op jit(solution)/shard_map/ppermute | solution.py:378
  128.8 13.6 %collective-permute-start.25 = (f32[2,128,128]{2,1,0:T(8,128)S(1)}, f32[2,128,128]{2,1,0:T(8,128)S(1)}, u32[]{:S(2)}, u32[]{:S(2)}) collective-permute-start(f32[2,128,128]{2,1,0:T(8,128)S(1)} %get-tuple-element.60), channel_id=1, source_target_pairs={{2,3},{6,7},{10,11},{14,15},{18,19},{22,23},{26,27},{30,31}} | collective-permute-start | bytes 393224 | tf_op jit(solution)/shard_map/ppermute | solution.py:378
  131.3 12.5 %collective-permute-start.21 = (f32[2,128,128]{2,1,0:T(8,128)S(1)}, f32[2,128,128]{2,1,0:T(8,128)S(1)}, u32[]{:S(2)}, u32[]{:S(2)}) collective-permute-start(f32[2,128,128]{2,1,0:T(8,128)S(1)} %get-tuple-element.56), channel_id=1, source_target_pairs={{2,3},{6,7},{10,11},{14,15},{18,19},{22,23},{26,27},{30,31}} | collective-permute-start | bytes 393224 | tf_op jit(solution)/shard_map/ppermute | solution.py:378

commit v4 on v3

--- a/solution.py
+++ b/solution.py
@@ -15,7 +15,7 @@
 
 CHUNKS = 8
 GRANT = 40
-SLOTS = 4
+SLOTS = 8
 VMEM = pl.BlockSpec(memory_space=pltpu.VMEM)
 HBM = pl.BlockSpec(memory_space=pltpu.HBM)
 
@@ -39,28 +39,27 @@
     return jnp.where(layer == depth - 1, jnp.expand_dims(high, -2), cells)
 
 
-def layers_kernel(f_ref, low_ref, high_ref, sems):
-    rows, _, depth, _ = f_ref.shape
+def layer_kernel(layer, f_ref, face_ref, sems):
+    rows = f_ref.shape[0]
     copies = []
-    for side, (layer, face_ref) in enumerate(((0, low_ref), (depth - 1, high_ref))):
-        for row in range(rows):
-            copies.append(pltpu.make_async_copy(f_ref.at[row, :, layer], face_ref.at[row], sems.at[side, row]))
-            copies[-1].start()
+    for row in range(rows):
+        copies.append(pltpu.make_async_copy(f_ref.at[row, :, layer], face_ref.at[row], sems.at[row]))
+        copies[-1].start()
     for copy in copies:
         copy.wait()
 
 
-def layers(field):
+def z_layer(field, layer):
     rows, span, _, lanes = field.shape
     return pl.pallas_call(
-        layers_kernel,
+        functools.partial(layer_kernel, layer),
         in_specs=[HBM],
-        out_specs=[VMEM] * 2,
-        out_shape=[like((rows, span, lanes), field)] * 2,
-        scratch_shapes=[pltpu.SemaphoreType.DMA((2, rows))],
+        out_specs=VMEM,
+        out_shape=like((rows, span, lanes), field),
+        scratch_shapes=[pltpu.SemaphoreType.DMA((rows,))],
         compiler_params=pltpu.CompilerParams(vmem_limit_bytes=50 * MIB),
         cost_estimate=pl.CostEstimate(flops=field.size, bytes_accessed=field.size, transcendentals=0),
-        name="layers",
+        name="layer",
     )(field)
 
 
@@ -225,19 +224,22 @@
         if k >= SLOTS:
             copy(k - SLOTS).wait()
 
-        def one(step, _):
-            at = step + k * chunk
+        def one(group, _):
+            start = pl.multiple_of(group * TILE, TILE)
+            some = pl.ds(pl.multiple_of(start + k * chunk, TILE), TILE)
             for row in range(rows):
-                for t in range(tiles):
-                    cells = h_ref[row, at, pl.ds(t * TILE, TILE), :]
-                    if t == 0:
-                        cells = cells + jnp.where(sub == 0, low_ref[row, pl.ds(at, 1), :], 0.0)
-                    if t == tiles - 1:
-                        cells = cells + jnp.where(sub == TILE - 1, high_ref[row, pl.ds(at, 1), :], 0.0)
-                    stage[k % SLOTS, row, step, pl.ds(t * TILE, TILE), :] = cells
+                low, high = low_ref[row, some, :], high_ref[row, some, :]
+                for j in range(TILE):
+                    for t in range(tiles):
+                        cells = h_ref[row, k * chunk + start + j, pl.ds(t * TILE, TILE), :]
+                        if t == 0:
+                            cells = cells + jnp.where(sub == 0, low[j : j + 1], 0.0)
+                        if t == tiles - 1:
+                            cells = cells + jnp.where(sub == TILE - 1, high[j : j + 1], 0.0)
+                        stage[k % SLOTS, row, start + j, pl.ds(t * TILE, TILE), :] = cells
             return 0
 
-        lax.fori_loop(0, chunk, one, 0, unroll=2)
+        lax.fori_loop(0, chunk // TILE, one, 0)
         copy(k).start()
     for k in range(CHUNKS - SLOTS, CHUNKS):
         copy(k).wait()
@@ -251,7 +253,7 @@
         out_specs=HBM,
         out_shape=like(h.shape, h),
         scratch_shapes=[pltpu.VMEM((SLOTS, rows, span // CHUNKS, depth, lanes), h.dtype), pltpu.SemaphoreType.DMA((CHUNKS,))],
-        compiler_params=pltpu.CompilerParams(vmem_limit_bytes=8 * MIB),
+        compiler_params=pltpu.CompilerParams(vmem_limit_bytes=11 * MIB),
         cost_estimate=pl.CostEstimate(flops=2 * h.size, bytes_accessed=8 * h.size, transcendentals=0),
         name="ending",
     )(h, low, high)
@@ -283,21 +285,27 @@
     pot_ref, stage, sems = refs[-3:]
     rows, span, depth, lanes = stage.shape
     chunk = span // CHUNKS
-    layer = lax.broadcasted_iota(jnp.int32, (depth, lanes), 0)
-
-    def one(at, _):
+    final = lax.broadcasted_iota(jnp.int32, (TILE, lanes), 0) == TILE - 1
+    tiles = depth // TILE
+
+    def one(group, _):
+        start = pl.multiple_of(group * TILE, TILE)
+        some = pl.ds(start, TILE)
         for row in range(rows):
-            base = got_ref[row, pl.ds(at, 1), :]
-            base = base if prior_ref is None else base + prior_ref[row, pl.ds(at, 1), :]
-            base = base + rest_ref[row + offset, pl.ds(at, 1), :]
-            high = high_ref[row + offset, pl.ds(at, 1), :]
-            cells = sum_ref[row + offset, at] + base
-            stage[row, at] = (cells + jnp.where(layer == depth - 1, high, 0.0)) * scale
+            base = got_ref[row, some, :] + rest_ref[row + offset, some, :]
+            base = base if prior_ref is None else base + prior_ref[row, some, :]
+            high = high_ref[row + offset, some, :]
+            for j in range(TILE):
+                for t in range(tiles):
+                    cells = sum_ref[row + offset, start + j, pl.ds(t * TILE, TILE), :] + base[j : j + 1]
+                    if t == tiles - 1:
+                        cells = cells + jnp.where(final, high[j : j + 1], 0.0)
+                    stage[row, start + j, pl.ds(t * TILE, TILE), :] = cells * scale
         return 0
 
     copies = []
     for k in range(CHUNKS):
-        lax.fori_loop(k * chunk, (k + 1) * chunk, one, 0, unroll=4)
+        lax.fori_loop(k * chunk // TILE, (k + 1) * chunk // TILE, one, 0)
         part = pl.ds(k * chunk, chunk)
         copies.append(pltpu.make_async_copy(stage.at[:, part], pot_ref.at[pl.ds(offset, rows), part], sems.at[k]))
         copies[-1].start()
@@ -347,7 +355,8 @@
     depth = field.shape[2]
     faces = None
     h, both, first, final, ground = peel(field)
-    low, high = layers(field)
+    high = z_layer(field, depth - 1)
+    low = z_layer(field, 0)
     raw_low, raw_high = low, high
     for step in range(STEPS):
         last = step == STEPS - 1

time: 146 us -> 145 us (level)
  waiting for transfers between devices: 60.2 us -> 55.9 us
  local copies, waits for them, and re-layouts: 6.93 us -> 10.3 us
    ppermute x4, waiting for transfers between devices: 20 us -> 15.4 us  [steps(): above = lax.ppermute(raw_low, 'lev', downs(levs))]
    unnamed x6 -> x10, local copies, waits for them, and re-layouts: 6.77 us -> 10.2 us
  transfers between devices with their start and end apart: 32 -> 32, of which waited for: 15 -> 15; matrix products, arithmetic and copies ran while one was open for 1% -> 1% of each run, Pallas kernels for 25% -> 26%
where the time goes in v4:
time: 145 us
  waiting for transfers between devices  55.9 us (39%)
  Pallas kernels  42.5 us (29%)
  starting transfers between devices  32.2 us (22%)
  local copies, waits for them, and re-layouts  10.3 us (7%)
  other arithmetic  2.77 us (2%)
    pallas_call x4, Pallas kernels, march(): pl.pallas_call(functools.partial(march_kernel, faces is not None, last, y...  24.1 us
    ppermute x4, waiting for transfers between devices, steps(): above = lax.ppermute(raw_low, 'lev', downs(levs))  15.4 us
    ppermute x12, waiting for transfers between devices, steps(): gots[part] = lax.ppermute(nexts[part], 'lev', [(hop, hop + 1)])  15.4 us
    ppermute x12, starting transfers between devices, steps(): gots[part] = lax.ppermute(nexts[part], 'lev', [(hop, hop + 1)])  13 us
    ppermute x4, waiting for transfers between devices, side_halos(): xlow = lax.ppermute(final, 'lon', ups(lons))  11 us
    unnamed x10, local copies, waits for them, and re-layouts  10.2 us
    ppermute x4, starting transfers between devices, side_halos(): xhigh = lax.ppermute(first, 'lon', downs(lons))  8.93 us
    ppermute x4, waiting for transfers between devices, steps(): below = lax.ppermute(raw_high, 'lev', ups(levs))  8.79 us
  transfers between devices with their start and end apart: 32, of which 15 were waited for; matrix products, arithmetic and copies ran while one was open for 1% of the time, Pallas kernels for 26%

profile of v4, /device:TPU:16, one launch (start us, length us, event | category | flops | bytes accessed | tf_op | source)
XLA Modules:
  0.0 144.9 jit_solution(2902228138601245973)
XLA Ops:
  0.6 3.5 %peel.1 = (f32[8,128,16,128]{3,2,1,0:T(8,128)S(1)}, f32[2,128,16,128]{3,2,1,0:T(8,128)S(1)}, f32[8,16,128]{2,1,0:T(8,128)S(1)}, f32[8,16,128]{2,1,0:T(8,128)S(1)}, f32[1,1,128]{2,1,0:T(1,128)S(1)}) custom-call(f32[8,128,16,128]{3,2,1,0:T(8,128)} %f_ref.5), custom_call_target="tpu_custom_call" | custom-call | flops 8388608 | bytes 2097152 | tf_op jit(solution)/shard_map/peel/pallas_call | solution.py:92
  4.2 1.2 layer.3
  5.4 0.5 collective-permute-start.4
  5.9 1.2 layer.2
  7.1 1.6 %collective-permute-start.3 = (f32[8,128,128]{2,1,0:T(8,128)S(1)}, f32[8,128,128]{2,1,0:T(8,128)S(1)}, u32[]{:S(2)}, u32[]{:S(2)}) collective-permute-start(f32[8,128,128]{2,1,0:T(8,128)S(1)} %layer.2), channel_id=1, source_target_pairs={{0,1},{1,2},{2,3},{3,0},{4,5},{5,6},{6,7},{7,4},{8,9},{9,10},{10,1... | collective-permute-start | bytes 1572872 | tf_op jit(solution)/shard_map/ppermute | solution.py:363
  8.7 1.5 %collective-permute-start = (f32[8,16,128]{2,1,0:T(8,128)S(1)}, f32[8,16,128]{2,1,0:T(8,128)S(1)}, u32[]{:S(2)}, u32[]{:S(2)}) collective-permute-start(f32[8,16,128]{2,1,0:T(8,128)S(1)} %get-tuple-element.35), channel_id=1, source_target_pairs={{0,4},{4,8},{8,12},{12,0},{1,5},{5,9},{9,13},{13,1},{2,6},{6,10},{... | collective-permute-start | bytes 196616 | tf_op jit(solution)/shard_map/ppermute | solution.py:341
  10.2 1.4 collective-permute-start.1
  11.7 2.7 %collective-permute-done.refs_1_ = f32[8,16,128]{2,1,0:T(8,128)S(1)} collective-permute-done((f32[8,16,128]{2,1,0:T(8,128)S(1)}, f32[8,16,128]{2,1,0:T(8,128)S(1)}, u32[]{:S(2)}, u32[]{:S(2)}) %collective-permute-start) | collective-permute-done | bytes 65568 | tf_op jit(solution)/shard_map/ppermute | solution.py:341
  14.4 0.7 collective-permute-done.1.refs_2_
  15.0 3.4 %copy-done = f32[8,128,16,128]{3,2,1,0:T(8,128)S(1)} copy-done((f32[8,128,16,128]{3,2,1,0:T(8,128)S(1)}, f32[8,128,16,128]{3,2,1,0:T(8,128)}, u32[]{:S(2)}) %copy-start) | copy-done | bytes 8388632
  18.4 5.1 %march.4 = (f32[8,128,16,128]{3,2,1,0:T(8,128)S(1)}, f32[8,128,128]{2,1,0:T(8,128)S(1)}, f32[8,128,128]{2,1,0:T(8,128)S(1)}) custom-call(f32[8,128,16,128]{3,2,1,0:T(8,128)S(1)} %get-tuple-element.34.refs_0_, f32[8,16,128]{2,1,0:T(8,128)S(1)} %collective-permute-done.refs_1_, ...), custom_call_target="tpu_custom_call", output_to_operand_aliasing={{0}: (0, {})} | custom-call | flops 33554432 | bytes 25165824 | tf_op jit(solution)/shard_map/march/pallas_call | solution.py:169
  23.7 8.8 %collective-permute-done.3 = f32[8,128,128]{2,1,0:T(8,128)S(1)} collective-permute-done((f32[8,128,128]{2,1,0:T(8,128)S(1)}, f32[8,128,128]{2,1,0:T(8,128)S(1)}, u32[]{:S(2)}, u32[]{:S(2)}) %collective-permute-start.3) | collective-permute-done | bytes 524320 | tf_op jit(solution)/shard_map/ppermute | solution.py:363
  32.5 0.4 select_select_fusion.5
  32.9 0.1 pad_maximum_fusion
  33.2 1.6 %collective-permute-start.8 = (f32[8,128,128]{2,1,0:T(8,128)S(1)}, f32[8,128,128]{2,1,0:T(8,128)S(1)}, u32[]{:S(2)}, u32[]{:S(2)}) collective-permute-start(f32[8,128,128]{2,1,0:T(8,128)S(1)} %get-tuple-element.40), channel_id=1, source_target_pairs={{0,1},{1,2},{2,3},{3,0},{4,5},{5,6},{6,7},{7,4},{8,9},{9,10},{10,1... | collective-permute-start | bytes 1572872 | tf_op jit(solution)/shard_map/ppermute | solution.py:363
  34.9 2.5 %collective-permute-start.6 = (f32[8,16,128]{2,1,0:T(8,128)S(1)}, f32[8,16,128]{2,1,0:T(8,128)S(1)}, u32[]{:S(2)}, u32[]{:S(2)}) collective-permute-start(f32[8,16,128]{2,1,0:T(8,128)S(1)} %get-tuple-element.78), channel_id=1, source_target_pairs={{4,0},{8,4},{12,8},{0,12},{5,1},{9,5},{13,9},{1,13},{6,2},{10,6},{... | collective-permute-start | bytes 196616 | tf_op jit(solution)/shard_map/ppermute | solution.py:342
  37.4 0.4 collective-permute-start.9
  37.9 1.9 %collective-permute-done.6.refs_4_ = f32[8,16,128]{2,1,0:T(8,128)S(1)} collective-permute-done((f32[8,16,128]{2,1,0:T(8,128)S(1)}, f32[8,16,128]{2,1,0:T(8,128)S(1)}, u32[]{:S(2)}, u32[]{:S(2)}) %collective-permute-start.6) | collective-permute-done | bytes 65568 | tf_op jit(solution)/shard_map/ppermute | solution.py:342
  39.8 2.8 %collective-permute-done.5.refs_3_ = f32[8,16,128]{2,1,0:T(8,128)S(1)} collective-permute-done((f32[8,16,128]{2,1,0:T(8,128)S(1)}, f32[8,16,128]{2,1,0:T(8,128)S(1)}, u32[]{:S(2)}, u32[]{:S(2)}) %collective-permute-start.5) | collective-permute-done | bytes 65568 | tf_op jit(solution)/shard_map/ppermute | solution.py:341
  42.6 3.4 %copy-done.1 = f32[8,128,16,128]{3,2,1,0:T(8,128)S(1)} copy-done((f32[8,128,16,128]{3,2,1,0:T(8,128)S(1)}, f32[8,128,16,128]{3,2,1,0:T(8,128)}, u32[]{:S(2)}) %copy-start.1) | copy-done | bytes 8388632
  46.0 6.0 %march.5 = (f32[8,128,16,128]{3,2,1,0:T(8,128)S(1)}, f32[8,128,128]{2,1,0:T(8,128)S(1)}, f32[8,128,128]{2,1,0:T(8,128)S(1)}) custom-call(f32[8,128,16,128]{3,2,1,0:T(8,128)S(1)} %get-tuple-element.38.refs_0_, f32[8,128,128]{2,1,0:T(8,128)S(1)} %multiply_add_fusion.6.refs_1_, ...), custom_call_target="tpu_custom_call", output_to_operand_aliasing={{0}: (0, {})} | custom-call | flops 33554432 | bytes 25165824 | tf_op jit(solution)/shard_map/march/pallas_call | solution.py:169
  52.1 7.0 %collective-permute-done.9 = f32[8,128,128]{2,1,0:T(8,128)S(1)} collective-permute-done((f32[8,128,128]{2,1,0:T(8,128)S(1)}, f32[8,128,128]{2,1,0:T(8,128)S(1)}, u32[]{:S(2)}, u32[]{:S(2)}) %collective-permute-start.9) | collective-permute-done | bytes 524320 | tf_op jit(solution)/shard_map/ppermute | solution.py:364
  59.3 0.4 select_select_fusion.3
  59.7 0.1 pad_maximum_fusion.1
  59.9 1.6 %collective-permute-start.13 = (f32[8,128,128]{2,1,0:T(8,128)S(1)}, f32[8,128,128]{2,1,0:T(8,128)S(1)}, u32[]{:S(2)}, u32[]{:S(2)}) collective-permute-start(f32[8,128,128]{2,1,0:T(8,128)S(1)} %get-tuple-element.43), channel_id=1, source_target_pairs={{0,1},{1,2},{2,3},{3,0},{4,5},{5,6},{6,7},{7,4},{8,9},{9,10},{10,1... | collective-permute-start | bytes 1572872 | tf_op jit(solution)/shard_map/ppermute | solution.py:363
  61.6 2.5 %collective-permute-start.11 = (f32[8,16,128]{2,1,0:T(8,128)S(1)}, f32[8,16,128]{2,1,0:T(8,128)S(1)}, u32[]{:S(2)}, u32[]{:S(2)}) collective-permute-start(f32[8,16,128]{2,1,0:T(8,128)S(1)} %get-tuple-element.74), channel_id=1, source_target_pairs={{4,0},{8,4},{12,8},{0,12},{5,1},{9,5},{13,9},{1,13},{6,2},{10,6},{... | collective-permute-start | bytes 196616 | tf_op jit(solution)/shard_map/ppermute | solution.py:342
  64.1 0.4 collective-permute-start.14
  64.6 1.9 %collective-permute-done.11.refs_4_ = f32[8,16,128]{2,1,0:T(8,128)S(1)} collective-permute-done((f32[8,16,128]{2,1,0:T(8,128)S(1)}, f32[8,16,128]{2,1,0:T(8,128)S(1)}, u32[]{:S(2)}, u32[]{:S(2)}) %collective-permute-start.11) | collective-permute-done | bytes 65568 | tf_op jit(solution)/shard_map/ppermute | solution.py:342
  66.5 2.8 %collective-permute-done.10.refs_3_ = f32[8,16,128]{2,1,0:T(8,128)S(1)} collective-permute-done((f32[8,16,128]{2,1,0:T(8,128)S(1)}, f32[8,16,128]{2,1,0:T(8,128)S(1)}, u32[]{:S(2)}, u32[]{:S(2)}) %collective-permute-start.10) | collective-permute-done | bytes 65568 | tf_op jit(solution)/shard_map/ppermute | solution.py:341
  69.3 3.4 %copy-done.2 = f32[8,128,16,128]{3,2,1,0:T(8,128)S(1)} copy-done((f32[8,128,16,128]{3,2,1,0:T(8,128)S(1)}, f32[8,128,16,128]{3,2,1,0:T(8,128)}, u32[]{:S(2)}) %copy-start.2) | copy-done | bytes 8388632
  72.7 6.0 %march.6 = (f32[8,128,16,128]{3,2,1,0:T(8,128)S(1)}, f32[8,128,128]{2,1,0:T(8,128)S(1)}, f32[8,128,128]{2,1,0:T(8,128)S(1)}) custom-call(f32[8,128,16,128]{3,2,1,0:T(8,128)S(1)} %get-tuple-element.41.refs_0_, f32[8,128,128]{2,1,0:T(8,128)S(1)} %multiply_add_fusion.4.refs_1_, ...), custom_call_target="tpu_custom_call", output_to_operand_aliasing={{0}: (0, {})} | custom-call | flops 33554432 | bytes 25165824 | tf_op jit(solution)/shard_map/march/pallas_call | solution.py:169
  78.9 8.4 %collective-permute-done.14 = f32[8,128,128]{2,1,0:T(8,128)S(1)} collective-permute-done((f32[8,128,128]{2,1,0:T(8,128)S(1)}, f32[8,128,128]{2,1,0:T(8,128)S(1)}, u32[]{:S(2)}, u32[]{:S(2)}) %collective-permute-start.14) | collective-permute-done | bytes 524320 | tf_op jit(solution)/shard_map/ppermute | solution.py:364
  87.3 0.1 multiply_add_fusion.1.refs_2_
  87.4 0.4 select_select_fusion.1
  87.8 0.1 pad_maximum_fusion.2
  88.0 0.6 collective-permute-start.18
  88.7 2.5 %collective-permute-start.16 = (f32[8,16,128]{2,1,0:T(8,128)S(1)}, f32[8,16,128]{2,1,0:T(8,128)S(1)}, u32[]{:S(2)}, u32[]{:S(2)}) collective-permute-start(f32[8,16,128]{2,1,0:T(8,128)S(1)} %get-tuple-element.70), channel_id=1, source_target_pairs={{4,0},{8,4},{12,8},{0,12},{5,1},{9,5},{13,9},{1,13},{6,2},{10,6},{... | collective-permute-start | bytes 196616 | tf_op jit(solution)/shard_map/ppermute | solution.py:342
  91.2 1.6 %collective-permute-start.22 = (f32[8,128,128]{2,1,0:T(8,128)S(1)}, f32[8,128,128]{2,1,0:T(8,128)S(1)}, u32[]{:S(2)}, u32[]{:S(2)}) collective-permute-start(f32[8,128,128]{2,1,0:T(8,128)S(1)} %get-tuple-element.45), channel_id=1, source_target_pairs={{1,0},{2,1},{3,2},{0,3},{5,4},{6,5},{7,6},{4,7},{9,8},{10,9},{11,1... | collective-permute-start | bytes 1572872 | tf_op jit(solution)/shard_map/ppermute | solution.py:364
  92.8 0.8 collective-permute-done.16.refs_4_
  93.6 2.8 %collective-permute-done.15.refs_3_ = f32[8,16,128]{2,1,0:T(8,128)S(1)} collective-permute-done((f32[8,16,128]{2,1,0:T(8,128)S(1)}, f32[8,16,128]{2,1,0:T(8,128)S(1)}, u32[]{:S(2)}, u32[]{:S(2)}) %collective-permute-start.15) | collective-permute-done | bytes 65568 | tf_op jit(solution)/shard_map/ppermute | solution.py:341
  96.4 6.9 %march.7 = (f32[8,128,16,128]{3,2,1,0:T(8,128)S(1)}, f32[8,128,128]{2,1,0:T(8,128)S(1)}) custom-call(f32[8,128,16,128]{3,2,1,0:T(8,128)S(1)} %get-tuple-element.44.refs_0_, f32[8,128,128]{2,1,0:T(8,128)S(1)} %multiply_add_fusion.2.refs_1_, f32[8,128,128]{2,1,0:T(8,128)S(1)} %multiply_add_fusion.1.refs_2_, ...), custom_call_target="tpu_custom_call", output_to_operand_aliasing={{0}: (0, {})} | custom-call | flops 33554432 | bytes 25165824 | tf_op jit(solution)/shard_map/march/pallas_call | solution.py:169
  103.3 0.2 add_add_fusion
  103.6 0.7 collective-permute-start.29
  104.3 0.7 collective-permute-start.26
  104.9 0.7 collective-permute-start.23
  105.6 0.7 collective-permute-start.19
  106.3 1.3 collective-permute-start.30
  107.7 1.3 collective-permute-start.27
  109.0 1.3 collective-permute-start.24
  110.4 1.3 collective-permute-start.20
  111.7 11.1 %collective-permute-done.30.got_ref = f32[2,128,128]{2,1,0:T(8,128)S(1)} collective-permute-done((f32[2,128,128]{2,1,0:T(8,128)S(1)}, f32[2,128,128]{2,1,0:T(8,128)S(1)}, u32[]{:S(2)}, u32[]{:S(2)}) %collective-permute-start.30) | collective-permute-done | bytes 131104 | tf_op jit(solution)/shard_map/ppermute | solution.py:387
  122.8 1.3 collective-permute-start.31
  124.1 1.5 %collective-permute-done.27.got_ref = f32[2,128,128]{2,1,0:T(8,128)S(1)} collective-permute-done((f32[2,128,128]{2,1,0:T(8,128)S(1)}, f32[2,128,128]{2,1,0:T(8,128)S(1)}, u32[]{:S(2)}, u32[]{:S(2)}) %collective-permute-start.27) | collective-permute-done | bytes 131104 | tf_op jit(solution)/shard_map/ppermute | solution.py:387
  125.6 1.3 collective-permute-start.28
  126.9 1.5 %collective-permute-done.24.got_ref = f32[2,128,128]{2,1,0:T(8,128)S(1)} collective-permute-done((f32[2,128,128]{2,1,0:T(8,128)S(1)}, f32[2,128,128]{2,1,0:T(8,128)S(1)}, u32[]{:S(2)}, u32[]{:S(2)}) %collective-permute-start.24) | collective-permute-done | bytes 131104 | tf_op jit(solution)/shard_map/ppermute | solution.py:387
  128.4 1.3 collective-permute-start.25
  129.7 1.3 collective-permute-done.20.got_ref
  131.0 1.3 collective-permute-start.21
  132.4 3.5 %ending.1 = f32[8,128,16,128]{3,2,1,0:T(8,128)} custom-call(f32[8,128,16,128]{3,2,1,0:T(8,128)S(1)} %get-tuple-element.47.h_ref, f32[8,128,128]{2,1,0:T(8,128)S(1)} %get-tuple-element.80.low_ref, f32[8,128,128]{2,1,0:T(8,128)S(1)} %add_multiply_fusion.high_ref), custom_call_target="tpu_custom_call" | custom-call | flops 4194304 | bytes 16777216 | tf_op jit(solution)/shard_map/ending/pallas_call | solution.py:250
  135.9 3.1 %sums.1.sum_ref = f32[8,128,16,128]{3,2,1,0:T(8,128)S(1)} custom-call(f32[8,128,16,128]{3,2,1,0:T(8,128)S(1)} %get-tuple-element.47.h_ref), custom_call_target="tpu_custom_call" | custom-call | flops 16777216 | bytes 16777216 | tf_op jit(solution)/shard_map/sums/pallas_call | solution.py:203
  139.1 1.4 potential.4.refs_1_
  140.5 1.4 potential.5.refs_1_
  142.0 1.4 potential.6.refs_1_
  143.4 1.4 potential.7
  (64 shorter events, 1.5 us)
Async XLA Ops:
  4.1 10.9 %collective-permute-start.2 = (f32[2,128,16,128]{3,2,1,0:T(8,128)S(1)}, f32[2,128,16,128]{3,2,1,0:T(8,128)S(1)}, u32[]{:S(2)}, u32[]{:S(2)}) collective-permute-start(f32[2,128,16,128]{3,2,1,0:T(8,128)S(1)} %get-tuple-element.37), channel_id=1, source_target_pairs={{0,16},{16,0},{1,17},{17,1},{2,18},{18,2},{3,19},{19,3},{4,20},{20... | collective-permute-start | bytes 6291464 | tf_op jit(solution)/shard_map/ppermute | solution.py:336
  5.4 18.1 %collective-permute-start.4 = (f32[8,128,128]{2,1,0:T(8,128)S(1)}, f32[8,128,128]{2,1,0:T(8,128)S(1)}, u32[]{:S(2)}, u32[]{:S(2)}) collective-permute-start(f32[8,128,128]{2,1,0:T(8,128)S(1)} %layer.3), channel_id=1, source_target_pairs={{1,0},{2,1},{3,2},{0,3},{5,4},{6,5},{7,6},{4,7},{9,8},{10,9},{11,1... | collective-permute-start | bytes 1572872 | tf_op jit(solution)/shard_map/ppermute | solution.py:364
  7.1 25.3 %collective-permute-start.3 = (f32[8,128,128]{2,1,0:T(8,128)S(1)}, f32[8,128,128]{2,1,0:T(8,128)S(1)}, u32[]{:S(2)}, u32[]{:S(2)}) collective-permute-start(f32[8,128,128]{2,1,0:T(8,128)S(1)} %layer.2), channel_id=1, source_target_pairs={{0,1},{1,2},{2,3},{3,0},{4,5},{5,6},{6,7},{7,4},{8,9},{9,10},{10,1... | collective-permute-start | bytes 1572872 | tf_op jit(solution)/shard_map/ppermute | solution.py:363
  8.7 5.6 %collective-permute-start = (f32[8,16,128]{2,1,0:T(8,128)S(1)}, f32[8,16,128]{2,1,0:T(8,128)S(1)}, u32[]{:S(2)}, u32[]{:S(2)}) collective-permute-start(f32[8,16,128]{2,1,0:T(8,128)S(1)} %get-tuple-element.35), channel_id=1, source_target_pairs={{0,4},{4,8},{8,12},{12,0},{1,5},{5,9},{9,13},{13,1},{2,6},{6,10},{... | collective-permute-start | bytes 196616 | tf_op jit(solution)/shard_map/ppermute | solution.py:341
  10.2 4.8 %collective-permute-start.1 = (f32[8,16,128]{2,1,0:T(8,128)S(1)}, f32[8,16,128]{2,1,0:T(8,128)S(1)}, u32[]{:S(2)}, u32[]{:S(2)}) collective-permute-start(f32[8,16,128]{2,1,0:T(8,128)S(1)} %get-tuple-element.36), channel_id=1, source_target_pairs={{4,0},{8,4},{12,8},{0,12},{5,1},{9,5},{13,9},{1,13},{6,2},{10,6},{... | collective-permute-start | bytes 196616 | tf_op jit(solution)/shard_map/ppermute | solution.py:342
  15.0 3.4 %copy-start = (f32[8,128,16,128]{3,2,1,0:T(8,128)S(1)}, f32[8,128,16,128]{3,2,1,0:T(8,128)}, u32[]{:S(2)}) copy-start(f32[8,128,16,128]{3,2,1,0:T(8,128)} %refs_7_.5) | copy-start | bytes 25165828
  32.4 63.9 %slice-start = ((s8[8388608]{0:T(1024)(128)(4,1)}), s8[4194304]{0:T(1024)(128)(4,1)S(1)}, s32[]{:S(2)}) async-start(s8[8388608]{0:T(1024)(128)(4,1)} %bitcast.74), calls=%async_computation | async-start | bytes 8388608
  33.1 9.5 %collective-permute-start.7 = (f32[2,128,16,128]{3,2,1,0:T(8,128)S(1)}, f32[2,128,16,128]{3,2,1,0:T(8,128)S(1)}, u32[]{:S(2)}, u32[]{:S(2)}) collective-permute-start(f32[2,128,16,128]{3,2,1,0:T(8,128)S(1)} %pad_maximum_fusion), channel_id=1, source_target_pairs={{0,16},{16,0},{1,17},{17,1},{2,18},{18,2},{3,19},{19,3},{4,20},{20... | collective-permute-start | bytes 6291464 | tf_op jit(solution)/shard_map/ppermute | solution.py:336
  33.2 18.8 %collective-permute-start.8 = (f32[8,128,128]{2,1,0:T(8,128)S(1)}, f32[8,128,128]{2,1,0:T(8,128)S(1)}, u32[]{:S(2)}, u32[]{:S(2)}) collective-permute-start(f32[8,128,128]{2,1,0:T(8,128)S(1)} %get-tuple-element.40), channel_id=1, source_target_pairs={{0,1},{1,2},{2,3},{3,0},{4,5},{5,6},{6,7},{7,4},{8,9},{9,10},{10,1... | collective-permute-start | bytes 1572872 | tf_op jit(solution)/shard_map/ppermute | solution.py:363
  34.9 4.9 %collective-permute-start.6 = (f32[8,16,128]{2,1,0:T(8,128)S(1)}, f32[8,16,128]{2,1,0:T(8,128)S(1)}, u32[]{:S(2)}, u32[]{:S(2)}) collective-permute-start(f32[8,16,128]{2,1,0:T(8,128)S(1)} %get-tuple-element.78), channel_id=1, source_target_pairs={{4,0},{8,4},{12,8},{0,12},{5,1},{9,5},{13,9},{1,13},{6,2},{10,6},{... | collective-permute-start | bytes 196616 | tf_op jit(solution)/shard_map/ppermute | solution.py:342
  37.4 5.2 %collective-permute-start.5 = (f32[8,16,128]{2,1,0:T(8,128)S(1)}, f32[8,16,128]{2,1,0:T(8,128)S(1)}, u32[]{:S(2)}, u32[]{:S(2)}) collective-permute-start(f32[8,16,128]{2,1,0:T(8,128)S(1)} %get-tuple-element.79), channel_id=1, source_target_pairs={{0,4},{4,8},{8,12},{12,0},{1,5},{5,9},{9,13},{13,1},{2,6},{6,10},{... | collective-permute-start | bytes 196616 | tf_op jit(solution)/shard_map/ppermute | solution.py:341
  37.4 21.7 %collective-permute-start.9 = (f32[8,128,128]{2,1,0:T(8,128)S(1)}, f32[8,128,128]{2,1,0:T(8,128)S(1)}, u32[]{:S(2)}, u32[]{:S(2)}) collective-permute-start(f32[8,128,128]{2,1,0:T(8,128)S(1)} %get-tuple-element.39), channel_id=1, source_target_pairs={{1,0},{2,1},{3,2},{0,3},{5,4},{6,5},{7,6},{4,7},{9,8},{10,9},{11,1... | collective-permute-start | bytes 1572872 | tf_op jit(solution)/shard_map/ppermute | solution.py:364
  42.6 3.4 %copy-start.1 = (f32[8,128,16,128]{3,2,1,0:T(8,128)S(1)}, f32[8,128,16,128]{3,2,1,0:T(8,128)}, u32[]{:S(2)}) copy-start(f32[8,128,16,128]{3,2,1,0:T(8,128)} %refs_7_.5) | copy-start | bytes 25165828
  59.3 37.1 %slice-start.1 = ((s8[8388608]{0:T(1024)(128)(4,1)}), s8[4194304]{0:T(1024)(128)(4,1)S(1)}, s32[]{:S(2)}) async-start(s8[8388608]{0:T(1024)(128)(4,1)} %bitcast.74), calls=%async_computation.1 | async-start | bytes 8388608
  59.8 9.5 %collective-permute-start.12 = (f32[2,128,16,128]{3,2,1,0:T(8,128)S(1)}, f32[2,128,16,128]{3,2,1,0:T(8,128)S(1)}, u32[]{:S(2)}, u32[]{:S(2)}) collective-permute-start(f32[2,128,16,128]{3,2,1,0:T(8,128)S(1)} %pad_maximum_fusion.1), channel_id=1, source_target_pairs={{0,16},{16,0},{1,17},{17,1},{2,18},{18,2},{3,19},{19,3},{4,20},{20... | collective-permute-start | bytes 6291464 | tf_op jit(solution)/shard_map/ppermute | solution.py:336
  59.9 18.8 %collective-permute-start.13 = (f32[8,128,128]{2,1,0:T(8,128)S(1)}, f32[8,128,128]{2,1,0:T(8,128)S(1)}, u32[]{:S(2)}, u32[]{:S(2)}) collective-permute-start(f32[8,128,128]{2,1,0:T(8,128)S(1)} %get-tuple-element.43), channel_id=1, source_target_pairs={{0,1},{1,2},{2,3},{3,0},{4,5},{5,6},{6,7},{7,4},{8,9},{9,10},{10,1... | collective-permute-start | bytes 1572872 | tf_op jit(solution)/shard_map/ppermute | solution.py:363
  61.6 4.9 %collective-permute-start.11 = (f32[8,16,128]{2,1,0:T(8,128)S(1)}, f32[8,16,128]{2,1,0:T(8,128)S(1)}, u32[]{:S(2)}, u32[]{:S(2)}) collective-permute-start(f32[8,16,128]{2,1,0:T(8,128)S(1)} %get-tuple-element.74), channel_id=1, source_target_pairs={{4,0},{8,4},{12,8},{0,12},{5,1},{9,5},{13,9},{1,13},{6,2},{10,6},{... | collective-permute-start | bytes 196616 | tf_op jit(solution)/shard_map/ppermute | solution.py:342
  64.1 5.2 %collective-permute-start.10 = (f32[8,16,128]{2,1,0:T(8,128)S(1)}, f32[8,16,128]{2,1,0:T(8,128)S(1)}, u32[]{:S(2)}, u32[]{:S(2)}) collective-permute-start(f32[8,16,128]{2,1,0:T(8,128)S(1)} %get-tuple-element.75), channel_id=1, source_target_pairs={{0,4},{4,8},{8,12},{12,0},{1,5},{5,9},{9,13},{13,1},{2,6},{6,10},{... | collective-permute-start | bytes 196616 | tf_op jit(solution)/shard_map/ppermute | solution.py:341
  64.1 23.1 %collective-permute-start.14 = (f32[8,128,128]{2,1,0:T(8,128)S(1)}, f32[8,128,128]{2,1,0:T(8,128)S(1)}, u32[]{:S(2)}, u32[]{:S(2)}) collective-permute-start(f32[8,128,128]{2,1,0:T(8,128)S(1)} %get-tuple-element.42), channel_id=1, source_target_pairs={{1,0},{2,1},{3,2},{0,3},{5,4},{6,5},{7,6},{4,7},{9,8},{10,9},{11,1... | collective-permute-start | bytes 1572872 | tf_op jit(solution)/shard_map/ppermute | solution.py:364
  69.3 3.4 %copy-start.2 = (f32[8,128,16,128]{3,2,1,0:T(8,128)S(1)}, f32[8,128,16,128]{3,2,1,0:T(8,128)}, u32[]{:S(2)}) copy-start(f32[8,128,16,128]{3,2,1,0:T(8,128)} %refs_7_.5) | copy-start | bytes 25165828
  87.9 8.4 %collective-permute-start.17 = (f32[2,128,16,128]{3,2,1,0:T(8,128)S(1)}, f32[2,128,16,128]{3,2,1,0:T(8,128)S(1)}, u32[]{:S(2)}, u32[]{:S(2)}) collective-permute-start(f32[2,128,16,128]{3,2,1,0:T(8,128)S(1)} %pad_maximum_fusion.2), channel_id=1, source_target_pairs={{0,16},{16,0},{1,17},{17,1},{2,18},{18,2},{3,19},{19,3},{4,20},{20... | collective-permute-start | bytes 6291464 | tf_op jit(solution)/shard_map/ppermute | solution.py:336
  88.0 15.3 %collective-permute-start.18 = (f32[8,128,128]{2,1,0:T(8,128)S(1)}, f32[8,128,128]{2,1,0:T(8,128)S(1)}, u32[]{:S(2)}, u32[]{:S(2)}) collective-permute-start(f32[8,128,128]{2,1,0:T(8,128)S(1)} %get-tuple-element.46), channel_id=1, source_target_pairs={{0,1},{1,2},{2,3},{3,0},{4,5},{5,6},{6,7},{7,4},{8,9},{9,10},{10,1... | collective-permute-start | bytes 1572872 | tf_op jit(solution)/shard_map/ppermute | solution.py:363
  88.7 4.9 %collective-permute-start.16 = (f32[8,16,128]{2,1,0:T(8,128)S(1)}, f32[8,16,128]{2,1,0:T(8,128)S(1)}, u32[]{:S(2)}, u32[]{:S(2)}) collective-permute-start(f32[8,16,128]{2,1,0:T(8,128)S(1)} %get-tuple-element.70), channel_id=1, source_target_pairs={{4,0},{8,4},{12,8},{0,12},{5,1},{9,5},{13,9},{1,13},{6,2},{10,6},{... | collective-permute-start | bytes 196616 | tf_op jit(solution)/shard_map/ppermute | solution.py:342
  91.2 5.2 %collective-permute-start.15 = (f32[8,16,128]{2,1,0:T(8,128)S(1)}, f32[8,16,128]{2,1,0:T(8,128)S(1)}, u32[]{:S(2)}, u32[]{:S(2)}) collective-permute-start(f32[8,16,128]{2,1,0:T(8,128)S(1)} %get-tuple-element.71), channel_id=1, source_target_pairs={{0,4},{4,8},{8,12},{12,0},{1,5},{5,9},{9,13},{13,1},{2,6},{6,10},{... | collective-permute-start | bytes 196616 | tf_op jit(solution)/shard_map/ppermute | solution.py:341
  91.2 41.1 %collective-permute-start.22 = (f32[8,128,128]{2,1,0:T(8,128)S(1)}, f32[8,128,128]{2,1,0:T(8,128)S(1)}, u32[]{:S(2)}, u32[]{:S(2)}) collective-permute-start(f32[8,128,128]{2,1,0:T(8,128)S(1)} %get-tuple-element.45), channel_id=1, source_target_pairs={{1,0},{2,1},{3,2},{0,3},{5,4},{6,5},{7,6},{4,7},{9,8},{10,9},{11,1... | collective-permute-start | bytes 1572872 | tf_op jit(solution)/shard_map/ppermute | solution.py:364
  103.6 2.7 %collective-permute-start.29 = (f32[2,128,128]{2,1,0:T(8,128)S(1)}, f32[2,128,128]{2,1,0:T(8,128)S(1)}, u32[]{:S(2)}, u32[]{:S(2)}) collective-permute-start(f32[2,128,128]{2,1,0:T(8,128)S(1)} %get-tuple-element.81), channel_id=1, source_target_pairs={{0,1},{4,5},{8,9},{12,13},{16,17},{20,21},{24,25},{28,29}} | collective-permute-start | bytes 393224 | tf_op jit(solution)/shard_map/ppermute | solution.py:387
  104.3 3.4 %collective-permute-start.26 = (f32[2,128,128]{2,1,0:T(8,128)S(1)}, f32[2,128,128]{2,1,0:T(8,128)S(1)}, u32[]{:S(2)}, u32[]{:S(2)}) collective-permute-start(f32[2,128,128]{2,1,0:T(8,128)S(1)} %get-tuple-element.82), channel_id=1, source_target_pairs={{0,1},{4,5},{8,9},{12,13},{16,17},{20,21},{24,25},{28,29}} | collective-permute-start | bytes 393224 | tf_op jit(solution)/shard_map/ppermute | solution.py:387
  104.9 4.0 %collective-permute-start.23 = (f32[2,128,128]{2,1,0:T(8,128)S(1)}, f32[2,128,128]{2,1,0:T(8,128)S(1)}, u32[]{:S(2)}, u32[]{:S(2)}) collective-permute-start(f32[2,128,128]{2,1,0:T(8,128)S(1)} %get-tuple-element.83), channel_id=1, source_target_pairs={{0,1},{4,5},{8,9},{12,13},{16,17},{20,21},{24,25},{28,29}} | collective-permute-start | bytes 393224 | tf_op jit(solution)/shard_map/ppermute | solution.py:387
  105.6 4.7 %collective-permute-start.19 = (f32[2,128,128]{2,1,0:T(8,128)S(1)}, f32[2,128,128]{2,1,0:T(8,128)S(1)}, u32[]{:S(2)}, u32[]{:S(2)}) collective-permute-start(f32[2,128,128]{2,1,0:T(8,128)S(1)} %get-tuple-element.84), channel_id=1, source_target_pairs={{0,1},{4,5},{8,9},{12,13},{16,17},{20,21},{24,25},{28,29}} | collective-permute-start | bytes 393224 | tf_op jit(solution)/shard_map/ppermute | solution.py:387
  106.3 16.4 %collective-permute-start.30 = (f32[2,128,128]{2,1,0:T(8,128)S(1)}, f32[2,128,128]{2,1,0:T(8,128)S(1)}, u32[]{:S(2)}, u32[]{:S(2)}) collective-permute-start(f32[2,128,128]{2,1,0:T(8,128)S(1)} %get-tuple-element.62), channel_id=1, source_target_pairs={{1,2},{5,6},{9,10},{13,14},{17,18},{21,22},{25,26},{29,30}} | collective-permute-start | bytes 393224 | tf_op jit(solution)/shard_map/ppermute | solution.py:387
  107.7 17.9 %collective-permute-start.27 = (f32[2,128,128]{2,1,0:T(8,128)S(1)}, f32[2,128,128]{2,1,0:T(8,128)S(1)}, u32[]{:S(2)}, u32[]{:S(2)}) collective-permute-start(f32[2,128,128]{2,1,0:T(8,128)S(1)} %get-tuple-element.58), channel_id=1, source_target_pairs={{1,2},{5,6},{9,10},{13,14},{17,18},{21,22},{25,26},{29,30}} | collective-permute-start | bytes 393224 | tf_op jit(solution)/shard_map/ppermute | solution.py:387
  109.0 19.4 %collective-permute-start.24 = (f32[2,128,128]{2,1,0:T(8,128)S(1)}, f32[2,128,128]{2,1,0:T(8,128)S(1)}, u32[]{:S(2)}, u32[]{:S(2)}) collective-permute-start(f32[2,128,128]{2,1,0:T(8,128)S(1)} %get-tuple-element.54), channel_id=1, source_target_pairs={{1,2},{5,6},{9,10},{13,14},{17,18},{21,22},{25,26},{29,30}} | collective-permute-start | bytes 393224 | tf_op jit(solution)/shard_map/ppermute | solution.py:387
  110.4 20.6 %collective-permute-start.20 = (f32[2,128,128]{2,1,0:T(8,128)S(1)}, f32[2,128,128]{2,1,0:T(8,128)S(1)}, u32[]{:S(2)}, u32[]{:S(2)}) collective-permute-start(f32[2,128,128]{2,1,0:T(8,128)S(1)} %get-tuple-element.50), channel_id=1, source_target_pairs={{1,2},{5,6},{9,10},{13,14},{17,18},{21,22},{25,26},{29,30}} | collective-permute-start | bytes 393224 | tf_op jit(solution)/shard_map/ppermute | solution.py:387
  122.8 16.3 %collective-permute-start.31 = (f32[2,128,128]{2,1,0:T(8,128)S(1)}, f32[2,128,128]{2,1,0:T(8,128)S(1)}, u32[]{:S(2)}, u32[]{:S(2)}) collective-permute-start(f32[2,128,128]{2,1,0:T(8,128)S(1)} %get-tuple-element.64), channel_id=1, source_target_pairs={{2,3},{6,7},{10,11},{14,15},{18,19},{22,23},{26,27},{30,31}} | collective-permute-start | bytes 393224 | tf_op jit(solution)/shard_map/ppermute | solution.py:387
  125.6 14.9 %collective-permute-start.28 = (f32[2,128,128]{2,1,0:T(8,128)S(1)}, f32[2,128,128]{2,1,0:T(8,128)S(1)}, u32[]{:S(2)}, u32[]{:S(2)}) collective-permute-start(f32[2,128,128]{2,1,0:T(8,128)S(1)} %get-tuple-element.60), channel_id=1, source_target_pairs={{2,3},{6,7},{10,11},{14,15},{18,19},{22,23},{26,27},{30,31}} | collective-permute-start | bytes 393224 | tf_op jit(solution)/shard_map/ppermute | solution.py:387
  128.4 13.6 %collective-permute-start.25 = (f32[2,128,128]{2,1,0:T(8,128)S(1)}, f32[2,128,128]{2,1,0:T(8,128)S(1)}, u32[]{:S(2)}, u32[]{:S(2)}) collective-permute-start(f32[2,128,128]{2,1,0:T(8,128)S(1)} %get-tuple-element.56), channel_id=1, source_target_pairs={{2,3},{6,7},{10,11},{14,15},{18,19},{22,23},{26,27},{30,31}} | collective-permute-start | bytes 393224 | tf_op jit(solution)/shard_map/ppermute | solution.py:387
  131.0 12.4 %collective-permute-start.21 = (f32[2,128,128]{2,1,0:T(8,128)S(1)}, f32[2,128,128]{2,1,0:T(8,128)S(1)}, u32[]{:S(2)}, u32[]{:S(2)}) collective-permute-start(f32[2,128,128]{2,1,0:T(8,128)S(1)} %get-tuple-element.52), channel_id=1, source_target_pairs={{2,3},{6,7},{10,11},{14,15},{18,19},{22,23},{26,27},{30,31}} | collective-permute-start | bytes 393224 | tf_op jit(solution)/shard_map/ppermute | solution.py:387
